TPU v7x, 256 devices: a whole 4x4x8 slice. The times are simulated.
256 devices in a mesh: row: 8 (over x_hi, y), col: 32 (over x_lo, z, core).
Axes of the slice: x: 4 (x_hi: 2, x_lo: 2; x = x_hi * 2 + x_lo), y: 4, z: 8, core: 2. Of those that a mesh axis runs over, the one named last changes fastest.
Arguments:
- out_grad: bfloat16 [32768, 512], P('col', 'row'), may hold values from -6 to 6
- node_in: bfloat16 [32768, 512], P(('row', 'col')), may hold values from -0.03125 to 0.03125
- weights: bfloat16 [3, 512, 512], replicated, may hold values from -0.25 to 0.25
- tile_vals: bfloat16 [3, 32, 8, 32, 128, 128], P(None, 'col', 'row'), may hold values from -0.15625 to 0.15625
- tile_rows: int32 [3, 32, 8, 32], P(None, 'col', 'row'), may hold values from 0 to 7
- tile_cols: int32 [3, 32, 8, 32], P(None, 'col', 'row'), may hold values from 0 to 31
- tile_count: int32 [3, 32, 8], P(None, 'col', 'row'), may hold values from 1 to 32, as said below
Outputs:
- d_nodes: bfloat16 [32768, 512], P(('row', 'col'))
- d_weights: float32 [3, 512, 512], replicated
Inputs may be any that keep to these rules, and one draw needn't show every extreme that they name: Only the first tile_count slots of a block's list hold tiles; later slots are ignored. In every relation some block uses all 32 slots. `tile_rows`: coordinates may repeat within a block's list; such tiles add.
All inputs are finite; a program needn't handle non-finite values.
Results may differ from a plain program's by a relative error of at most 0.005.
Values may be sent and summed in bfloat16 or wider, within the bound.
No kernel may reach another device: no remote copies, remote signals or barrier semaphores. Data moves between devices by JAX's collectives and lax.ppermute only.
A program may use at most 256 MiB of HBM per device.

v0:
```python
import jax
import jax.numpy as jnp
from jax import lax
from jax.experimental import pallas as pl
from jax.experimental.pallas import tpu as pltpu
from jax.sharding import Mesh
from jax.sharding import PartitionSpec as P


XHI, Y, XLO, Z, CORE = "row_0", "row_1", "col_0", "col_1", "col_2"
ROW = (XHI, Y)
COL = (XLO, Z, CORE)
NEAR = (XLO, Z)
X4 = (XHI, XLO)

UNROLL = 4
CAP = 32
TILE = 128
F32 = jnp.float32
BF16 = jnp.bfloat16
SMEM = pl.BlockSpec(memory_space=pltpu.SMEM)
VMEM = pl.BlockSpec(memory_space=pltpu.VMEM)
ANY = pl.BlockSpec(memory_space=pltpu.HBM)
BUSY = pl.CostEstimate(flops=40 * 10**9, transcendentals=0, bytes_accessed=2**23)
ROOMY = pltpu.CompilerParams(vmem_limit_bytes=24 * 2**20)
SMALL = pltpu.CompilerParams(vmem_limit_bytes=8 * 2**20)


def shifted(value, axis, step):
    n = lax.axis_size(axis)
    return lax.ppermute(value, axis, [(i, (i + step) % n) for i in range(n)])


def around(value, axis):
    n = lax.axis_size(axis)
    held = {0: value}
    for step in range(1, n // 2 + 1):
        held[step] = shifted(held[step - 1], axis, 1)
        if n - step > step:
            held[n - step] = shifted(held[(n - step + 1) % n], axis, -1)
    return [held[k] for k in range(n)]


def swapped(value, axis, step):
    return lax.ppermute(value, axis, [(i, i ^ step) for i in range(lax.axis_size(axis))])


def added(first, *others):
    total = first.astype(F32)
    for other in others:
        total = total + other.astype(F32)
    return total


def columns(core, meta, r, picked, body):
    count = meta[r, 2 * CAP]

    def pick(s, n):
        picked[n] = s
        return n + jnp.where((meta[r, CAP + s] & 1) == core, 1, 0)

    found = lax.fori_loop(0, count, pick, 0)
    for u in range(UNROLL):
        picked[found + u] = 0

    def group(g, carry):
        at = [g * UNROLL + u for u in range(UNROLL)]
        ids = [picked[i] for i in at]
        body([(s, i < found, meta[r, s], meta[r, CAP + s]) for i, s in zip(at, ids)])
        return carry

    lax.fori_loop(0, (found + UNROLL - 1) // UNROLL, group, 0)


def fetches(tiles0, tiles1, tiles, arrived):
    return lambda a, r: pltpu.make_async_copy((tiles0, tiles1)[a].at[r], tiles.at[a, r], arrived.at[a, r])


def masked(tile, keep):
    return jnp.where(keep, tile, jnp.zeros_like(tile))


def prepare_kernel(node_in, rows, cols, counts, turned, meta):
    turned[...] = node_in[...].astype(F32).T.astype(BF16)
    for r in range(meta.shape[0]):
        meta[r : r + 1, :CAP] = rows[r, 0]
        meta[r : r + 1, CAP : 2 * CAP] = cols[r, 0]
        meta[r : r + 1, 2 * CAP :] = jnp.full((1, meta.shape[1] - 2 * CAP), counts[r, 0, 0], jnp.int32)


def grad_kernel(g0, g1, g2, g3, grad):
    x_hi, y = lax.axis_index(XHI), lax.axis_index(Y)
    for k, block in enumerate((g0, g1, g2, g3)):
        for a in range(2):
            grad[(x_hi ^ a) * 4 + ((y - k) & 3)] = block[a]


def mix_kernel(meta0, meta1, grad0, grad1, weights, tiles0, tiles1, out, picked, premixed, acc, held_tiles, arrived):
    core = lax.axis_index(CORE)
    fetch = fetches(tiles0, tiles1, held_tiles, arrived)
    for r in range(weights.shape[0]):
        for a in range(2):
            fetch(a, r).start()
    acc[...] = jnp.zeros_like(acc)

    def relation(r, carry):
        for a, (meta, grad) in enumerate(((meta0, grad0), (meta1, grad1))):
            mixed = lax.dot_general(
                weights[r], grad[...], (((1,), (0,)), ((), ())), preferred_element_type=F32
            ).astype(BF16)
            for k in range(premixed.shape[0]):
                premixed[k] = mixed[:, TILE * k : TILE * (k + 1)]

            fetch(a, r).wait()

            def group(entries, a=a):
                products = [
                    jnp.dot(premixed[row], masked(held_tiles[a, r, s], keep), preferred_element_type=F32)
                    for s, keep, row, col in entries
                ]
                for (s, keep, row, col), product in zip(entries, products):
                    acc[col >> 1] += product

            columns(core, meta, r, picked, group)
        return carry

    lax.fori_loop(0, weights.shape[0], relation, 0)
    out[...] = acc[...].astype(BF16)


def weight_kernel(meta0, meta1, *refs):
    parts = refs[:8]
    grad0, grad1, tiles0, tiles1, kept, sent, picked, inputs, sums, held, held_tiles, arrived = refs[8:]
    core, x_hi, y, x_lo, z = [lax.axis_index(a) for a in (CORE, XHI, Y, XLO, Z)]
    fetch = fetches(tiles0, tiles1, held_tiles, arrived)
    for r in range(tiles0.shape[0]):
        for a in range(2):
            fetch(a, r).start()
    x = x_hi * 2 + x_lo
    for k, part in enumerate(parts):
        inputs[2 * k] = part[0]
        inputs[2 * k + 1] = part[1]

    def relation(r, carry):
        terms = None
        for a, (meta, grad) in enumerate(((meta0, grad0), (meta1, grad1))):
            fetch(a, r).wait()
            sums[...] = jnp.zeros_like(sums)

            def group(entries, a=a):
                products = [
                    lax.dot_general(
                        inputs[((z - (col >> 1)) & 7) * 2 + ((col >> 4) ^ x_lo)],
                        masked(held_tiles[a, r, s], keep),
                        (((1,), (1,)), ((), ())),
                        preferred_element_type=F32,
                    )
                    for s, keep, row, col in entries
                ]
                for (s, keep, row, col), product in zip(entries, products):
                    sums[row] += product

            columns(core, meta, r, picked, group)
            for k in range(sums.shape[0]):
                held[:, TILE * k : TILE * (k + 1)] = sums[k].astype(BF16)
            part = lax.dot_general(
                held[...], grad[...], (((1,), (1,)), ((), ())), preferred_element_type=F32
            )
            terms = part if terms is None else terms + part
        half = terms.shape[0] // 2
        low, high = terms[:half], terms[half:]
        mine = jnp.where(core == 0, low, high)
        theirs = jnp.where(core == 0, high, low).astype(BF16)
        for yb in range(4):
            for xb in range(4):
                d = (yb * 4 + xb) * 16
                kept[(yb - y) & 3, (xb - x) & 3, r] = mine[d : d + 16]
                sent[(yb - y) & 3, (xb - x) & 3, r] = theirs[d : d + 16]
        return carry

    lax.fori_loop(0, tiles0.shape[0], relation, 0)


def nodes_kernel(parts, out):
    total = parts[0].astype(F32)
    for k in range(1, parts.shape[0]):
        total += parts[k].astype(F32)
    out[...] = total.T.astype(BF16)


def join_kernel(own, other, out):
    core, x_hi, y, x_lo = [lax.axis_index(a) for a in (CORE, XHI, Y, XLO)]
    x = x_hi * 2 + x_lo
    for a, block in enumerate((own, other)):
        for ky in range(4):
            for kx in range(4):
                d = ((core ^ a) * 16 + ((y - ky) & 3) * 4 + ((x - kx) & 3)) * 16
                out[0, pl.ds(pl.multiple_of(d, 16), 16), :] = block[ky, kx, 0].astype(F32)


def body(out_grad, node_in, weights, tile_vals, tile_rows, tile_cols, tile_count):
    relations, d_in, d_out = weights.shape
    tiles = tile_vals[:, 0, 0]
    rows, width = out_grad.shape

    turned, meta = pl.pallas_call(
        prepare_kernel,
        out_shape=(
            jax.ShapeDtypeStruct((d_in, TILE), BF16),
            jax.ShapeDtypeStruct((relations, TILE), jnp.int32),
        ),
        in_specs=[VMEM] * 3 + [SMEM],
        out_specs=(VMEM, VMEM),
        compiler_params=SMALL,
        name="prepare",
    )(node_in, tile_rows, tile_cols, tile_count)
    packed = out_grad.T
    pair = jnp.stack([packed, shifted(packed, XHI, 1)])
    grads = [pair] + [shifted(pair, Y, k) for k in (1, 2, 3)]
    parts = around(jnp.stack([turned, shifted(turned, XLO, 1)]), Z)
    tiles_near = shifted(tiles, CORE, 1)
    meta_near = shifted(meta, CORE, 1)

    grad = pl.pallas_call(
        grad_kernel,
        out_shape=jax.ShapeDtypeStruct((d_out // width, width, rows), BF16),
        in_specs=[VMEM] * 4,
        out_specs=VMEM,
        compiler_params=SMALL,
        name="join_grad",
    )(*grads).reshape(d_out, rows)
    grad_near = shifted(grad, CORE, 1)

    partial = pl.pallas_call(
        mix_kernel,
        out_shape=jax.ShapeDtypeStruct((16, d_in, TILE), BF16),
        in_specs=[SMEM] * 2 + [VMEM] * 3 + [ANY] * 2,
        out_specs=VMEM,
        scratch_shapes=[
            pltpu.SMEM((CAP + UNROLL,), jnp.int32),
            pltpu.VMEM((8, d_in, TILE), BF16),
            pltpu.VMEM((16, d_in, TILE), F32),
            pltpu.VMEM((2, *tiles.shape), BF16),
            pltpu.SemaphoreType.DMA((2, relations)),
        ],
        compiler_params=ROOMY,
        cost_estimate=BUSY,
        name="mix",
    )(meta, meta_near, grad, grad_near, weights, tiles, tiles_near)
    mixed = lax.all_to_all(partial, NEAR, 0, 0)
    d_nodes = pl.pallas_call(
        nodes_kernel,
        out_shape=jax.ShapeDtypeStruct(node_in.shape, BF16),
        in_specs=[VMEM],
        out_specs=VMEM,
        compiler_params=SMALL,
        name="nodes",
    )(mixed)

    kept, sent = pl.pallas_call(
        weight_kernel,
        out_shape=(
            jax.ShapeDtypeStruct((4, 4, relations, 16, d_out), F32),
            jax.ShapeDtypeStruct((4, 4, relations, 16, d_out), BF16),
        ),
        in_specs=[SMEM] * 2 + [VMEM] * 10 + [ANY] * 2,
        out_specs=(VMEM, VMEM),
        scratch_shapes=[
            pltpu.SMEM((CAP + UNROLL,), jnp.int32),
            pltpu.VMEM((16, d_in, TILE), BF16),
            pltpu.VMEM((8, d_in, TILE), F32),
            pltpu.VMEM((d_in, rows), BF16),
            pltpu.VMEM((2, *tiles.shape), BF16),
            pltpu.SemaphoreType.DMA((2, relations)),
        ],
        compiler_params=ROOMY,
        cost_estimate=BUSY,
        name="weight_terms",
    )(meta, meta_near, *parts, grad, grad_near, tiles, tiles_near)

    met = shifted(sent, CORE, 1)
    on_y = [added(kept[k], met[k]) for k in range(4)]
    on_y = added(on_y[0], *[shifted(on_y[k].astype(BF16), Y, k) for k in (1, 2, 3)])
    on_x = added(on_y[0], *[shifted(on_y[k].astype(BF16), X4, k) for k in (1, 2, 3)])
    on_z = (on_x + swapped(on_x, Z, 1)).astype(BF16)
    by = [on_z] + [shifted(on_z, Z, k) for k in (2, 4, 6)]
    total = (added(by[0], by[2]) + added(by[1], by[3])).astype(BF16)
    total = jnp.stack([total] + [shifted(total, X4, k) for k in (1, 2, 3)])
    total = jnp.stack([total] + [shifted(total, Y, k) for k in (1, 2, 3)])
    share = pl.BlockSpec((4, 4, 1, 16, d_out), lambda r: (0, 0, r, 0, 0))
    d_weights = pl.pallas_call(
        join_kernel,
        out_shape=jax.ShapeDtypeStruct((relations, d_in, d_out), F32),
        grid=(relations,),
        in_specs=[share, share],
        out_specs=pl.BlockSpec((1, d_in, d_out), lambda r: (r, 0, 0)),
        compiler_params=SMALL,
        name="join",
    )(total, shifted(total, CORE, 1))
    return d_nodes, d_weights


def solution(mesh):
    finer = Mesh(mesh.devices.reshape(2, 4, 2, 8, 2), (XHI, Y, XLO, Z, CORE))
    in_specs = (
        P(COL, ROW),
        P(ROW + COL, None),
        P(),
        P(None, COL, ROW, None, None, None),
        P(None, COL, ROW, None),
        P(None, COL, ROW, None),
        P(None, COL, ROW),
    )
    out_specs = (P(ROW + COL, None), P())
    return jax.shard_map(body, mesh=finer, in_specs=in_specs, out_specs=out_specs, check_vma=False)
```

profile of v0, /device:TPU:1, one launch (start us, length us, event | category | flops | bytes accessed | tf_op | source)
XLA Modules:
  0.0 173.9 jit_solution(4773359927869569575)
XLA Ops:
  0.7 3.3 %collective-permute-start.6 = (bf16[3,32,128,128]{3,2,1,0:T(8,128)(2,1)}, bf16[3,32,128,128]{3,2,1,0:T(8,128)(2,1)}, u32[]{:S(2)}, u32[]{:S(2)}) collective-permute-start(bf16[3,32,128,128]{3,2,1,0:T(8,128)(2,1)} %bitcast.48), channel_id=1, source_target_pairs={{0,1},{1,0},{2,3},{3,2},{4,5},{5,4},{6,7},{7,6},{8,9},{9,8},{10,11... | collective-permute-start | bytes 9437192 | tf_op jit(solution)/shard_map/ppermute | solution.py:31
  4.0 1.0 collective-permute-start.1
  5.0 5.6 %collective-permute-done.1 = bf16[64,1024]{1,0:T(8,128)(2,1)S(1)} collective-permute-done((bf16[64,1024]{1,0:T(8,128)(2,1)}, bf16[64,1024]{1,0:T(8,128)(2,1)S(1)}, u32[]{:S(2)}, u32[]{:S(2)}) %collective-permute-start.1) | collective-permute-done | bytes 131104 | tf_op jit(solution)/shard_map/ppermute | solution.py:31
  11.6 1.1 collective-permute-start.4
  13.7 4.8 %collective-permute-done.4.g3 = bf16[2,64,1024]{2,1,0:T(8,128)(2,1)S(1)} collective-permute-done((bf16[2,64,1024]{2,1,0:T(8,128)(2,1)S(1)}, bf16[2,64,1024]{2,1,0:T(8,128)(2,1)S(1)}, u32[]{:S(2)}, u32[]{:S(2)}) %collective-permute-start.4) | collective-permute-done | bytes 262176 | tf_op jit(solution)/shard_map/ppermute | solution.py:31
  18.5 2.3 %collective-permute-done.3.g2 = bf16[2,64,1024]{2,1,0:T(8,128)(2,1)S(1)} collective-permute-done((bf16[2,64,1024]{2,1,0:T(8,128)(2,1)S(1)}, bf16[2,64,1024]{2,1,0:T(8,128)(2,1)S(1)}, u32[]{:S(2)}, u32[]{:S(2)}) %collective-permute-start.3) | collective-permute-done | bytes 262176 | tf_op jit(solution)/shard_map/ppermute | solution.py:31
  20.9 7.2 %collective-permute-done.2.g1 = bf16[2,64,1024]{2,1,0:T(8,128)(2,1)S(1)} collective-permute-done((bf16[2,64,1024]{2,1,0:T(8,128)(2,1)S(1)}, bf16[2,64,1024]{2,1,0:T(8,128)(2,1)S(1)}, u32[]{:S(2)}, u32[]{:S(2)}) %collective-permute-start.2) | collective-permute-done | bytes 262176 | tf_op jit(solution)/shard_map/ppermute | solution.py:31
  29.5 1.3 collective-permute-start.7
  30.8 3.8 %collective-permute-done.7 = bf16[512,128]{1,0:T(8,128)(2,1)S(1)} collective-permute-done((bf16[512,128]{1,0:T(8,128)(2,1)S(1)}, bf16[512,128]{1,0:T(8,128)(2,1)S(1)}, u32[]{:S(2)}, u32[]{:S(2)}) %collective-permute-start.7) | collective-permute-done | bytes 131104 | tf_op jit(solution)/shard_map/ppermute | solution.py:31
  34.6 1.7 collective-permute-start.8
  36.3 4.0 %collective-permute-start.12 = (bf16[2,512,128]{2,1,0:T(8,128)(2,1)S(1)}, bf16[2,512,128]{2,1,0:T(8,128)(2,1)S(1)}, u32[]{:S(2)}, u32[]{:S(2)}) collective-permute-start(bf16[2,512,128]{2,1,0:T(8,128)(2,1)S(1)} %pad_maximum_fusion.2.refs_0_), channel_id=1, source_target_pairs={{0,14},{2,0},{4,2},{6,4},{8,6},{10,8},{12,10},{14,12},{1,15},{3,1}... | collective-permute-start | bytes 786440 | tf_op jit(solution)/shard_map/ppermute | solution.py:31
  40.3 5.7 %collective-permute-done.8.refs_1_ = bf16[2,512,128]{2,1,0:T(8,128)(2,1)S(1)} collective-permute-done((bf16[2,512,128]{2,1,0:T(8,128)(2,1)S(1)}, bf16[2,512,128]{2,1,0:T(8,128)(2,1)S(1)}, u32[]{:S(2)}, u32[]{:S(2)}) %collective-permute-start.8) | collective-permute-done | bytes 262176 | tf_op jit(solution)/shard_map/ppermute | solution.py:31
  46.8 2.7 %collective-permute-start.13 = (bf16[2,512,128]{2,1,0:T(8,128)(2,1)S(1)}, bf16[2,512,128]{2,1,0:T(8,128)(2,1)}, u32[]{:S(2)}, u32[]{:S(2)}) collective-permute-start(bf16[2,512,128]{2,1,0:T(8,128)(2,1)S(1)} %collective-permute-done.12.refs_7_), channel_id=1, source_target_pairs={{0,14},{2,0},{4,2},{6,4},{8,6},{10,8},{12,10},{14,12},{1,15},{3,1}... | collective-permute-start | bytes 786440 | tf_op jit(solution)/shard_map/ppermute | solution.py:31
  50.2 3.5 %collective-permute-done.9.refs_2_ = bf16[2,512,128]{2,1,0:T(8,128)(2,1)S(1)} collective-permute-done((bf16[2,512,128]{2,1,0:T(8,128)(2,1)S(1)}, bf16[2,512,128]{2,1,0:T(8,128)(2,1)S(1)}, u32[]{:S(2)}, u32[]{:S(2)}) %collective-permute-start.9) | collective-permute-done | bytes 262176 | tf_op jit(solution)/shard_map/ppermute | solution.py:31
  54.4 2.3 %collective-permute-start = (s32[3,128]{1,0:T(4,128)S(1)}, s32[3,128]{1,0:T(4,128)S(1)}, u32[]{:S(2)}, u32[]{:S(2)}) collective-permute-start(s32[3,128]{1,0:T(4,128)S(1)} %get-tuple-element.6.meta0), channel_id=1, source_target_pairs={{0,1},{1,0},{2,3},{3,2},{4,5},{5,4},{6,7},{7,6},{8,9},{9,8},{10,11... | collective-permute-start | bytes 4616 | tf_op jit(solution)/shard_map/ppermute | solution.py:31
  56.7 3.0 %collective-permute-start.14 = (bf16[2,512,128]{2,1,0:T(8,128)(2,1)}, bf16[2,512,128]{2,1,0:T(8,128)(2,1)}, u32[]{:S(2)}, u32[]{:S(2)}) collective-permute-start(bf16[2,512,128]{2,1,0:T(8,128)(2,1)} %collective-permute-done.13.refs_6_), channel_id=1, source_target_pairs={{0,14},{2,0},{4,2},{6,4},{8,6},{10,8},{12,10},{14,12},{1,15},{3,1}... | collective-permute-start | bytes 786440 | tf_op jit(solution)/shard_map/ppermute | solution.py:31
  61.5 1.9 %copy-done.4 = bf16[3,1,1,32,128,128]{5,4,3,2,1,0:T(8,128)(2,1)S(1)} copy-done((bf16[3,1,1,32,128,128]{5,4,3,2,1,0:T(8,128)(2,1)S(1)}, bf16[3,1,1,32,128,128]{5,4,3,2,1,0:T(8,128)(2,1)}, u32[]{:S(2)}) %copy-start.4) | copy-done | bytes 3145752
  63.4 1.4 copy-done.6
  64.8 1.2 copy-done.8
  66.1 11.0 %mix.1 = bf16[16,512,128]{2,1,0:T(8,128)(2,1)S(1)} custom-call(s32[3,128]{1,0:T(4,128)S(1)} %get-tuple-element.6.meta0, s32[3,128]{1,0:T(4,128)S(1)} %collective-permute-done.meta1, bf16[512,1024]{1,0:T(8,128)(2,1)S(1)} %bitcast.45, bf16[512,1024]{1,0:T(8,128)(2,1)S(1)} %copy-done.8, bf16[3,512,512]{2,1,0:T(8,128)(2,1)S(1)} %copy-done.6, ...), custom_call_target="tpu_custom_call" | custom-call | flops 40000000000 | bytes 8388608 | tf_op jit(solution)/shard_map/mix/pallas_call | solution.py:234
  77.1 1.3 copy-done
  78.4 6.9 %all-to-all-start = ((bf16[16,512,128]{2,1,0:T(8,128)(2,1)}), bf16[16,512,128]{2,1,0:T(8,128)(2,1)S(1)}, u32[]{:S(2)}, u32[]{:S(2)}) async-start(bf16[16,512,128]{2,1,0:T(8,128)(2,1)} %copy-done), calls=%async_computation | async-start | bytes 4194304 | tf_op jit(solution)/shard_map/all_to_all | solution.py:250
  85.4 1.9 %copy-done.5 = bf16[3,1,1,32,128,128]{5,4,3,2,1,0:T(8,128)(2,1)S(1)} copy-done((bf16[3,1,1,32,128,128]{5,4,3,2,1,0:T(8,128)(2,1)S(1)}, bf16[3,1,1,32,128,128]{5,4,3,2,1,0:T(8,128)(2,1)}, u32[]{:S(2)}) %copy-start.5) | copy-done | bytes 3145752
  87.3 1.2 copy-done.9
  91.4 13.2 %weight_terms.1 = (f32[4,4,3,16,512]{4,3,2,1,0:T(8,128)S(1)}, bf16[4,4,3,16,512]{4,3,2,1,0:T(8,128)(2,1)S(1)}) custom-call(s32[3,128]{1,0:T(4,128)S(1)} %get-tuple-element.6.meta0, s32[3,128]{1,0:T(4,128)S(1)} %collective-permute-done.meta1, bf16[2,512,128]{2,1,0:T(8,128)(2,1)S(1)} %pad_maximum_fusion.2.refs_0_, bf16[2,512,128]{2,1,0:T(8,128)(2,1)S(1)} %copy-done.11, ...), custom_call_target="tpu_custom_call" | custom-call | flops 40000000000 | bytes 8388608 | tf_op jit(solution)/shard_map/weight_terms/pallas_call | solution.py:260
  104.5 4.1 %collective-permute-start.15 = (bf16[4,4,3,16,512]{4,3,2,1,0:T(8,128)(2,1)S(1)}, bf16[4,4,3,16,512]{4,3,2,1,0:T(8,128)(2,1)S(1)}, u32[]{:S(2)}, u32[]{:S(2)}) collective-permute-start(bf16[4,4,3,16,512]{4,3,2,1,0:T(8,128)(2,1)S(1)} %get-tuple-element.9), channel_id=1, source_target_pairs={{0,1},{1,0},{2,3},{3,2},{4,5},{5,4},{6,7},{7,6},{8,9},{9,8},{10,11... | collective-permute-start | bytes 2359304 | tf_op jit(solution)/shard_map/ppermute | solution.py:31
  108.7 1.9 %collective-permute-done.15 = bf16[4,4,3,16,512]{4,3,2,1,0:T(8,128)(2,1)S(1)} collective-permute-done((bf16[4,4,3,16,512]{4,3,2,1,0:T(8,128)(2,1)S(1)}, bf16[4,4,3,16,512]{4,3,2,1,0:T(8,128)(2,1)S(1)}, u32[]{:S(2)}, u32[]{:S(2)}) %collective-permute-start.15) | collective-permute-done | bytes 786464 | tf_op jit(solution)/shard_map/ppermute | solution.py:31
  111.6 1.9 %collective-permute-start.18 = (bf16[4,3,16,512]{3,2,1,0:T(8,128)(2,1)S(1)}, bf16[4,3,16,512]{3,2,1,0:T(8,128)(2,1)S(1)}, u32[]{:S(2)}, u32[]{:S(2)}) collective-permute-start(bf16[4,3,16,512]{3,2,1,0:T(8,128)(2,1)S(1)} %get-tuple-element.13), channel_id=1, source_target_pairs={{0,96},{32,0},{64,32},{96,64},{1,97},{33,1},{65,33},{97,65},{2,98}... | collective-permute-start | bytes 589832 | tf_op jit(solution)/shard_map/ppermute | solution.py:31
  113.5 8.8 %collective-permute-done.16 = bf16[4,3,16,512]{3,2,1,0:T(8,128)(2,1)S(1)} collective-permute-done((bf16[4,3,16,512]{3,2,1,0:T(8,128)(2,1)S(1)}, bf16[4,3,16,512]{3,2,1,0:T(8,128)(2,1)S(1)}, u32[]{:S(2)}, u32[]{:S(2)}) %collective-permute-start.16) | collective-permute-done | bytes 196640 | tf_op jit(solution)/shard_map/ppermute | solution.py:31
  122.6 4.2 %collective-permute-start.21 = (bf16[3,16,512]{2,1,0:T(8,128)(2,1)S(1)}, bf16[3,16,512]{2,1,0:T(8,128)(2,1)S(1)}, u32[]{:S(2)}, u32[]{:S(2)}) collective-permute-start(bf16[3,16,512]{2,1,0:T(8,128)(2,1)S(1)} %get-tuple-element.18), channel_id=1, source_target_pairs={{0,144},{16,0},{128,16},{144,128},{1,145},{17,1},{129,17},{145,129... | collective-permute-start | bytes 147464 | tf_op jit(solution)/shard_map/ppermute | solution.py:31
  126.9 1.1 collective-permute-start.20
  128.6 3.5 %collective-permute-done.20 = bf16[3,16,512]{2,1,0:T(8,128)(2,1)S(1)} collective-permute-done((bf16[3,16,512]{2,1,0:T(8,128)(2,1)S(1)}, bf16[3,16,512]{2,1,0:T(8,128)(2,1)S(1)}, u32[]{:S(2)}, u32[]{:S(2)}) %collective-permute-start.20) | collective-permute-done | bytes 49184 | tf_op jit(solution)/shard_map/ppermute | solution.py:31
  132.2 3.4 %collective-permute-done.22 = f32[3,16,512]{2,1,0:T(8,128)S(1)} collective-permute-done((f32[3,16,512]{2,1,0:T(8,128)S(1)}, f32[3,16,512]{2,1,0:T(8,128)S(1)}, u32[]{:S(2)}, u32[]{:S(2)}) %collective-permute-start.22) | collective-permute-done | bytes 98336 | tf_op jit(solution)/shard_map/ppermute | solution.py:45
  135.7 3.3 %collective-permute-start.25 = (bf16[3,16,512]{2,1,0:T(8,128)(2,1)S(1)}, bf16[3,16,512]{2,1,0:T(8,128)(2,1)S(1)}, u32[]{:S(2)}, u32[]{:S(2)}) collective-permute-start(bf16[3,16,512]{2,1,0:T(8,128)(2,1)S(1)} %add_convert_fusion.4), channel_id=1, source_target_pairs={{0,12},{2,14},{4,0},{6,2},{8,4},{10,6},{12,8},{14,10},{1,13},{3,15... | collective-permute-start | bytes 147464 | tf_op jit(solution)/shard_map/ppermute | solution.py:31
  139.0 2.2 %collective-permute-start.23 = (bf16[3,16,512]{2,1,0:T(8,128)(2,1)S(1)}, bf16[3,16,512]{2,1,0:T(8,128)(2,1)S(1)}, u32[]{:S(2)}, u32[]{:S(2)}) collective-permute-start(bf16[3,16,512]{2,1,0:T(8,128)(2,1)S(1)} %add_convert_fusion.4), channel_id=1, source_target_pairs={{0,8},{2,10},{4,12},{6,14},{8,0},{10,2},{12,4},{14,6},{1,9},{3,11}... | collective-permute-start | bytes 147464 | tf_op jit(solution)/shard_map/ppermute | solution.py:31
  141.2 2.9 %collective-permute-done.24 = bf16[3,16,512]{2,1,0:T(8,128)(2,1)S(1)} collective-permute-done((bf16[3,16,512]{2,1,0:T(8,128)(2,1)S(1)}, bf16[3,16,512]{2,1,0:T(8,128)(2,1)S(1)}, u32[]{:S(2)}, u32[]{:S(2)}) %collective-permute-start.24) | collective-permute-done | bytes 49184 | tf_op jit(solution)/shard_map/ppermute | solution.py:31
  144.0 2.0 %collective-permute-done.23 = bf16[3,16,512]{2,1,0:T(8,128)(2,1)S(1)} collective-permute-done((bf16[3,16,512]{2,1,0:T(8,128)(2,1)S(1)}, bf16[3,16,512]{2,1,0:T(8,128)(2,1)S(1)}, u32[]{:S(2)}, u32[]{:S(2)}) %collective-permute-start.23) | collective-permute-done | bytes 49184 | tf_op jit(solution)/shard_map/ppermute | solution.py:31
  148.0 1.4 collective-permute-done.28
  149.4 2.1 %collective-permute-done.27 = bf16[3,16,512]{2,1,0:T(8,128)(2,1)S(1)} collective-permute-done((bf16[3,16,512]{2,1,0:T(8,128)(2,1)S(1)}, bf16[3,16,512]{2,1,0:T(8,128)(2,1)S(1)}, u32[]{:S(2)}, u32[]{:S(2)}) %collective-permute-start.27) | collective-permute-done | bytes 49184 | tf_op jit(solution)/shard_map/ppermute | solution.py:31
  152.0 1.8 %collective-permute-start.30 = (bf16[4,3,16,512]{3,2,1,0:T(8,128)(2,1)S(1)}, bf16[4,3,16,512]{3,2,1,0:T(8,128)(2,1)S(1)}, u32[]{:S(2)}, u32[]{:S(2)}) collective-permute-start(bf16[4,3,16,512]{3,2,1,0:T(8,128)(2,1)S(1)} %get-tuple-element.16), channel_id=1, source_target_pairs={{0,64},{32,96},{64,0},{96,32},{1,65},{33,97},{65,1},{97,33},{2,66}... | collective-permute-start | bytes 589832 | tf_op jit(solution)/shard_map/ppermute | solution.py:31
  153.8 1.2 collective-permute-start.29
  155.0 1.5 collective-permute-start.31
  156.5 1.7 collective-permute-done.30
  158.2 2.0 %collective-permute-done.29 = bf16[4,3,16,512]{3,2,1,0:T(8,128)(2,1)S(1)} collective-permute-done((bf16[4,3,16,512]{3,2,1,0:T(8,128)(2,1)S(1)}, bf16[4,3,16,512]{3,2,1,0:T(8,128)(2,1)S(1)}, u32[]{:S(2)}, u32[]{:S(2)}) %collective-permute-start.29) | collective-permute-done | bytes 196640 | tf_op jit(solution)/shard_map/ppermute | solution.py:31
  160.3 8.3 %collective-permute-start.32 = (bf16[4,4,3,16,512]{4,3,2,1,0:T(8,128)(2,1)S(1)}, bf16[4,4,3,16,512]{4,3,2,1,0:T(8,128)(2,1)S(1)}, u32[]{:S(2)}, u32[]{:S(2)}) collective-permute-start(bf16[4,4,3,16,512]{4,3,2,1,0:T(8,128)(2,1)S(1)} %pad_maximum_fusion.own), channel_id=1, source_target_pairs={{0,1},{1,0},{2,3},{3,2},{4,5},{5,4},{6,7},{7,6},{8,9},{9,8},{10,11... | collective-permute-start | bytes 2359304 | tf_op jit(solution)/shard_map/ppermute | solution.py:31
  168.7 1.9 %collective-permute-done.32.other = bf16[4,4,3,16,512]{4,3,2,1,0:T(8,128)(2,1)S(1)} collective-permute-done((bf16[4,4,3,16,512]{4,3,2,1,0:T(8,128)(2,1)S(1)}, bf16[4,4,3,16,512]{4,3,2,1,0:T(8,128)(2,1)S(1)}, u32[]{:S(2)}, u32[]{:S(2)}) %collective-permute-start.32) | collective-permute-done | bytes 786464 | tf_op jit(solution)/shard_map/ppermute | solution.py:31
  170.6 2.3 %join.1 = f32[3,512,512]{2,1,0:T(8,128)} custom-call(bf16[4,4,3,16,512]{4,3,2,1,0:T(8,128)(2,1)S(1)} %pad_maximum_fusion.own, bf16[4,4,3,16,512]{4,3,2,1,0:T(8,128)(2,1)S(1)} %collective-permute-done.32.other), custom_call_target="tpu_custom_call" | custom-call | tf_op jit(solution)/shard_map/join/pallas_call | solution.py:291
  172.8 1.1 nodes.1
  (71 shorter events, 14.9 us)
Async XLA Ops:
  0.6 28.1 %copy-start.16 = (s32[3,1,1]{0,2,1:T(1,128)S(1)}, s32[3,1,1]{0,2,1:T(1,128)}, u32[]{:S(2)}) copy-start(s32[3,1,1]{0,2,1:T(1,128)} %param.13) | copy-start | bytes 40
  0.6 28.1 %copy-start.3 = (s32[3,1,1,32]{3,2,1,0:T(1,128)S(1)}, s32[3,1,1,32]{3,2,1,0:T(1,128)}, u32[]{:S(2)}) copy-start(s32[3,1,1,32]{3,2,1,0:T(1,128)} %cols.1) | copy-start | bytes 1156
  0.7 28.1 %copy-start.2 = (s32[3,1,1,32]{3,2,1,0:T(1,128)S(1)}, s32[3,1,1,32]{3,2,1,0:T(1,128)}, u32[]{:S(2)}) copy-start(s32[3,1,1,32]{3,2,1,0:T(1,128)} %rows.1) | copy-start | bytes 1156
  0.7 28.1 %copy-start.1 = (bf16[128,512]{1,0:T(8,128)(2,1)S(1)}, bf16[128,512]{1,0:T(8,128)(2,1)}, u32[]{:S(2)}) copy-start(bf16[128,512]{1,0:T(8,128)(2,1)} %node_in.1) | copy-start | bytes 393220
  0.7 60.9 %collective-permute-start.6 = (bf16[3,32,128,128]{3,2,1,0:T(8,128)(2,1)}, bf16[3,32,128,128]{3,2,1,0:T(8,128)(2,1)}, u32[]{:S(2)}, u32[]{:S(2)}) collective-permute-start(bf16[3,32,128,128]{3,2,1,0:T(8,128)(2,1)} %bitcast.48), channel_id=1, source_target_pairs={{0,1},{1,0},{2,3},{3,2},{4,5},{5,4},{6,7},{7,6},{8,9},{9,8},{10,11... | collective-permute-start | bytes 9437192 | tf_op jit(solution)/shard_map/ppermute | solution.py:31
  4.0 6.7 %collective-permute-start.1 = (bf16[64,1024]{1,0:T(8,128)(2,1)}, bf16[64,1024]{1,0:T(8,128)(2,1)S(1)}, u32[]{:S(2)}, u32[]{:S(2)}) collective-permute-start(bf16[64,1024]{1,0:T(8,128)(2,1)} %bitcast.55), channel_id=1, source_target_pairs={{0,128},{128,0},{1,129},{129,1},{2,130},{130,2},{3,131},{131,3},{4... | collective-permute-start | bytes 393224 | tf_op jit(solution)/shard_map/ppermute | solution.py:31
  11.6 7.0 %collective-permute-start.4 = (bf16[2,64,1024]{2,1,0:T(8,128)(2,1)S(1)}, bf16[2,64,1024]{2,1,0:T(8,128)(2,1)S(1)}, u32[]{:S(2)}, u32[]{:S(2)}) collective-permute-start(bf16[2,64,1024]{2,1,0:T(8,128)(2,1)S(1)} %pad_maximum_fusion.1.g0), channel_id=1, source_target_pairs={{0,96},{32,0},{64,32},{96,64},{1,97},{33,1},{65,33},{97,65},{2,98}... | collective-permute-start | bytes 786440 | tf_op jit(solution)/shard_map/ppermute | solution.py:31
  12.7 8.2 %collective-permute-start.3 = (bf16[2,64,1024]{2,1,0:T(8,128)(2,1)S(1)}, bf16[2,64,1024]{2,1,0:T(8,128)(2,1)S(1)}, u32[]{:S(2)}, u32[]{:S(2)}) collective-permute-start(bf16[2,64,1024]{2,1,0:T(8,128)(2,1)S(1)} %pad_maximum_fusion.1.g0), channel_id=1, source_target_pairs={{0,64},{32,96},{64,0},{96,32},{1,65},{33,97},{65,1},{97,33},{2,66}... | collective-permute-start | bytes 786440 | tf_op jit(solution)/shard_map/ppermute | solution.py:31
  13.0 15.0 %collective-permute-start.2 = (bf16[2,64,1024]{2,1,0:T(8,128)(2,1)S(1)}, bf16[2,64,1024]{2,1,0:T(8,128)(2,1)S(1)}, u32[]{:S(2)}, u32[]{:S(2)}) collective-permute-start(bf16[2,64,1024]{2,1,0:T(8,128)(2,1)S(1)} %pad_maximum_fusion.1.g0), channel_id=1, source_target_pairs={{0,32},{32,64},{64,96},{96,0},{1,33},{33,65},{65,97},{97,1},{2,34}... | collective-permute-start | bytes 786440 | tf_op jit(solution)/shard_map/ppermute | solution.py:31
  28.1 32.5 %collective-permute-start.5 = (bf16[512,1024]{1,0:T(8,128)(2,1)S(1)}, bf16[512,1024]{1,0:T(8,128)(2,1)S(1)}, u32[]{:S(2)}, u32[]{:S(2)}) collective-permute-start(bf16[512,1024]{1,0:T(8,128)(2,1)S(1)} %bitcast.44), channel_id=1, source_target_pairs={{0,1},{1,0},{2,3},{3,2},{4,5},{5,4},{6,7},{7,6},{8,9},{9,8},{10,11... | collective-permute-start | bytes 3145736 | tf_op jit(solution)/shard_map/ppermute | solution.py:31
  29.5 5.1 %collective-permute-start.7 = (bf16[512,128]{1,0:T(8,128)(2,1)S(1)}, bf16[512,128]{1,0:T(8,128)(2,1)S(1)}, u32[]{:S(2)}, u32[]{:S(2)}) collective-permute-start(bf16[512,128]{1,0:T(8,128)(2,1)S(1)} %get-tuple-element.7), channel_id=1, source_target_pairs={{0,16},{16,0},{1,17},{17,1},{2,18},{18,2},{3,19},{19,3},{4,20},{20... | collective-permute-start | bytes 393224 | tf_op jit(solution)/shard_map/ppermute | solution.py:31
  34.6 11.5 %collective-permute-start.8 = (bf16[2,512,128]{2,1,0:T(8,128)(2,1)S(1)}, bf16[2,512,128]{2,1,0:T(8,128)(2,1)S(1)}, u32[]{:S(2)}, u32[]{:S(2)}) collective-permute-start(bf16[2,512,128]{2,1,0:T(8,128)(2,1)S(1)} %pad_maximum_fusion.2.refs_0_), channel_id=1, source_target_pairs={{0,2},{2,4},{4,6},{6,8},{8,10},{10,12},{12,14},{14,0},{1,3},{3,5},... | collective-permute-start | bytes 786440 | tf_op jit(solution)/shard_map/ppermute | solution.py:31
  36.3 10.5 %collective-permute-start.12 = (bf16[2,512,128]{2,1,0:T(8,128)(2,1)S(1)}, bf16[2,512,128]{2,1,0:T(8,128)(2,1)S(1)}, u32[]{:S(2)}, u32[]{:S(2)}) collective-permute-start(bf16[2,512,128]{2,1,0:T(8,128)(2,1)S(1)} %pad_maximum_fusion.2.refs_0_), channel_id=1, source_target_pairs={{0,14},{2,0},{4,2},{6,4},{8,6},{10,8},{12,10},{14,12},{1,15},{3,1}... | collective-permute-start | bytes 786440 | tf_op jit(solution)/shard_map/ppermute | solution.py:31
  46.1 7.6 %collective-permute-start.9 = (bf16[2,512,128]{2,1,0:T(8,128)(2,1)S(1)}, bf16[2,512,128]{2,1,0:T(8,128)(2,1)S(1)}, u32[]{:S(2)}, u32[]{:S(2)}) collective-permute-start(bf16[2,512,128]{2,1,0:T(8,128)(2,1)S(1)} %collective-permute-done.8.refs_1_), channel_id=1, source_target_pairs={{0,2},{2,4},{4,6},{6,8},{8,10},{10,12},{12,14},{14,0},{1,3},{3,5},... | collective-permute-start | bytes 786440 | tf_op jit(solution)/shard_map/ppermute | solution.py:31
  46.8 9.9 %collective-permute-start.13 = (bf16[2,512,128]{2,1,0:T(8,128)(2,1)S(1)}, bf16[2,512,128]{2,1,0:T(8,128)(2,1)}, u32[]{:S(2)}, u32[]{:S(2)}) collective-permute-start(bf16[2,512,128]{2,1,0:T(8,128)(2,1)S(1)} %collective-permute-done.12.refs_7_), channel_id=1, source_target_pairs={{0,14},{2,0},{4,2},{6,4},{8,6},{10,8},{12,10},{14,12},{1,15},{3,1}... | collective-permute-start | bytes 786440 | tf_op jit(solution)/shard_map/ppermute | solution.py:31
  53.7 6.9 %collective-permute-start.10 = (bf16[2,512,128]{2,1,0:T(8,128)(2,1)S(1)}, bf16[2,512,128]{2,1,0:T(8,128)(2,1)}, u32[]{:S(2)}, u32[]{:S(2)}) collective-permute-start(bf16[2,512,128]{2,1,0:T(8,128)(2,1)S(1)} %collective-permute-done.9.refs_2_), channel_id=1, source_target_pairs={{0,2},{2,4},{4,6},{6,8},{8,10},{10,12},{12,14},{14,0},{1,3},{3,5},... | collective-permute-start | bytes 786440 | tf_op jit(solution)/shard_map/ppermute | solution.py:31
  54.4 6.2 %collective-permute-start = (s32[3,128]{1,0:T(4,128)S(1)}, s32[3,128]{1,0:T(4,128)S(1)}, u32[]{:S(2)}, u32[]{:S(2)}) collective-permute-start(s32[3,128]{1,0:T(4,128)S(1)} %get-tuple-element.6.meta0), channel_id=1, source_target_pairs={{0,1},{1,0},{2,3},{3,2},{4,5},{5,4},{6,7},{7,6},{8,9},{9,8},{10,11... | collective-permute-start | bytes 4616 | tf_op jit(solution)/shard_map/ppermute | solution.py:31
  56.7 28.7 %collective-permute-start.14 = (bf16[2,512,128]{2,1,0:T(8,128)(2,1)}, bf16[2,512,128]{2,1,0:T(8,128)(2,1)}, u32[]{:S(2)}, u32[]{:S(2)}) collective-permute-start(bf16[2,512,128]{2,1,0:T(8,128)(2,1)} %collective-permute-done.13.refs_6_), channel_id=1, source_target_pairs={{0,14},{2,0},{4,2},{6,4},{8,6},{10,8},{12,10},{14,12},{1,15},{3,1}... | collective-permute-start | bytes 786440 | tf_op jit(solution)/shard_map/ppermute | solution.py:31
  60.6 24.8 %collective-permute-start.11 = (bf16[2,512,128]{2,1,0:T(8,128)(2,1)}, bf16[2,512,128]{2,1,0:T(8,128)(2,1)}, u32[]{:S(2)}, u32[]{:S(2)}) collective-permute-start(bf16[2,512,128]{2,1,0:T(8,128)(2,1)} %collective-permute-done.10.refs_3_), channel_id=1, source_target_pairs={{0,2},{2,4},{4,6},{6,8},{8,10},{10,12},{12,14},{14,0},{1,3},{3,5},... | collective-permute-start | bytes 786440 | tf_op jit(solution)/shard_map/ppermute | solution.py:31
  60.6 1.0 copy-start.7
  61.5 1.9 %copy-start.4 = (bf16[3,1,1,32,128,128]{5,4,3,2,1,0:T(8,128)(2,1)S(1)}, bf16[3,1,1,32,128,128]{5,4,3,2,1,0:T(8,128)(2,1)}, u32[]{:S(2)}) copy-start(bf16[3,1,1,32,128,128]{5,4,3,2,1,0:T(8,128)(2,1)} %param.10) | copy-start | bytes 9437188
  63.4 1.4 copy-start.6
  64.8 1.2 copy-start.8
  77.1 1.3 copy-start
  78.4 94.4 %all-to-all-start = ((bf16[16,512,128]{2,1,0:T(8,128)(2,1)}), bf16[16,512,128]{2,1,0:T(8,128)(2,1)S(1)}, u32[]{:S(2)}, u32[]{:S(2)}) async-start(bf16[16,512,128]{2,1,0:T(8,128)(2,1)} %copy-done), calls=%async_computation | async-start | bytes 4194304 | tf_op jit(solution)/shard_map/all_to_all | solution.py:250
  85.4 1.9 %copy-start.5 = (bf16[3,1,1,32,128,128]{5,4,3,2,1,0:T(8,128)(2,1)S(1)}, bf16[3,1,1,32,128,128]{5,4,3,2,1,0:T(8,128)(2,1)}, u32[]{:S(2)}) copy-start(bf16[3,1,1,32,128,128]{5,4,3,2,1,0:T(8,128)(2,1)} %param.10) | copy-start | bytes 9437188
  87.3 1.2 copy-start.9
  88.5 0.9 copy-start.11
  89.5 0.9 copy-start.13
  90.4 0.9 copy-start.15
  104.5 6.0 %collective-permute-start.15 = (bf16[4,4,3,16,512]{4,3,2,1,0:T(8,128)(2,1)S(1)}, bf16[4,4,3,16,512]{4,3,2,1,0:T(8,128)(2,1)S(1)}, u32[]{:S(2)}, u32[]{:S(2)}) collective-permute-start(bf16[4,4,3,16,512]{4,3,2,1,0:T(8,128)(2,1)S(1)} %get-tuple-element.9), channel_id=1, source_target_pairs={{0,1},{1,0},{2,3},{3,2},{4,5},{5,4},{6,7},{7,6},{8,9},{9,8},{10,11... | collective-permute-start | bytes 2359304 | tf_op jit(solution)/shard_map/ppermute | solution.py:31
  110.8 11.6 %collective-permute-start.16 = (bf16[4,3,16,512]{3,2,1,0:T(8,128)(2,1)S(1)}, bf16[4,3,16,512]{3,2,1,0:T(8,128)(2,1)S(1)}, u32[]{:S(2)}, u32[]{:S(2)}) collective-permute-start(bf16[4,3,16,512]{3,2,1,0:T(8,128)(2,1)S(1)} %get-tuple-element.12), channel_id=1, source_target_pairs={{0,32},{32,64},{64,96},{96,0},{1,33},{33,65},{65,97},{97,1},{2,34}... | collective-permute-start | bytes 589832 | tf_op jit(solution)/shard_map/ppermute | solution.py:31
  111.6 10.8 %collective-permute-start.18 = (bf16[4,3,16,512]{3,2,1,0:T(8,128)(2,1)S(1)}, bf16[4,3,16,512]{3,2,1,0:T(8,128)(2,1)S(1)}, u32[]{:S(2)}, u32[]{:S(2)}) collective-permute-start(bf16[4,3,16,512]{3,2,1,0:T(8,128)(2,1)S(1)} %get-tuple-element.13), channel_id=1, source_target_pairs={{0,96},{32,0},{64,32},{96,64},{1,97},{33,1},{65,33},{97,65},{2,98}... | collective-permute-start | bytes 589832 | tf_op jit(solution)/shard_map/ppermute | solution.py:31
  113.5 8.8 %collective-permute-start.17 = (bf16[4,3,16,512]{3,2,1,0:T(8,128)(2,1)S(1)}, bf16[4,3,16,512]{3,2,1,0:T(8,128)(2,1)S(1)}, u32[]{:S(2)}, u32[]{:S(2)}) collective-permute-start(bf16[4,3,16,512]{3,2,1,0:T(8,128)(2,1)S(1)} %get-tuple-element.14), channel_id=1, source_target_pairs={{0,64},{32,96},{64,0},{96,32},{1,65},{33,97},{65,1},{97,33},{2,66}... | collective-permute-start | bytes 589832 | tf_op jit(solution)/shard_map/ppermute | solution.py:31
  122.6 6.0 %collective-permute-start.19 = (bf16[3,16,512]{2,1,0:T(8,128)(2,1)S(1)}, bf16[3,16,512]{2,1,0:T(8,128)(2,1)S(1)}, u32[]{:S(2)}, u32[]{:S(2)}) collective-permute-start(bf16[3,16,512]{2,1,0:T(8,128)(2,1)S(1)} %get-tuple-element.17), channel_id=1, source_target_pairs={{0,16},{16,128},{128,144},{144,0},{1,17},{17,129},{129,145},{145,1... | collective-permute-start | bytes 147464 | tf_op jit(solution)/shard_map/ppermute | solution.py:31
  122.6 5.9 %collective-permute-start.21 = (bf16[3,16,512]{2,1,0:T(8,128)(2,1)S(1)}, bf16[3,16,512]{2,1,0:T(8,128)(2,1)S(1)}, u32[]{:S(2)}, u32[]{:S(2)}) collective-permute-start(bf16[3,16,512]{2,1,0:T(8,128)(2,1)S(1)} %get-tuple-element.18), channel_id=1, source_target_pairs={{0,144},{16,0},{128,16},{144,128},{1,145},{17,1},{129,17},{145,129... | collective-permute-start | bytes 147464 | tf_op jit(solution)/shard_map/ppermute | solution.py:31
  126.9 5.2 %collective-permute-start.20 = (bf16[3,16,512]{2,1,0:T(8,128)(2,1)S(1)}, bf16[3,16,512]{2,1,0:T(8,128)(2,1)S(1)}, u32[]{:S(2)}, u32[]{:S(2)}) collective-permute-start(bf16[3,16,512]{2,1,0:T(8,128)(2,1)S(1)} %get-tuple-element.19), channel_id=1, source_target_pairs={{0,128},{16,144},{128,0},{144,16},{1,129},{17,145},{129,1},{145,17... | collective-permute-start | bytes 147464 | tf_op jit(solution)/shard_map/ppermute | solution.py:31
  132.1 3.6 %collective-permute-start.22 = (f32[3,16,512]{2,1,0:T(8,128)S(1)}, f32[3,16,512]{2,1,0:T(8,128)S(1)}, u32[]{:S(2)}, u32[]{:S(2)}) collective-permute-start(f32[3,16,512]{2,1,0:T(8,128)S(1)} %fusion.7), channel_id=1, source_target_pairs={{0,2},{2,0},{4,6},{6,4},{8,10},{10,8},{12,14},{14,12},{1,3},{3,1},... | collective-permute-start | bytes 294920 | tf_op jit(solution)/shard_map/ppermute | solution.py:45
  135.7 5.5 %collective-permute-start.25 = (bf16[3,16,512]{2,1,0:T(8,128)(2,1)S(1)}, bf16[3,16,512]{2,1,0:T(8,128)(2,1)S(1)}, u32[]{:S(2)}, u32[]{:S(2)}) collective-permute-start(bf16[3,16,512]{2,1,0:T(8,128)(2,1)S(1)} %add_convert_fusion.4), channel_id=1, source_target_pairs={{0,12},{2,14},{4,0},{6,2},{8,4},{10,6},{12,8},{14,10},{1,13},{3,15... | collective-permute-start | bytes 147464 | tf_op jit(solution)/shard_map/ppermute | solution.py:31
  139.0 5.0 %collective-permute-start.24 = (bf16[3,16,512]{2,1,0:T(8,128)(2,1)S(1)}, bf16[3,16,512]{2,1,0:T(8,128)(2,1)S(1)}, u32[]{:S(2)}, u32[]{:S(2)}) collective-permute-start(bf16[3,16,512]{2,1,0:T(8,128)(2,1)S(1)} %add_convert_fusion.4), channel_id=1, source_target_pairs={{0,4},{2,6},{4,8},{6,10},{8,12},{10,14},{12,0},{14,2},{1,5},{3,7},... | collective-permute-start | bytes 147464 | tf_op jit(solution)/shard_map/ppermute | solution.py:31
  139.0 7.0 %collective-permute-start.23 = (bf16[3,16,512]{2,1,0:T(8,128)(2,1)S(1)}, bf16[3,16,512]{2,1,0:T(8,128)(2,1)S(1)}, u32[]{:S(2)}, u32[]{:S(2)}) collective-permute-start(bf16[3,16,512]{2,1,0:T(8,128)(2,1)S(1)} %add_convert_fusion.4), channel_id=1, source_target_pairs={{0,8},{2,10},{4,12},{6,14},{8,0},{10,2},{12,4},{14,6},{1,9},{3,11}... | collective-permute-start | bytes 147464 | tf_op jit(solution)/shard_map/ppermute | solution.py:31
  146.1 3.3 %collective-permute-start.28 = (bf16[3,16,512]{2,1,0:T(8,128)(2,1)S(1)}, bf16[3,16,512]{2,1,0:T(8,128)(2,1)S(1)}, u32[]{:S(2)}, u32[]{:S(2)}) collective-permute-start(bf16[3,16,512]{2,1,0:T(8,128)(2,1)S(1)} %add_convert_fusion.3), channel_id=1, source_target_pairs={{0,144},{16,0},{128,16},{144,128},{1,145},{17,1},{129,17},{145,129... | collective-permute-start | bytes 147464 | tf_op jit(solution)/shard_map/ppermute | solution.py:31
  147.0 4.5 %collective-permute-start.27 = (bf16[3,16,512]{2,1,0:T(8,128)(2,1)S(1)}, bf16[3,16,512]{2,1,0:T(8,128)(2,1)S(1)}, u32[]{:S(2)}, u32[]{:S(2)}) collective-permute-start(bf16[3,16,512]{2,1,0:T(8,128)(2,1)S(1)} %add_convert_fusion.3), channel_id=1, source_target_pairs={{0,128},{16,144},{128,0},{144,16},{1,129},{17,145},{129,1},{145,17... | collective-permute-start | bytes 147464 | tf_op jit(solution)/shard_map/ppermute | solution.py:31
  147.2 4.7 %collective-permute-start.26 = (bf16[3,16,512]{2,1,0:T(8,128)(2,1)S(1)}, bf16[3,16,512]{2,1,0:T(8,128)(2,1)S(1)}, u32[]{:S(2)}, u32[]{:S(2)}) collective-permute-start(bf16[3,16,512]{2,1,0:T(8,128)(2,1)S(1)} %add_convert_fusion.3), channel_id=1, source_target_pairs={{0,16},{16,128},{128,144},{144,0},{1,17},{17,129},{129,145},{145,1... | collective-permute-start | bytes 147464 | tf_op jit(solution)/shard_map/ppermute | solution.py:31
  152.0 6.2 %collective-permute-start.30 = (bf16[4,3,16,512]{3,2,1,0:T(8,128)(2,1)S(1)}, bf16[4,3,16,512]{3,2,1,0:T(8,128)(2,1)S(1)}, u32[]{:S(2)}, u32[]{:S(2)}) collective-permute-start(bf16[4,3,16,512]{3,2,1,0:T(8,128)(2,1)S(1)} %get-tuple-element.16), channel_id=1, source_target_pairs={{0,64},{32,96},{64,0},{96,32},{1,65},{33,97},{65,1},{97,33},{2,66}... | collective-permute-start | bytes 589832 | tf_op jit(solution)/shard_map/ppermute | solution.py:31
  153.8 6.4 %collective-permute-start.29 = (bf16[4,3,16,512]{3,2,1,0:T(8,128)(2,1)S(1)}, bf16[4,3,16,512]{3,2,1,0:T(8,128)(2,1)S(1)}, u32[]{:S(2)}, u32[]{:S(2)}) collective-permute-start(bf16[4,3,16,512]{3,2,1,0:T(8,128)(2,1)S(1)} %get-tuple-element.16), channel_id=1, source_target_pairs={{0,32},{32,64},{64,96},{96,0},{1,33},{33,65},{65,97},{97,1},{2,34}... | collective-permute-start | bytes 589832 | tf_op jit(solution)/shard_map/ppermute | solution.py:31
  155.0 5.2 %collective-permute-start.31 = (bf16[4,3,16,512]{3,2,1,0:T(8,128)(2,1)S(1)}, bf16[4,3,16,512]{3,2,1,0:T(8,128)(2,1)S(1)}, u32[]{:S(2)}, u32[]{:S(2)}) collective-permute-start(bf16[4,3,16,512]{3,2,1,0:T(8,128)(2,1)S(1)} %get-tuple-element.16), channel_id=1, source_target_pairs={{0,96},{32,0},{64,32},{96,64},{1,97},{33,1},{65,33},{97,65},{2,98}... | collective-permute-start | bytes 589832 | tf_op jit(solution)/shard_map/ppermute | solution.py:31
  160.3 10.3 %collective-permute-start.32 = (bf16[4,4,3,16,512]{4,3,2,1,0:T(8,128)(2,1)S(1)}, bf16[4,4,3,16,512]{4,3,2,1,0:T(8,128)(2,1)S(1)}, u32[]{:S(2)}, u32[]{:S(2)}) collective-permute-start(bf16[4,4,3,16,512]{4,3,2,1,0:T(8,128)(2,1)S(1)} %pad_maximum_fusion.own), channel_id=1, source_target_pairs={{0,1},{1,0},{2,3},{3,2},{4,5},{5,4},{6,7},{7,6},{8,9},{9,8},{10,11... | collective-permute-start | bytes 2359304 | tf_op jit(solution)/shard_map/ppermute | solution.py:31
  (3 other events, 2.1 us)
where the time goes:
time: 174 us
  waiting for transfers between devices  66.7 us (38%)
  starting transfers between devices  61.6 us (35%)
  Pallas kernels  28.3 us (16%)
  local copies, waits for them, and re-layouts  15 us (9%)
    ppermute x32, waiting for transfers between devices, shifted(): return lax.ppermute(value, axis, [(i, (i + step) % n) for i in range(n)])  63.3 us
    ppermute x32, starting transfers between devices, shifted(): return lax.ppermute(value, axis, [(i, (i + step) % n) for i in range(n)])  54.5 us
    unnamed x35, local copies, waits for them, and re-layouts  15 us
    pallas_call x1, Pallas kernels, body(): pl.pallas_call(weight_kernel, out_shape=(jax.ShapeDtypeStruct((4, 4, rela...  13.2 us
    pallas_call x1, Pallas kernels, body(): pl.pallas_call(mix_kernel, out_shape=jax.ShapeDtypeStruct((16, d_in, TILE...  11 us
    all_to_all x1, starting transfers between devices, body(): mixed = lax.all_to_all(partial, NEAR, 0, 0)  6.94 us
  transfers between devices with their start and end apart: 34, of which 21 were waited for; matrix products, arithmetic and copies ran while one was open for 1% of the time, Pallas kernels for 16%

commit v1 on v0

v1 whole, which is shorter than its diff:
```python
import jax
import jax.numpy as jnp
from jax import lax
from jax.experimental import pallas as pl
from jax.experimental.pallas import tpu as pltpu
from jax.sharding import Mesh
from jax.sharding import PartitionSpec as P


XHI, Y, XLO, Z, CORE = "row_0", "row_1", "col_0", "col_1", "col_2"
ROW = (XHI, Y)
COL = (XLO, Z, CORE)
X4 = (XHI, XLO)

UNROLL = 4
CAP = 32
TILE = 128
F32 = jnp.float32
BF16 = jnp.bfloat16
SMEM = pl.BlockSpec(memory_space=pltpu.SMEM)
VMEM = pl.BlockSpec(memory_space=pltpu.VMEM)
ANY = pl.BlockSpec(memory_space=pltpu.HBM)
BUSY = pl.CostEstimate(flops=40 * 10**9, transcendentals=0, bytes_accessed=2**23)
SMALL = pltpu.CompilerParams(vmem_limit_bytes=8 * 2**20)


def shifted(value, axis, step):
    n = lax.axis_size(axis)
    return lax.ppermute(value, axis, [(i, (i + step) % n) for i in range(n)])


def gathered(value, axes):
    copies = jnp.broadcast_to(value[None], (lax.axis_size(axes), *value.shape))
    return lax.all_to_all(copies, axes, 0, 0)


def swapped(value, axis, step):
    return lax.ppermute(value, axis, [(i, i ^ step) for i in range(lax.axis_size(axis))])


def added(first, *others):
    total = first.astype(F32)
    for other in others:
        total = total + other.astype(F32)
    return total


def columns(core, meta, r, picked, body):
    count = meta[r, 2 * CAP]

    def pick(s, n):
        picked[n] = s
        return n + jnp.where((meta[r, CAP + s] & 1) == core, 1, 0)

    found = lax.fori_loop(0, count, pick, 0)
    for u in range(UNROLL):
        picked[found + u] = 0

    def group(g, carry):
        at = [g * UNROLL + u for u in range(UNROLL)]
        ids = [picked[i] for i in at]
        body([(s, i < found, meta[r, s], meta[r, CAP + s]) for i, s in zip(at, ids)])
        return carry

    lax.fori_loop(0, (found + UNROLL - 1) // UNROLL, group, 0)


def fetches(tiles0, tiles1, tiles, arrived):
    return lambda a, r: pltpu.make_async_copy((tiles0, tiles1)[a].at[r], tiles.at[a, r], arrived.at[a, r])


def masked(tile, keep):
    return jnp.where(keep, tile, jnp.zeros_like(tile))


def turn_kernel(node_in, turned):
    turned[...] = node_in[...].astype(F32).T.astype(BF16)


def meta_kernel(rows, cols, counts, meta):
    for r in range(meta.shape[0]):
        meta[r : r + 1, :CAP] = rows[r, 0]
        meta[r : r + 1, CAP : 2 * CAP] = cols[r, 0]
        meta[r : r + 1, 2 * CAP :] = jnp.full((1, meta.shape[1] - 2 * CAP), counts[r], jnp.int32)


def grad_kernel(g0, g1, g2, g3, grad):
    x_hi, y = lax.axis_index(XHI), lax.axis_index(Y)
    for k, block in enumerate((g0, g1, g2, g3)):
        for a in range(2):
            grad[(x_hi ^ a) * 4 + ((y - k) & 3)] = block[a]


def mix_kernel(
    meta0, meta1, grad0, grad1, weights, tiles0, tiles1,
    kept, sent, sums, picked, operands, mixed_acc, own_acc, held_tiles, arrived,
):
    core, x_lo = lax.axis_index(CORE), lax.axis_index(XLO)
    fetch = fetches(tiles0, tiles1, held_tiles, arrived)
    for r in range(weights.shape[0]):
        for a in range(2):
            fetch(a, r).start()
    d_in = weights.shape[1]
    mixed_acc[...] = jnp.zeros_like(mixed_acc)
    for a, grad in enumerate((grad0, grad1)):
        for k in range(operands.shape[1]):
            operands[a, k, d_in:] = grad[:, TILE * k : TILE * (k + 1)]

    def relation(r, carry):
        own_acc[...] = jnp.zeros_like(own_acc)
        for a, (meta, grad) in enumerate(((meta0, grad0), (meta1, grad1))):
            mixed = jnp.dot(weights[r], grad[...], preferred_element_type=F32).astype(BF16)
            for k in range(operands.shape[1]):
                operands[a, k, :d_in] = mixed[:, TILE * k : TILE * (k + 1)]
            fetch(a, r).wait()

            def group(entries, a=a):
                products = [
                    jnp.dot(operands[a, row], masked(held_tiles[a, r, s], keep), preferred_element_type=F32)
                    for s, keep, row, col in entries
                ]
                for (s, keep, row, col), product in zip(entries, products):
                    mixed_acc[((col >> 4) ^ x_lo) * 8 + ((col >> 1) & 7)] += product[:d_in]
                    own_acc[col >> 1] += product[d_in:]

            columns(core, meta, r, picked, group)
        for k in range(own_acc.shape[0]):
            sums[r, :, TILE * k : TILE * (k + 1)] = own_acc[k].astype(BF16)
        return carry

    lax.fori_loop(0, weights.shape[0], relation, 0)
    kept[...] = mixed_acc[:8].astype(BF16)
    sent[...] = mixed_acc[8:].astype(BF16)


def weight_kernel(inputs, sums, kept, sent, held):
    core, x_hi, y, x_lo = [lax.axis_index(a) for a in (CORE, XHI, Y, XLO)]
    x = x_hi * 2 + x_lo
    for k in range(inputs.shape[0]):
        held[:, TILE * k : TILE * (k + 1)] = inputs[k]
    for r in range(sums.shape[0]):
        terms = lax.dot_general(held[...], sums[r], (((1,), (1,)), ((), ())), preferred_element_type=F32)
        half = terms.shape[0] // 2
        low, high = terms[:half], terms[half:]
        mine = jnp.where(core == 0, low, high)
        theirs = jnp.where(core == 0, high, low).astype(BF16)
        for yb in range(4):
            for xb in range(4):
                d = (yb * 4 + xb) * 16
                kept[(yb - y) & 3, (xb - x) & 3, r] = mine[d : d + 16]
                sent[(yb - y) & 3, (xb - x) & 3, r] = theirs[d : d + 16]


def nodes_kernel(parts, out):
    total = parts[0].astype(F32)
    for k in range(1, parts.shape[0]):
        total += parts[k].astype(F32)
    out[...] = total.T.astype(BF16)


def join_kernel(own, other, out):
    core, x_hi, y, x_lo = [lax.axis_index(a) for a in (CORE, XHI, Y, XLO)]
    x = x_hi * 2 + x_lo
    for a, block in enumerate((own, other)):
        for ky in range(4):
            for kx in range(4):
                d = ((core ^ a) * 16 + ((y - ky) & 3) * 4 + ((x - kx) & 3)) * 16
                out[0, pl.ds(pl.multiple_of(d, 16), 16), :] = block[ky, kx, 0].astype(F32)


def body(out_grad, node_in, weights, tile_vals, tile_rows, tile_cols, tile_count):
    relations, d_in, d_out = weights.shape
    tiles = tile_vals[:, 0, 0]
    rows, width = out_grad.shape

    turned = pl.pallas_call(
        turn_kernel,
        out_shape=jax.ShapeDtypeStruct((d_in, TILE), BF16),
        in_specs=[VMEM],
        out_specs=VMEM,
        compiler_params=SMALL,
        name="turn",
    )(node_in)
    meta = pl.pallas_call(
        meta_kernel,
        out_shape=jax.ShapeDtypeStruct((relations, TILE), jnp.int32),
        in_specs=[VMEM] * 2 + [SMEM],
        out_specs=VMEM,
        compiler_params=SMALL,
        name="meta",
    )(tile_rows, tile_cols, tile_count.reshape(-1))
    packed = out_grad.T
    pair = jnp.stack([packed, shifted(packed, XHI, 1)])
    grads = [pair] + [shifted(pair, Y, k) for k in (1, 2, 3)]
    inputs = gathered(turned, (XLO, Z))
    tiles_near = shifted(tiles, CORE, 1)
    meta_near = shifted(meta, CORE, 1)

    grad = pl.pallas_call(
        grad_kernel,
        out_shape=jax.ShapeDtypeStruct((d_out // width, width, rows), BF16),
        in_specs=[VMEM] * 4,
        out_specs=VMEM,
        compiler_params=SMALL,
        name="join_grad",
    )(*grads).reshape(d_out, rows)
    grad_near = shifted(grad, CORE, 1)

    mixed, mixed_sent, sums = pl.pallas_call(
        mix_kernel,
        out_shape=(
            jax.ShapeDtypeStruct((8, d_in, TILE), BF16),
            jax.ShapeDtypeStruct((8, d_in, TILE), BF16),
            jax.ShapeDtypeStruct((relations, d_out, 16 * TILE), BF16),
        ),
        in_specs=[SMEM] * 2 + [VMEM] * 3 + [ANY] * 2,
        out_specs=(VMEM,) * 3,
        scratch_shapes=[
            pltpu.SMEM((CAP + UNROLL,), jnp.int32),
            pltpu.VMEM((2, rows // TILE, d_in + d_out, TILE), BF16),
            pltpu.VMEM((16, d_in, TILE), F32),
            pltpu.VMEM((16, d_out, TILE), F32),
            pltpu.VMEM((2, *tiles.shape), BF16),
            pltpu.SemaphoreType.DMA((2, relations)),
        ],
        compiler_params=pltpu.CompilerParams(vmem_limit_bytes=50 * 2**20),
        cost_estimate=BUSY,
        name="mix",
    )(meta, meta_near, grad, grad_near, weights, tiles, tiles_near)
    mixed_met = shifted(mixed_sent, XLO, 1)

    kept, sent = pl.pallas_call(
        weight_kernel,
        out_shape=(
            jax.ShapeDtypeStruct((4, 4, relations, 16, d_out), F32),
            jax.ShapeDtypeStruct((4, 4, relations, 16, d_out), BF16),
        ),
        in_specs=[VMEM] * 2,
        out_specs=(VMEM, VMEM),
        scratch_shapes=[pltpu.VMEM((d_in, 16 * TILE), BF16)],
        compiler_params=pltpu.CompilerParams(vmem_limit_bytes=20 * 2**20),
        cost_estimate=BUSY,
        name="weight_terms",
    )(inputs, sums)

    met = shifted(sent, CORE, 1)
    on_y = [added(kept[k], met[k]) for k in range(4)]
    on_y = [on_y[0]] + [shifted(on_y[k].astype(BF16), Y, k) for k in (1, 2, 3)]
    on_y = added(*on_y)
    on_x = added(on_y[0], *[shifted(on_y[k].astype(BF16), X4, k) for k in (1, 2, 3)])
    on_x, mixed_met = lax.optimization_barrier((on_x, mixed_met))
    on_z = (on_x + swapped(on_x, Z, 1)).astype(BF16)
    mixed = added(mixed, mixed_met).astype(BF16)
    mixed = lax.all_to_all(mixed, Z, 0, 0)
    d_nodes = pl.pallas_call(
        nodes_kernel,
        out_shape=jax.ShapeDtypeStruct(node_in.shape, BF16),
        in_specs=[VMEM],
        out_specs=VMEM,
        compiler_params=SMALL,
        name="nodes",
    )(mixed)

    by = [on_z] + [shifted(on_z, Z, k) for k in (2, 4, 6)]
    total = (added(by[0], by[2]) + added(by[1], by[3])).astype(BF16)
    total = jnp.stack([total] + [shifted(total, X4, k) for k in (1, 2, 3)])
    total = jnp.stack([total] + [shifted(total, Y, k) for k in (1, 2, 3)])
    share = pl.BlockSpec((4, 4, 1, 16, d_out), lambda r: (0, 0, r, 0, 0))
    d_weights = pl.pallas_call(
        join_kernel,
        out_shape=jax.ShapeDtypeStruct((relations, d_in, d_out), F32),
        grid=(relations,),
        in_specs=[share, share],
        out_specs=pl.BlockSpec((1, d_in, d_out), lambda r: (r, 0, 0)),
        compiler_params=SMALL,
        name="join",
    )(total, shifted(total, CORE, 1))
    return d_nodes, d_weights


def solution(mesh):
    finer = Mesh(mesh.devices.reshape(2, 4, 2, 8, 2), (XHI, Y, XLO, Z, CORE))
    in_specs = (
        P(COL, ROW),
        P(ROW + COL, None),
        P(),
        P(None, COL, ROW, None, None, None),
        P(None, COL, ROW, None),
        P(None, COL, ROW, None),
        P(None, COL, ROW),
    )
    out_specs = (P(ROW + COL, None), P())
    return jax.shard_map(body, mesh=finer, in_specs=in_specs, out_specs=out_specs, check_vma=False)
```

time: 174 us -> 184 us (1.057)
  waiting for transfers between devices: 66.7 us -> 91.8 us
  local copies, waits for them, and re-layouts: 15 us -> 6.74 us
  starting transfers between devices: 61.6 us -> 54.9 us
    all_to_all x1 -> x2, waiting for transfers between devices: 0.01 us -> 24.9 us  [the longest x1 24.9 us: gathered(): return lax.all_to_all(copies, axes, 0, 0)]
    ppermute x32 -> x25, starting transfers between devices: 54.5 us -> 40.7 us  [shifted(): return lax.ppermute(value, axis, [(i, (i + step) % n) for i in range(n)])]
    unnamed x35 -> x18, local copies, waits for them, and re-layouts: 15 us -> 5.01 us
    pallas_call x1, Pallas kernels: 13.2 us -> 3.52 us  [body(): pl.pallas_call(weight_kernel, out_shape=(jax.ShapeDtypeStruct((4, 4, rela...]
    pallas_call x2 -> x3, Pallas kernels: 11.7 us -> 20.4 us  [the longest x1 19.7 us: body(): pl.pallas_call(mix_kernel, out_shape=(jax.ShapeDtypeStruct((8, d_in, TILE...]
    all_to_all x1 -> x2, starting transfers between devices: 6.94 us -> 13 us  [the longest x1 8.28 us: gathered(): return lax.all_to_all(copies, axes, 0, 0)]
    ppermute x32 -> x25, waiting for transfers between devices: 63.3 us -> 66.9 us  [shifted(): return lax.ppermute(value, axis, [(i, (i + step) % n) for i in range(n)])]
    ppermute x1, waiting for transfers between devices: 3.39 us -> 0.01 us  [swapped(): lax.ppermute(value, axis, [(i, i ^ step) for i in range(lax.axis_size(axi...]
  transfers between devices with their start and end apart: 34 -> 28, of which waited for: 21 -> 20; matrix products, arithmetic and copies ran while one was open for 1% -> 2% of each run, Pallas kernels for 16% -> 12%
where the time goes in v1:
time: 184 us
  waiting for transfers between devices  91.8 us (50%)
  starting transfers between devices  54.9 us (30%)
  Pallas kernels  27.1 us (15%)
  local copies, waits for them, and re-layouts  6.74 us (4%)
  other arithmetic  2.79 us (2%)
    ppermute x25, waiting for transfers between devices, shifted(): return lax.ppermute(value, axis, [(i, (i + step) % n) for i in range(n)])  66.9 us
    ppermute x25, starting transfers between devices, shifted(): return lax.ppermute(value, axis, [(i, (i + step) % n) for i in range(n)])  40.7 us
    all_to_all x1, waiting for transfers between devices, gathered(): return lax.all_to_all(copies, axes, 0, 0)  24.9 us
    pallas_call x1, Pallas kernels, body(): pl.pallas_call(mix_kernel, out_shape=(jax.ShapeDtypeStruct((8, d_in, TILE...  19.7 us
    all_to_all x1, starting transfers between devices, gathered(): return lax.all_to_all(copies, axes, 0, 0)  8.28 us
    unnamed x18, local copies, waits for them, and re-layouts  5.01 us
    all_to_all x1, starting transfers between devices, body(): mixed = lax.all_to_all(mixed, Z, 0, 0)  4.75 us
  transfers between devices with their start and end apart: 28, of which 20 were waited for; matrix products, arithmetic and copies ran while one was open for 2% of the time, Pallas kernels for 12%

profile of v1, /device:TPU:1, one launch (start us, length us, event | category | flops | bytes accessed | tf_op | source)
XLA Modules:
  0.0 184.2 jit_solution(7685954288991666154)
XLA Ops:
  0.6 3.3 %collective-permute-start.6 = (bf16[3,32,128,128]{3,2,1,0:T(8,128)(2,1)}, bf16[3,32,128,128]{3,2,1,0:T(8,128)(2,1)}, u32[]{:S(2)}, u32[]{:S(2)}) collective-permute-start(bf16[3,32,128,128]{3,2,1,0:T(8,128)(2,1)} %bitcast.56), channel_id=1, source_target_pairs={{0,1},{1,0},{2,3},{3,2},{4,5},{5,4},{6,7},{7,6},{8,9},{9,8},{10,11... | collective-permute-start | bytes 9437192 | tf_op jit(solution)/shard_map/ppermute | solution.py:29
  3.9 1.0 collective-permute-start.1
  5.0 5.6 %collective-permute-done.1 = bf16[64,1024]{1,0:T(8,128)(2,1)S(1)} collective-permute-done((bf16[64,1024]{1,0:T(8,128)(2,1)}, bf16[64,1024]{1,0:T(8,128)(2,1)S(1)}, u32[]{:S(2)}, u32[]{:S(2)}) %collective-permute-start.1) | collective-permute-done | bytes 131104 | tf_op jit(solution)/shard_map/ppermute | solution.py:29
  10.6 0.9 pad_maximum_fusion.1.g0
  11.6 2.2 %collective-permute-start.3 = (bf16[2,64,1024]{2,1,0:T(8,128)(2,1)S(1)}, bf16[2,64,1024]{2,1,0:T(8,128)(2,1)S(1)}, u32[]{:S(2)}, u32[]{:S(2)}) collective-permute-start(bf16[2,64,1024]{2,1,0:T(8,128)(2,1)S(1)} %pad_maximum_fusion.1.g0), channel_id=1, source_target_pairs={{0,64},{32,96},{64,0},{96,32},{1,65},{33,97},{65,1},{97,33},{2,66}... | collective-permute-start | bytes 786440 | tf_op jit(solution)/shard_map/ppermute | solution.py:29
  13.8 1.1 collective-permute-start.4
  14.9 5.3 %collective-permute-done.2.g1 = bf16[2,64,1024]{2,1,0:T(8,128)(2,1)S(1)} collective-permute-done((bf16[2,64,1024]{2,1,0:T(8,128)(2,1)S(1)}, bf16[2,64,1024]{2,1,0:T(8,128)(2,1)S(1)}, u32[]{:S(2)}, u32[]{:S(2)}) %collective-permute-start.2) | collective-permute-done | bytes 262176 | tf_op jit(solution)/shard_map/ppermute | solution.py:29
  20.2 4.7 %collective-permute-done.3.g2 = bf16[2,64,1024]{2,1,0:T(8,128)(2,1)S(1)} collective-permute-done((bf16[2,64,1024]{2,1,0:T(8,128)(2,1)S(1)}, bf16[2,64,1024]{2,1,0:T(8,128)(2,1)S(1)}, u32[]{:S(2)}, u32[]{:S(2)}) %collective-permute-start.3) | collective-permute-done | bytes 262176 | tf_op jit(solution)/shard_map/ppermute | solution.py:29
  24.9 1.3 collective-permute-done.4.g3
  26.3 1.6 collective-permute-start.5
  28.1 1.7 broadcast_in_dim.2
  29.8 8.3 %all-to-all-start = ((bf16[16,512,128]{2,1,0:T(8,128)(2,1)}), bf16[16,512,128]{2,1,0:T(8,128)(2,1)S(1)}, u32[]{:S(2)}, u32[]{:S(2)}) async-start(bf16[16,512,128]{2,1,0:T(8,128)(2,1)} %broadcast_in_dim.2), calls=%async_computation | async-start | bytes 4194304 | tf_op jit(solution)/shard_map/all_to_all | solution.py:34
  39.1 0.9 collective-permute-done.meta1
  39.9 1.2 copy-done.1
  41.2 19.7 %mix.1 = (bf16[8,512,128]{2,1,0:T(8,128)(2,1)S(1)}, bf16[8,512,128]{2,1,0:T(8,128)(2,1)S(1)}, bf16[3,512,2048]{2,1,0:T(8,128)(2,1)}) custom-call(s32[3,128]{1,0:T(4,128)S(1)} %meta.1.meta0, s32[3,128]{1,0:T(4,128)S(1)} %collective-permute-done.meta1, bf16[512,1024]{1,0:T(8,128)(2,1)S(1)} %bitcast.44, bf16[512,1024]{1,0:T(8,128)(2,1)} %collective-permute-done.5.grad1, ...), custom_call_target="tpu_custom_call" | custom-call | flops 40000000000 | bytes 8388608 | tf_op jit(solution)/shard_map/mix/pallas_call | solution.py:209
  60.8 1.0 copy-done.6
  61.8 24.9 %all-to-all-done.inputs = bf16[16,512,128]{2,1,0:T(8,128)(2,1)S(1)} async-done(((bf16[16,512,128]{2,1,0:T(8,128)(2,1)}), bf16[16,512,128]{2,1,0:T(8,128)(2,1)S(1)}, u32[]{:S(2)}, u32[]{:S(2)}) %all-to-all-start) | async-done | bytes 2097184 | tf_op jit(solution)/shard_map/all_to_all | solution.py:34
  86.7 2.8 %copy-done.8 = bf16[3,512,2048]{2,1,0:T(8,128)(2,1)S(1)} copy-done((bf16[3,512,2048]{2,1,0:T(8,128)(2,1)S(1)}, bf16[3,512,2048]{2,1,0:T(8,128)(2,1)}, u32[]{:S(2)}) %copy-start.8) | copy-done | bytes 6291480
  89.5 3.5 %weight_terms.1 = (f32[4,4,3,16,512]{4,3,2,1,0:T(8,128)S(1)}, bf16[4,4,3,16,512]{4,3,2,1,0:T(8,128)(2,1)S(1)}) custom-call(bf16[16,512,128]{2,1,0:T(8,128)(2,1)S(1)} %all-to-all-done.inputs, bf16[3,512,2048]{2,1,0:T(8,128)(2,1)S(1)} %copy-done.8), custom_call_target="tpu_custom_call" | custom-call | flops 40000000000 | bytes 8388608 | tf_op jit(solution)/shard_map/weight_terms/pallas_call | solution.py:232
  93.0 1.3 collective-permute-start.7
  95.1 1.1 collective-permute-done.7
  96.4 2.0 %collective-permute-start.10 = (bf16[4,3,16,512]{3,2,1,0:T(8,128)(2,1)S(1)}, bf16[4,3,16,512]{3,2,1,0:T(8,128)(2,1)S(1)}, u32[]{:S(2)}, u32[]{:S(2)}) collective-permute-start(bf16[4,3,16,512]{3,2,1,0:T(8,128)(2,1)S(1)} %get-tuple-element.19), channel_id=1, source_target_pairs={{0,96},{32,0},{64,32},{96,64},{1,97},{33,1},{65,33},{97,65},{2,98}... | collective-permute-start | bytes 589832 | tf_op jit(solution)/shard_map/ppermute | solution.py:29
  98.4 1.9 %collective-permute-start.9 = (bf16[4,3,16,512]{3,2,1,0:T(8,128)(2,1)S(1)}, bf16[4,3,16,512]{3,2,1,0:T(8,128)(2,1)S(1)}, u32[]{:S(2)}, u32[]{:S(2)}) collective-permute-start(bf16[4,3,16,512]{3,2,1,0:T(8,128)(2,1)S(1)} %get-tuple-element.20), channel_id=1, source_target_pairs={{0,64},{32,96},{64,0},{96,32},{1,65},{33,97},{65,1},{97,33},{2,66}... | collective-permute-start | bytes 589832 | tf_op jit(solution)/shard_map/ppermute | solution.py:29
  100.2 2.3 %collective-permute-done.10 = bf16[4,3,16,512]{3,2,1,0:T(8,128)(2,1)S(1)} collective-permute-done((bf16[4,3,16,512]{3,2,1,0:T(8,128)(2,1)S(1)}, bf16[4,3,16,512]{3,2,1,0:T(8,128)(2,1)S(1)}, u32[]{:S(2)}, u32[]{:S(2)}) %collective-permute-start.10) | collective-permute-done | bytes 196640 | tf_op jit(solution)/shard_map/ppermute | solution.py:29
  102.6 3.6 %collective-permute-done.8 = bf16[4,3,16,512]{3,2,1,0:T(8,128)(2,1)S(1)} collective-permute-done((bf16[4,3,16,512]{3,2,1,0:T(8,128)(2,1)S(1)}, bf16[4,3,16,512]{3,2,1,0:T(8,128)(2,1)S(1)}, u32[]{:S(2)}, u32[]{:S(2)}) %collective-permute-start.8) | collective-permute-done | bytes 196640 | tf_op jit(solution)/shard_map/ppermute | solution.py:29
  106.2 2.7 %collective-permute-done.9 = bf16[4,3,16,512]{3,2,1,0:T(8,128)(2,1)S(1)} collective-permute-done((bf16[4,3,16,512]{3,2,1,0:T(8,128)(2,1)S(1)}, bf16[4,3,16,512]{3,2,1,0:T(8,128)(2,1)S(1)}, u32[]{:S(2)}, u32[]{:S(2)}) %collective-permute-start.9) | collective-permute-done | bytes 196640 | tf_op jit(solution)/shard_map/ppermute | solution.py:29
  109.0 0.9 collective-permute-start.11
  109.9 2.4 %collective-permute-start.12 = (bf16[3,16,512]{2,1,0:T(8,128)(2,1)S(1)}, bf16[3,16,512]{2,1,0:T(8,128)(2,1)S(1)}, u32[]{:S(2)}, u32[]{:S(2)}) collective-permute-start(bf16[3,16,512]{2,1,0:T(8,128)(2,1)S(1)} %get-tuple-element.25), channel_id=1, source_target_pairs={{0,128},{16,144},{128,0},{144,16},{1,129},{17,145},{129,1},{145,17... | collective-permute-start | bytes 147464 | tf_op jit(solution)/shard_map/ppermute | solution.py:29
  112.4 1.2 collective-permute-start.13
  113.6 4.8 %collective-permute-done.11 = bf16[3,16,512]{2,1,0:T(8,128)(2,1)S(1)} collective-permute-done((bf16[3,16,512]{2,1,0:T(8,128)(2,1)S(1)}, bf16[3,16,512]{2,1,0:T(8,128)(2,1)S(1)}, u32[]{:S(2)}, u32[]{:S(2)}) %collective-permute-start.11) | collective-permute-done | bytes 49184 | tf_op jit(solution)/shard_map/ppermute | solution.py:29
  118.4 3.9 %collective-permute-done.12 = bf16[3,16,512]{2,1,0:T(8,128)(2,1)S(1)} collective-permute-done((bf16[3,16,512]{2,1,0:T(8,128)(2,1)S(1)}, bf16[3,16,512]{2,1,0:T(8,128)(2,1)S(1)}, u32[]{:S(2)}, u32[]{:S(2)}) %collective-permute-start.12) | collective-permute-done | bytes 49184 | tf_op jit(solution)/shard_map/ppermute | solution.py:29
  122.4 1.2 collective-permute-start.15
  123.6 1.3 add_convert_fusion
  124.8 4.8 %all-to-all-start.1 = ((bf16[8,512,128]{2,1,0:T(8,128)(2,1)}), bf16[8,512,128]{2,1,0:T(8,128)(2,1)S(1)}, u32[]{:S(2)}, u32[]{:S(2)}) async-start(bf16[8,512,128]{2,1,0:T(8,128)(2,1)} %add_convert_fusion), calls=%async_computation.1 | async-start | bytes 2097152 | tf_op jit(solution)/shard_map/all_to_all | solution.py:254
  129.6 5.4 %collective-permute-start.16 = (bf16[3,16,512]{2,1,0:T(8,128)(2,1)S(1)}, bf16[3,16,512]{2,1,0:T(8,128)(2,1)S(1)}, u32[]{:S(2)}, u32[]{:S(2)}) collective-permute-start(bf16[3,16,512]{2,1,0:T(8,128)(2,1)S(1)} %add_convert_fusion.5), channel_id=1, source_target_pairs={{0,8},{2,10},{4,12},{6,14},{8,0},{10,2},{12,4},{14,6},{1,9},{3,11}... | collective-permute-start | bytes 147464 | tf_op jit(solution)/shard_map/ppermute | solution.py:29
  135.3 3.3 %collective-permute-start.18 = (bf16[3,16,512]{2,1,0:T(8,128)(2,1)S(1)}, bf16[3,16,512]{2,1,0:T(8,128)(2,1)S(1)}, u32[]{:S(2)}, u32[]{:S(2)}) collective-permute-start(bf16[3,16,512]{2,1,0:T(8,128)(2,1)S(1)} %add_convert_fusion.5), channel_id=1, source_target_pairs={{0,12},{2,14},{4,0},{6,2},{8,4},{10,6},{12,8},{14,10},{1,13},{3,15... | collective-permute-start | bytes 147464 | tf_op jit(solution)/shard_map/ppermute | solution.py:29
  138.6 21.5 %collective-permute-done.16 = bf16[3,16,512]{2,1,0:T(8,128)(2,1)S(1)} collective-permute-done((bf16[3,16,512]{2,1,0:T(8,128)(2,1)S(1)}, bf16[3,16,512]{2,1,0:T(8,128)(2,1)S(1)}, u32[]{:S(2)}, u32[]{:S(2)}) %collective-permute-start.16) | collective-permute-done | bytes 49184 | tf_op jit(solution)/shard_map/ppermute | solution.py:29
  161.0 1.9 %collective-permute-start.21 = (bf16[3,16,512]{2,1,0:T(8,128)(2,1)S(1)}, bf16[3,16,512]{2,1,0:T(8,128)(2,1)S(1)}, u32[]{:S(2)}, u32[]{:S(2)}) collective-permute-start(bf16[3,16,512]{2,1,0:T(8,128)(2,1)S(1)} %add_convert_fusion.4), channel_id=1, source_target_pairs={{0,144},{16,0},{128,16},{144,128},{1,145},{17,1},{129,17},{145,129... | collective-permute-start | bytes 147464 | tf_op jit(solution)/shard_map/ppermute | solution.py:29
  162.9 1.6 collective-permute-done.19
  165.5 1.0 collective-permute-start.22
  166.6 2.1 %collective-permute-start.23 = (bf16[4,3,16,512]{3,2,1,0:T(8,128)(2,1)S(1)}, bf16[4,3,16,512]{3,2,1,0:T(8,128)(2,1)S(1)}, u32[]{:S(2)}, u32[]{:S(2)}) collective-permute-start(bf16[4,3,16,512]{3,2,1,0:T(8,128)(2,1)S(1)} %get-tuple-element.22), channel_id=1, source_target_pairs={{0,64},{32,96},{64,0},{96,32},{1,65},{33,97},{65,1},{97,33},{2,66}... | collective-permute-start | bytes 589832 | tf_op jit(solution)/shard_map/ppermute | solution.py:29
  168.7 1.3 collective-permute-start.24
  170.0 1.4 collective-permute-done.22
  171.3 3.2 %collective-permute-done.23 = bf16[4,3,16,512]{3,2,1,0:T(8,128)(2,1)S(1)} collective-permute-done((bf16[4,3,16,512]{3,2,1,0:T(8,128)(2,1)S(1)}, bf16[4,3,16,512]{3,2,1,0:T(8,128)(2,1)S(1)}, u32[]{:S(2)}, u32[]{:S(2)}) %collective-permute-start.23) | collective-permute-done | bytes 196640 | tf_op jit(solution)/shard_map/ppermute | solution.py:29
  174.8 4.3 %collective-permute-start.25 = (bf16[4,4,3,16,512]{4,3,2,1,0:T(8,128)(2,1)S(1)}, bf16[4,4,3,16,512]{4,3,2,1,0:T(8,128)(2,1)S(1)}, u32[]{:S(2)}, u32[]{:S(2)}) collective-permute-start(bf16[4,4,3,16,512]{4,3,2,1,0:T(8,128)(2,1)S(1)} %pad_maximum_fusion.own), channel_id=1, source_target_pairs={{0,1},{1,0},{2,3},{3,2},{4,5},{5,4},{6,7},{7,6},{8,9},{9,8},{10,11... | collective-permute-start | bytes 2359304 | tf_op jit(solution)/shard_map/ppermute | solution.py:29
  179.1 1.9 %collective-permute-done.25.other = bf16[4,4,3,16,512]{4,3,2,1,0:T(8,128)(2,1)S(1)} collective-permute-done((bf16[4,4,3,16,512]{4,3,2,1,0:T(8,128)(2,1)S(1)}, bf16[4,4,3,16,512]{4,3,2,1,0:T(8,128)(2,1)S(1)}, u32[]{:S(2)}, u32[]{:S(2)}) %collective-permute-start.25) | collective-permute-done | bytes 786464 | tf_op jit(solution)/shard_map/ppermute | solution.py:29
  181.0 2.3 %join.1 = f32[3,512,512]{2,1,0:T(8,128)} custom-call(bf16[4,4,3,16,512]{4,3,2,1,0:T(8,128)(2,1)S(1)} %pad_maximum_fusion.own, bf16[4,4,3,16,512]{4,3,2,1,0:T(8,128)(2,1)S(1)} %collective-permute-done.25.other), custom_call_target="tpu_custom_call" | custom-call | tf_op jit(solution)/shard_map/join/pallas_call | solution.py:269
  183.3 0.9 nodes.1
  (44 shorter events, 5.1 us)
Async XLA Ops:
  0.6 27.3 %copy-start.2 = (bf16[128,512]{1,0:T(8,128)(2,1)S(1)}, bf16[128,512]{1,0:T(8,128)(2,1)}, u32[]{:S(2)}) copy-start(bf16[128,512]{1,0:T(8,128)(2,1)} %node_in.1) | copy-start | bytes 393220
  0.6 39.3 %collective-permute-start.6 = (bf16[3,32,128,128]{3,2,1,0:T(8,128)(2,1)}, bf16[3,32,128,128]{3,2,1,0:T(8,128)(2,1)}, u32[]{:S(2)}, u32[]{:S(2)}) collective-permute-start(bf16[3,32,128,128]{3,2,1,0:T(8,128)(2,1)} %bitcast.56), channel_id=1, source_target_pairs={{0,1},{1,0},{2,3},{3,2},{4,5},{5,4},{6,7},{7,6},{8,9},{9,8},{10,11... | collective-permute-start | bytes 9437192 | tf_op jit(solution)/shard_map/ppermute | solution.py:29
  3.9 6.7 %collective-permute-start.1 = (bf16[64,1024]{1,0:T(8,128)(2,1)}, bf16[64,1024]{1,0:T(8,128)(2,1)S(1)}, u32[]{:S(2)}, u32[]{:S(2)}) collective-permute-start(bf16[64,1024]{1,0:T(8,128)(2,1)} %bitcast.50), channel_id=1, source_target_pairs={{0,128},{128,0},{1,129},{129,1},{2,130},{130,2},{3,131},{131,3},{4... | collective-permute-start | bytes 393224 | tf_op jit(solution)/shard_map/ppermute | solution.py:29
  11.5 8.7 %collective-permute-start.2 = (bf16[2,64,1024]{2,1,0:T(8,128)(2,1)S(1)}, bf16[2,64,1024]{2,1,0:T(8,128)(2,1)S(1)}, u32[]{:S(2)}, u32[]{:S(2)}) collective-permute-start(bf16[2,64,1024]{2,1,0:T(8,128)(2,1)S(1)} %pad_maximum_fusion.1.g0), channel_id=1, source_target_pairs={{0,32},{32,64},{64,96},{96,0},{1,33},{33,65},{65,97},{97,1},{2,34}... | collective-permute-start | bytes 786440 | tf_op jit(solution)/shard_map/ppermute | solution.py:29
  11.6 13.3 %collective-permute-start.3 = (bf16[2,64,1024]{2,1,0:T(8,128)(2,1)S(1)}, bf16[2,64,1024]{2,1,0:T(8,128)(2,1)S(1)}, u32[]{:S(2)}, u32[]{:S(2)}) collective-permute-start(bf16[2,64,1024]{2,1,0:T(8,128)(2,1)S(1)} %pad_maximum_fusion.1.g0), channel_id=1, source_target_pairs={{0,64},{32,96},{64,0},{96,32},{1,65},{33,97},{65,1},{97,33},{2,66}... | collective-permute-start | bytes 786440 | tf_op jit(solution)/shard_map/ppermute | solution.py:29
  13.8 12.4 %collective-permute-start.4 = (bf16[2,64,1024]{2,1,0:T(8,128)(2,1)S(1)}, bf16[2,64,1024]{2,1,0:T(8,128)(2,1)S(1)}, u32[]{:S(2)}, u32[]{:S(2)}) collective-permute-start(bf16[2,64,1024]{2,1,0:T(8,128)(2,1)S(1)} %pad_maximum_fusion.1.g0), channel_id=1, source_target_pairs={{0,96},{32,0},{64,32},{96,64},{1,97},{33,1},{65,33},{97,65},{2,98}... | collective-permute-start | bytes 786440 | tf_op jit(solution)/shard_map/ppermute | solution.py:29
  26.3 3.5 %copy-start = (bf16[8,64,1024]{2,1,0:T(8,128)(2,1)}, bf16[8,64,1024]{2,1,0:T(8,128)(2,1)S(1)}, u32[]{:S(2)}) copy-start(bf16[8,64,1024]{2,1,0:T(8,128)(2,1)S(1)} %join_grad.1) | copy-start | bytes 3145732
  26.3 13.6 %collective-permute-start.5 = (bf16[512,1024]{1,0:T(8,128)(2,1)S(1)}, bf16[512,1024]{1,0:T(8,128)(2,1)}, u32[]{:S(2)}, u32[]{:S(2)}) collective-permute-start(bf16[512,1024]{1,0:T(8,128)(2,1)S(1)} %bitcast.43), channel_id=1, source_target_pairs={{0,1},{1,0},{2,3},{3,2},{4,5},{5,4},{6,7},{7,6},{8,9},{9,8},{10,11... | collective-permute-start | bytes 3145736 | tf_op jit(solution)/shard_map/ppermute | solution.py:29
  29.8 8.3 %copy-start.3 = (s32[3,1,1,32]{3,2,1,0:T(1,128)S(1)}, s32[3,1,1,32]{3,2,1,0:T(1,128)}, u32[]{:S(2)}) copy-start(s32[3,1,1,32]{3,2,1,0:T(1,128)} %rows.1) | copy-start | bytes 1156
  29.8 8.3 %copy-start.4 = (s32[3,1,1,32]{3,2,1,0:T(1,128)S(1)}, s32[3,1,1,32]{3,2,1,0:T(1,128)}, u32[]{:S(2)}) copy-start(s32[3,1,1,32]{3,2,1,0:T(1,128)} %cols.1) | copy-start | bytes 1156
  29.8 8.3 %copy-start.5 = (s32[3,1,1]{0,2,1:T(1,128)S(1)}, s32[3,1,1]{0,2,1:T(1,128)}, u32[]{:S(2)}) copy-start(s32[3,1,1]{0,2,1:T(1,128)} %param.13) | copy-start | bytes 40
  29.8 56.9 %all-to-all-start = ((bf16[16,512,128]{2,1,0:T(8,128)(2,1)}), bf16[16,512,128]{2,1,0:T(8,128)(2,1)S(1)}, u32[]{:S(2)}, u32[]{:S(2)}) async-start(bf16[16,512,128]{2,1,0:T(8,128)(2,1)} %broadcast_in_dim.2), calls=%async_computation | async-start | bytes 4194304 | tf_op jit(solution)/shard_map/all_to_all | solution.py:34
  38.7 1.2 collective-permute-start
  39.9 1.2 copy-start.1
  60.8 1.0 copy-start.6
  86.7 2.8 %copy-start.8 = (bf16[3,512,2048]{2,1,0:T(8,128)(2,1)S(1)}, bf16[3,512,2048]{2,1,0:T(8,128)(2,1)}, u32[]{:S(2)}) copy-start(bf16[3,512,2048]{2,1,0:T(8,128)(2,1)} %get-tuple-element.10.sums) | copy-start | bytes 18874372
  89.5 4.8 %copy-start.7 = (bf16[8,512,128]{2,1,0:T(8,128)(2,1)S(1)}, bf16[8,512,128]{2,1,0:T(8,128)(2,1)}, u32[]{:S(2)}) copy-start(bf16[8,512,128]{2,1,0:T(8,128)(2,1)} %copy-done.6) | copy-start | bytes 3145732
  93.0 3.2 %collective-permute-start.7 = (bf16[4,4,3,16,512]{4,3,2,1,0:T(8,128)(2,1)S(1)}, bf16[4,4,3,16,512]{4,3,2,1,0:T(8,128)(2,1)S(1)}, u32[]{:S(2)}, u32[]{:S(2)}) collective-permute-start(bf16[4,4,3,16,512]{4,3,2,1,0:T(8,128)(2,1)S(1)} %get-tuple-element.12), channel_id=1, source_target_pairs={{0,1},{1,0},{2,3},{3,2},{4,5},{5,4},{6,7},{7,6},{8,9},{9,8},{10,11... | collective-permute-start | bytes 2359304 | tf_op jit(solution)/shard_map/ppermute | solution.py:29
  94.2 28.1 %collective-permute-start.14 = (bf16[8,512,128]{2,1,0:T(8,128)(2,1)S(1)}, bf16[8,512,128]{2,1,0:T(8,128)(2,1)S(1)}, u32[]{:S(2)}, u32[]{:S(2)}) collective-permute-start(bf16[8,512,128]{2,1,0:T(8,128)(2,1)S(1)} %copy-done.7), channel_id=1, source_target_pairs={{0,16},{16,0},{1,17},{17,1},{2,18},{18,2},{3,19},{19,3},{4,20},{20... | collective-permute-start | bytes 3145736 | tf_op jit(solution)/shard_map/ppermute | solution.py:29
  96.4 6.2 %collective-permute-start.10 = (bf16[4,3,16,512]{3,2,1,0:T(8,128)(2,1)S(1)}, bf16[4,3,16,512]{3,2,1,0:T(8,128)(2,1)S(1)}, u32[]{:S(2)}, u32[]{:S(2)}) collective-permute-start(bf16[4,3,16,512]{3,2,1,0:T(8,128)(2,1)S(1)} %get-tuple-element.19), channel_id=1, source_target_pairs={{0,96},{32,0},{64,32},{96,64},{1,97},{33,1},{65,33},{97,65},{2,98}... | collective-permute-start | bytes 589832 | tf_op jit(solution)/shard_map/ppermute | solution.py:29
  98.4 7.8 %collective-permute-start.8 = (bf16[4,3,16,512]{3,2,1,0:T(8,128)(2,1)S(1)}, bf16[4,3,16,512]{3,2,1,0:T(8,128)(2,1)S(1)}, u32[]{:S(2)}, u32[]{:S(2)}) collective-permute-start(bf16[4,3,16,512]{3,2,1,0:T(8,128)(2,1)S(1)} %get-tuple-element.18), channel_id=1, source_target_pairs={{0,32},{32,64},{64,96},{96,0},{1,33},{33,65},{65,97},{97,1},{2,34}... | collective-permute-start | bytes 589832 | tf_op jit(solution)/shard_map/ppermute | solution.py:29
  98.4 10.5 %collective-permute-start.9 = (bf16[4,3,16,512]{3,2,1,0:T(8,128)(2,1)S(1)}, bf16[4,3,16,512]{3,2,1,0:T(8,128)(2,1)S(1)}, u32[]{:S(2)}, u32[]{:S(2)}) collective-permute-start(bf16[4,3,16,512]{3,2,1,0:T(8,128)(2,1)S(1)} %get-tuple-element.20), channel_id=1, source_target_pairs={{0,64},{32,96},{64,0},{96,32},{1,65},{33,97},{65,1},{97,33},{2,66}... | collective-permute-start | bytes 589832 | tf_op jit(solution)/shard_map/ppermute | solution.py:29
  109.0 9.4 %collective-permute-start.11 = (bf16[3,16,512]{2,1,0:T(8,128)(2,1)S(1)}, bf16[3,16,512]{2,1,0:T(8,128)(2,1)S(1)}, u32[]{:S(2)}, u32[]{:S(2)}) collective-permute-start(bf16[3,16,512]{2,1,0:T(8,128)(2,1)S(1)} %get-tuple-element.23), channel_id=1, source_target_pairs={{0,16},{16,128},{128,144},{144,0},{1,17},{17,129},{129,145},{145,1... | collective-permute-start | bytes 147464 | tf_op jit(solution)/shard_map/ppermute | solution.py:29
  109.9 12.4 %collective-permute-start.12 = (bf16[3,16,512]{2,1,0:T(8,128)(2,1)S(1)}, bf16[3,16,512]{2,1,0:T(8,128)(2,1)S(1)}, u32[]{:S(2)}, u32[]{:S(2)}) collective-permute-start(bf16[3,16,512]{2,1,0:T(8,128)(2,1)S(1)} %get-tuple-element.25), channel_id=1, source_target_pairs={{0,128},{16,144},{128,0},{144,16},{1,129},{17,145},{129,1},{145,17... | collective-permute-start | bytes 147464 | tf_op jit(solution)/shard_map/ppermute | solution.py:29
  112.4 9.9 %collective-permute-start.13 = (bf16[3,16,512]{2,1,0:T(8,128)(2,1)S(1)}, bf16[3,16,512]{2,1,0:T(8,128)(2,1)S(1)}, u32[]{:S(2)}, u32[]{:S(2)}) collective-permute-start(bf16[3,16,512]{2,1,0:T(8,128)(2,1)S(1)} %get-tuple-element.24), channel_id=1, source_target_pairs={{0,144},{16,0},{128,16},{144,128},{1,145},{17,1},{129,17},{145,129... | collective-permute-start | bytes 147464 | tf_op jit(solution)/shard_map/ppermute | solution.py:29
  122.4 7.2 %collective-permute-start.15 = (f32[3,16,512]{2,1,0:T(8,128)S(1)}, f32[3,16,512]{2,1,0:T(8,128)S(1)}, u32[]{:S(2)}, u32[]{:S(2)}) collective-permute-start(f32[3,16,512]{2,1,0:T(8,128)S(1)} %fusion.7), channel_id=1, source_target_pairs={{0,2},{2,0},{4,6},{6,4},{8,10},{10,8},{12,14},{14,12},{1,3},{3,1},... | collective-permute-start | bytes 294920 | tf_op jit(solution)/shard_map/ppermute | solution.py:38
  124.8 58.5 %all-to-all-start.1 = ((bf16[8,512,128]{2,1,0:T(8,128)(2,1)}), bf16[8,512,128]{2,1,0:T(8,128)(2,1)S(1)}, u32[]{:S(2)}, u32[]{:S(2)}) async-start(bf16[8,512,128]{2,1,0:T(8,128)(2,1)} %add_convert_fusion), calls=%async_computation.1 | async-start | bytes 2097152 | tf_op jit(solution)/shard_map/all_to_all | solution.py:254
  129.6 30.5 %collective-permute-start.16 = (bf16[3,16,512]{2,1,0:T(8,128)(2,1)S(1)}, bf16[3,16,512]{2,1,0:T(8,128)(2,1)S(1)}, u32[]{:S(2)}, u32[]{:S(2)}) collective-permute-start(bf16[3,16,512]{2,1,0:T(8,128)(2,1)S(1)} %add_convert_fusion.5), channel_id=1, source_target_pairs={{0,8},{2,10},{4,12},{6,14},{8,0},{10,2},{12,4},{14,6},{1,9},{3,11}... | collective-permute-start | bytes 147464 | tf_op jit(solution)/shard_map/ppermute | solution.py:29
  135.1 25.1 %collective-permute-start.17 = (bf16[3,16,512]{2,1,0:T(8,128)(2,1)S(1)}, bf16[3,16,512]{2,1,0:T(8,128)(2,1)S(1)}, u32[]{:S(2)}, u32[]{:S(2)}) collective-permute-start(bf16[3,16,512]{2,1,0:T(8,128)(2,1)S(1)} %add_convert_fusion.5), channel_id=1, source_target_pairs={{0,4},{2,6},{4,8},{6,10},{8,12},{10,14},{12,0},{14,2},{1,5},{3,7},... | collective-permute-start | bytes 147464 | tf_op jit(solution)/shard_map/ppermute | solution.py:29
  135.3 24.8 %collective-permute-start.18 = (bf16[3,16,512]{2,1,0:T(8,128)(2,1)S(1)}, bf16[3,16,512]{2,1,0:T(8,128)(2,1)S(1)}, u32[]{:S(2)}, u32[]{:S(2)}) collective-permute-start(bf16[3,16,512]{2,1,0:T(8,128)(2,1)S(1)} %add_convert_fusion.5), channel_id=1, source_target_pairs={{0,12},{2,14},{4,0},{6,2},{8,4},{10,6},{12,8},{14,10},{1,13},{3,15... | collective-permute-start | bytes 147464 | tf_op jit(solution)/shard_map/ppermute | solution.py:29
  160.1 4.4 %collective-permute-start.19 = (bf16[3,16,512]{2,1,0:T(8,128)(2,1)S(1)}, bf16[3,16,512]{2,1,0:T(8,128)(2,1)S(1)}, u32[]{:S(2)}, u32[]{:S(2)}) collective-permute-start(bf16[3,16,512]{2,1,0:T(8,128)(2,1)S(1)} %add_convert_fusion.4), channel_id=1, source_target_pairs={{0,16},{16,128},{128,144},{144,0},{1,17},{17,129},{129,145},{145,1... | collective-permute-start | bytes 147464 | tf_op jit(solution)/shard_map/ppermute | solution.py:29
  160.2 4.8 %collective-permute-start.20 = (bf16[3,16,512]{2,1,0:T(8,128)(2,1)S(1)}, bf16[3,16,512]{2,1,0:T(8,128)(2,1)S(1)}, u32[]{:S(2)}, u32[]{:S(2)}) collective-permute-start(bf16[3,16,512]{2,1,0:T(8,128)(2,1)S(1)} %add_convert_fusion.4), channel_id=1, source_target_pairs={{0,128},{16,144},{128,0},{144,16},{1,129},{17,145},{129,1},{145,17... | collective-permute-start | bytes 147464 | tf_op jit(solution)/shard_map/ppermute | solution.py:29
  161.0 4.5 %collective-permute-start.21 = (bf16[3,16,512]{2,1,0:T(8,128)(2,1)S(1)}, bf16[3,16,512]{2,1,0:T(8,128)(2,1)S(1)}, u32[]{:S(2)}, u32[]{:S(2)}) collective-permute-start(bf16[3,16,512]{2,1,0:T(8,128)(2,1)S(1)} %add_convert_fusion.4), channel_id=1, source_target_pairs={{0,144},{16,0},{128,16},{144,128},{1,145},{17,1},{129,17},{145,129... | collective-permute-start | bytes 147464 | tf_op jit(solution)/shard_map/ppermute | solution.py:29
  165.5 5.8 %collective-permute-start.22 = (bf16[4,3,16,512]{3,2,1,0:T(8,128)(2,1)S(1)}, bf16[4,3,16,512]{3,2,1,0:T(8,128)(2,1)S(1)}, u32[]{:S(2)}, u32[]{:S(2)}) collective-permute-start(bf16[4,3,16,512]{3,2,1,0:T(8,128)(2,1)S(1)} %get-tuple-element.22), channel_id=1, source_target_pairs={{0,32},{32,64},{64,96},{96,0},{1,33},{33,65},{65,97},{97,1},{2,34}... | collective-permute-start | bytes 589832 | tf_op jit(solution)/shard_map/ppermute | solution.py:29
  166.6 8.0 %collective-permute-start.23 = (bf16[4,3,16,512]{3,2,1,0:T(8,128)(2,1)S(1)}, bf16[4,3,16,512]{3,2,1,0:T(8,128)(2,1)S(1)}, u32[]{:S(2)}, u32[]{:S(2)}) collective-permute-start(bf16[4,3,16,512]{3,2,1,0:T(8,128)(2,1)S(1)} %get-tuple-element.22), channel_id=1, source_target_pairs={{0,64},{32,96},{64,0},{96,32},{1,65},{33,97},{65,1},{97,33},{2,66}... | collective-permute-start | bytes 589832 | tf_op jit(solution)/shard_map/ppermute | solution.py:29
  168.7 6.1 %collective-permute-start.24 = (bf16[4,3,16,512]{3,2,1,0:T(8,128)(2,1)S(1)}, bf16[4,3,16,512]{3,2,1,0:T(8,128)(2,1)S(1)}, u32[]{:S(2)}, u32[]{:S(2)}) collective-permute-start(bf16[4,3,16,512]{3,2,1,0:T(8,128)(2,1)S(1)} %get-tuple-element.22), channel_id=1, source_target_pairs={{0,96},{32,0},{64,32},{96,64},{1,97},{33,1},{65,33},{97,65},{2,98}... | collective-permute-start | bytes 589832 | tf_op jit(solution)/shard_map/ppermute | solution.py:29
  174.8 6.2 %collective-permute-start.25 = (bf16[4,4,3,16,512]{4,3,2,1,0:T(8,128)(2,1)S(1)}, bf16[4,4,3,16,512]{4,3,2,1,0:T(8,128)(2,1)S(1)}, u32[]{:S(2)}, u32[]{:S(2)}) collective-permute-start(bf16[4,4,3,16,512]{4,3,2,1,0:T(8,128)(2,1)S(1)} %pad_maximum_fusion.own), channel_id=1, source_target_pairs={{0,1},{1,0},{2,3},{3,2},{4,5},{5,4},{6,7},{7,6},{8,9},{9,8},{10,11... | collective-permute-start | bytes 2359304 | tf_op jit(solution)/shard_map/ppermute | solution.py:29

commit v2 on v1

--- a/solution.py
+++ b/solution.py
@@ -12,7 +12,7 @@
 COL = (XLO, Z, CORE)
 X4 = (XHI, XLO)
 
-UNROLL = 4
+UNROLL = 8
 CAP = 32
 TILE = 128
 F32 = jnp.float32
@@ -21,6 +21,7 @@
 VMEM = pl.BlockSpec(memory_space=pltpu.VMEM)
 ANY = pl.BlockSpec(memory_space=pltpu.HBM)
 BUSY = pl.CostEstimate(flops=40 * 10**9, transcendentals=0, bytes_accessed=2**23)
+ROOMY = pltpu.CompilerParams(vmem_limit_bytes=26 * 2**20)
 SMALL = pltpu.CompilerParams(vmem_limit_bytes=8 * 2**20)
 
 
@@ -92,26 +93,51 @@
 
 
 def mix_kernel(
-    meta0, meta1, grad0, grad1, weights, tiles0, tiles1,
-    kept, sent, sums, picked, operands, mixed_acc, own_acc, held_tiles, arrived,
+    meta0, meta1, grad0, grad1, weights, tiles0, tiles1, kept, sent, picked, operands, acc, held_tiles, arrived
 ):
     core, x_lo = lax.axis_index(CORE), lax.axis_index(XLO)
     fetch = fetches(tiles0, tiles1, held_tiles, arrived)
     for r in range(weights.shape[0]):
         for a in range(2):
             fetch(a, r).start()
-    d_in = weights.shape[1]
-    mixed_acc[...] = jnp.zeros_like(mixed_acc)
+    acc[...] = jnp.zeros_like(acc)
+
+    def relation(r, carry):
+        for a, (meta, grad) in enumerate(((meta0, grad0), (meta1, grad1))):
+            mixed = jnp.dot(weights[r], grad[...], preferred_element_type=F32).astype(BF16)
+            for k in range(operands.shape[0]):
+                operands[k] = mixed[:, TILE * k : TILE * (k + 1)]
+            fetch(a, r).wait()
+
+            def group(entries, a=a):
+                products = [
+                    jnp.dot(operands[row], masked(held_tiles[a, r, s], keep), preferred_element_type=F32)
+                    for s, keep, row, col in entries
+                ]
+                for (s, keep, row, col), product in zip(entries, products):
+                    acc[((col >> 4) ^ x_lo) * 8 + ((col >> 1) & 7)] += product
+
+            columns(core, meta, r, picked, group)
+        return carry
+
+    lax.fori_loop(0, weights.shape[0], relation, 0)
+    kept[...] = acc[:8].astype(BF16)
+    sent[...] = acc[8:].astype(BF16)
+
+
+def own_kernel(meta0, meta1, grad0, grad1, tiles0, tiles1, sums, picked, operands, acc, held_tiles, arrived):
+    core = lax.axis_index(CORE)
+    fetch = fetches(tiles0, tiles1, held_tiles, arrived)
+    for r in range(tiles0.shape[0]):
+        for a in range(2):
+            fetch(a, r).start()
     for a, grad in enumerate((grad0, grad1)):
         for k in range(operands.shape[1]):
-            operands[a, k, d_in:] = grad[:, TILE * k : TILE * (k + 1)]
+            operands[a, k] = grad[:, TILE * k : TILE * (k + 1)]
 
     def relation(r, carry):
-        own_acc[...] = jnp.zeros_like(own_acc)
-        for a, (meta, grad) in enumerate(((meta0, grad0), (meta1, grad1))):
-            mixed = jnp.dot(weights[r], grad[...], preferred_element_type=F32).astype(BF16)
-            for k in range(operands.shape[1]):
-                operands[a, k, :d_in] = mixed[:, TILE * k : TILE * (k + 1)]
+        acc[...] = jnp.zeros_like(acc)
+        for a, meta in enumerate((meta0, meta1)):
             fetch(a, r).wait()
 
             def group(entries, a=a):
@@ -120,17 +146,14 @@
                     for s, keep, row, col in entries
                 ]
                 for (s, keep, row, col), product in zip(entries, products):
-                    mixed_acc[((col >> 4) ^ x_lo) * 8 + ((col >> 1) & 7)] += product[:d_in]
-                    own_acc[col >> 1] += product[d_in:]
+                    acc[col >> 1] += product
 
             columns(core, meta, r, picked, group)
-        for k in range(own_acc.shape[0]):
-            sums[r, :, TILE * k : TILE * (k + 1)] = own_acc[k].astype(BF16)
+        for k in range(acc.shape[0]):
+            sums[r, :, TILE * k : TILE * (k + 1)] = acc[k].astype(BF16)
         return carry
 
-    lax.fori_loop(0, weights.shape[0], relation, 0)
-    kept[...] = mixed_acc[:8].astype(BF16)
-    sent[...] = mixed_acc[8:].astype(BF16)
+    lax.fori_loop(0, tiles0.shape[0], relation, 0)
 
 
 def weight_kernel(inputs, sums, kept, sent, held):
@@ -206,27 +229,44 @@
     )(*grads).reshape(d_out, rows)
     grad_near = shifted(grad, CORE, 1)
 
-    mixed, mixed_sent, sums = pl.pallas_call(
+    tile_scratch = [
+        pltpu.VMEM((2, *tiles.shape), BF16),
+        pltpu.SemaphoreType.DMA((2, relations)),
+    ]
+    mixed, mixed_sent = pl.pallas_call(
         mix_kernel,
         out_shape=(
             jax.ShapeDtypeStruct((8, d_in, TILE), BF16),
             jax.ShapeDtypeStruct((8, d_in, TILE), BF16),
-            jax.ShapeDtypeStruct((relations, d_out, 16 * TILE), BF16),
         ),
         in_specs=[SMEM] * 2 + [VMEM] * 3 + [ANY] * 2,
-        out_specs=(VMEM,) * 3,
+        out_specs=(VMEM, VMEM),
         scratch_shapes=[
             pltpu.SMEM((CAP + UNROLL,), jnp.int32),
-            pltpu.VMEM((2, rows // TILE, d_in + d_out, TILE), BF16),
+            pltpu.VMEM((rows // TILE, d_in, TILE), BF16),
             pltpu.VMEM((16, d_in, TILE), F32),
-            pltpu.VMEM((16, d_out, TILE), F32),
-            pltpu.VMEM((2, *tiles.shape), BF16),
-            pltpu.SemaphoreType.DMA((2, relations)),
+            *tile_scratch,
         ],
-        compiler_params=pltpu.CompilerParams(vmem_limit_bytes=50 * 2**20),
+        compiler_params=ROOMY,
         cost_estimate=BUSY,
         name="mix",
     )(meta, meta_near, grad, grad_near, weights, tiles, tiles_near)
+    sums = pl.pallas_call(
+        own_kernel,
+        out_shape=jax.ShapeDtypeStruct((relations, d_out, 16 * TILE), BF16),
+        in_specs=[SMEM] * 2 + [VMEM] * 2 + [ANY] * 2,
+        out_specs=VMEM,
+        scratch_shapes=[
+            pltpu.SMEM((CAP + UNROLL,), jnp.int32),
+            pltpu.VMEM((2, rows // TILE, d_out, TILE), BF16),
+            pltpu.VMEM((16, d_out, TILE), F32),
+            *tile_scratch,
+        ],
+        compiler_params=ROOMY,
+        cost_estimate=BUSY,
+        name="own",
+    )(meta, meta_near, grad, grad_near, tiles, tiles_near)
+
     mixed_met = shifted(mixed_sent, XLO, 1)
 
     kept, sent = pl.pallas_call(

time: 184 us -> 200 us (1.087)
  waiting for transfers between devices: 91.8 us -> 112 us
  starting transfers between devices: 54.9 us -> 47.2 us
  local copies, waits for them, and re-layouts: 6.74 us -> 9.1 us
    ppermute x25, waiting for transfers between devices: 66.9 us -> 79.4 us  [shifted(): return lax.ppermute(value, axis, [(i, (i + step) % n) for i in range(n)])]
    ppermute x25, starting transfers between devices: 40.7 us -> 31 us  [shifted(): return lax.ppermute(value, axis, [(i, (i + step) % n) for i in range(n)])]
    pallas_call x0 -> x1, Pallas kernels: none -> 9.16 us  [body(): pl.pallas_call(own_kernel, out_shape=jax.ShapeDtypeStruct((relations, d_o...]
    pallas_call x1, Pallas kernels: 19.7 us -> 11.1 us  [body(): pl.pallas_call(mix_kernel, out_shape=(jax.ShapeDtypeStruct((8, d_in, TILE...]
    all_to_all x1, waiting for transfers between devices: 24.9 us -> 33 us  [gathered(): return lax.all_to_all(copies, axes, 0, 0)]
    unnamed x18, local copies, waits for them, and re-layouts: 5.01 us -> 7.37 us
where the time goes in v2:
time: 200 us
  waiting for transfers between devices  112 us (56%)
  starting transfers between devices  47.2 us (24%)
  Pallas kernels  27.7 us (14%)
  local copies, waits for them, and re-layouts  9.1 us (5%)
  other arithmetic  2.79 us (1%)
    ppermute x25, waiting for transfers between devices, shifted(): return lax.ppermute(value, axis, [(i, (i + step) % n) for i in range(n)])  79.4 us
    all_to_all x1, waiting for transfers between devices, gathered(): return lax.all_to_all(copies, axes, 0, 0)  33 us
    ppermute x25, starting transfers between devices, shifted(): return lax.ppermute(value, axis, [(i, (i + step) % n) for i in range(n)])  31 us
    pallas_call x1, Pallas kernels, body(): pl.pallas_call(mix_kernel, out_shape=(jax.ShapeDtypeStruct((8, d_in, TILE...  11.1 us
    all_to_all x1, starting transfers between devices, gathered(): return lax.all_to_all(copies, axes, 0, 0)  9.35 us
    pallas_call x1, Pallas kernels, body(): pl.pallas_call(own_kernel, out_shape=jax.ShapeDtypeStruct((relations, d_o...  9.16 us
    unnamed x18, local copies, waits for them, and re-layouts  7.37 us
    all_to_all x1, starting transfers between devices, body(): mixed = lax.all_to_all(mixed, Z, 0, 0)  5.66 us
  transfers between devices with their start and end apart: 28, of which 20 were waited for; matrix products, arithmetic and copies ran while one was open for 2% of the time, Pallas kernels for 12%

profile of v2, /device:TPU:1, one launch (start us, length us, event | category | flops | bytes accessed | tf_op | source)
XLA Modules:
  0.0 200.1 jit_solution(3256861100772489202)
XLA Ops:
  0.6 3.3 %collective-permute-start.6 = (bf16[3,32,128,128]{3,2,1,0:T(8,128)(2,1)}, bf16[3,32,128,128]{3,2,1,0:T(8,128)(2,1)}, u32[]{:S(2)}, u32[]{:S(2)}) collective-permute-start(bf16[3,32,128,128]{3,2,1,0:T(8,128)(2,1)} %bitcast.47), channel_id=1, source_target_pairs={{0,1},{1,0},{2,3},{3,2},{4,5},{5,4},{6,7},{7,6},{8,9},{9,8},{10,11... | collective-permute-start | bytes 9437192 | tf_op jit(solution)/shard_map/ppermute | solution.py:30
  3.9 1.0 collective-permute-start.1
  5.0 5.6 %collective-permute-done.1 = bf16[64,1024]{1,0:T(8,128)(2,1)S(1)} collective-permute-done((bf16[64,1024]{1,0:T(8,128)(2,1)}, bf16[64,1024]{1,0:T(8,128)(2,1)S(1)}, u32[]{:S(2)}, u32[]{:S(2)}) %collective-permute-start.1) | collective-permute-done | bytes 131104 | tf_op jit(solution)/shard_map/ppermute | solution.py:30
  10.6 0.9 pad_maximum_fusion.1.g0
  11.5 1.1 collective-permute-start.4
  13.0 0.7 collective-permute-start.2
  13.7 4.8 %collective-permute-done.4.g3 = bf16[2,64,1024]{2,1,0:T(8,128)(2,1)S(1)} collective-permute-done((bf16[2,64,1024]{2,1,0:T(8,128)(2,1)S(1)}, bf16[2,64,1024]{2,1,0:T(8,128)(2,1)S(1)}, u32[]{:S(2)}, u32[]{:S(2)}) %collective-permute-start.4) | collective-permute-done | bytes 262176 | tf_op jit(solution)/shard_map/ppermute | solution.py:30
  18.5 2.3 %collective-permute-done.3.g2 = bf16[2,64,1024]{2,1,0:T(8,128)(2,1)S(1)} collective-permute-done((bf16[2,64,1024]{2,1,0:T(8,128)(2,1)S(1)}, bf16[2,64,1024]{2,1,0:T(8,128)(2,1)S(1)}, u32[]{:S(2)}, u32[]{:S(2)}) %collective-permute-start.3) | collective-permute-done | bytes 262176 | tf_op jit(solution)/shard_map/ppermute | solution.py:30
  20.8 7.2 %collective-permute-done.2.g1 = bf16[2,64,1024]{2,1,0:T(8,128)(2,1)S(1)} collective-permute-done((bf16[2,64,1024]{2,1,0:T(8,128)(2,1)S(1)}, bf16[2,64,1024]{2,1,0:T(8,128)(2,1)S(1)}, u32[]{:S(2)}, u32[]{:S(2)}) %collective-permute-start.2) | collective-permute-done | bytes 262176 | tf_op jit(solution)/shard_map/ppermute | solution.py:30
  28.8 1.7 broadcast_in_dim.2
  30.5 9.3 %all-to-all-start = ((bf16[16,512,128]{2,1,0:T(8,128)(2,1)}), bf16[16,512,128]{2,1,0:T(8,128)(2,1)S(1)}, u32[]{:S(2)}, u32[]{:S(2)}) async-start(bf16[16,512,128]{2,1,0:T(8,128)(2,1)} %broadcast_in_dim.2), calls=%async_computation | async-start | bytes 4194304 | tf_op jit(solution)/shard_map/all_to_all | solution.py:35
  40.8 0.9 collective-permute-done.meta1
  41.7 1.9 copy-done.4
  43.6 9.2 %own.1.sums = bf16[3,512,2048]{2,1,0:T(8,128)(2,1)S(1)} custom-call(s32[3,128]{1,0:T(4,128)S(1)} %meta.1.meta0, s32[3,128]{1,0:T(4,128)S(1)} %collective-permute-done.meta1, bf16[512,1024]{1,0:T(8,128)(2,1)S(1)} %bitcast.44, bf16[512,1024]{1,0:T(8,128)(2,1)} %collective-permute-done.5.grad1, bf16[3,32,128,128]{3,2,1,0:T(8,128)(2,1)S(1)} %bitcast.48, ...), custom_call_target="tpu_custom_call" | custom-call | flops 40000000000 | bytes 8388608 | tf_op jit(solution)/shard_map/own/pallas_call | solution.py:254
  52.8 2.7 %copy-done.7 = bf16[3,512,2048]{2,1,0:T(8,128)(2,1)} copy-done((bf16[3,512,2048]{2,1,0:T(8,128)(2,1)}, bf16[3,512,2048]{2,1,0:T(8,128)(2,1)S(1)}, u32[]{:S(2)}) %copy-start.7) | copy-done | bytes 6291480
  55.4 33.0 %all-to-all-done.inputs = bf16[16,512,128]{2,1,0:T(8,128)(2,1)S(1)} async-done(((bf16[16,512,128]{2,1,0:T(8,128)(2,1)}), bf16[16,512,128]{2,1,0:T(8,128)(2,1)S(1)}, u32[]{:S(2)}, u32[]{:S(2)}) %all-to-all-start) | async-done | bytes 2097184 | tf_op jit(solution)/shard_map/all_to_all | solution.py:35
  88.4 2.8 %copy-done.8 = bf16[3,512,2048]{2,1,0:T(8,128)(2,1)S(1)} copy-done((bf16[3,512,2048]{2,1,0:T(8,128)(2,1)S(1)}, bf16[3,512,2048]{2,1,0:T(8,128)(2,1)}, u32[]{:S(2)}) %copy-start.8) | copy-done | bytes 6291480
  91.2 3.6 %weight_terms.1 = (f32[4,4,3,16,512]{4,3,2,1,0:T(8,128)S(1)}, bf16[4,4,3,16,512]{4,3,2,1,0:T(8,128)(2,1)S(1)}) custom-call(bf16[16,512,128]{2,1,0:T(8,128)(2,1)S(1)} %all-to-all-done.inputs, bf16[3,512,2048]{2,1,0:T(8,128)(2,1)S(1)} %copy-done.8), custom_call_target="tpu_custom_call" | custom-call | flops 40000000000 | bytes 8388608 | tf_op jit(solution)/shard_map/weight_terms/pallas_call | solution.py:272
  94.8 1.4 collective-permute-start.7
  96.2 11.1 %mix.1 = (bf16[8,512,128]{2,1,0:T(8,128)(2,1)S(1)}, bf16[8,512,128]{2,1,0:T(8,128)(2,1)S(1)}) custom-call(s32[3,128]{1,0:T(4,128)S(1)} %meta.1.meta0, s32[3,128]{1,0:T(4,128)S(1)} %collective-permute-done.meta1, bf16[512,1024]{1,0:T(8,128)(2,1)S(1)} %bitcast.45, bf16[512,1024]{1,0:T(8,128)(2,1)} %collective-permute-done.5.grad1, ...), custom_call_target="tpu_custom_call" | custom-call | flops 40000000000 | bytes 8388608 | tf_op jit(solution)/shard_map/mix/pallas_call | solution.py:236
  107.7 2.7 %collective-permute-start.10 = (bf16[4,3,16,512]{3,2,1,0:T(8,128)(2,1)S(1)}, bf16[4,3,16,512]{3,2,1,0:T(8,128)(2,1)S(1)}, u32[]{:S(2)}, u32[]{:S(2)}) collective-permute-start(bf16[4,3,16,512]{3,2,1,0:T(8,128)(2,1)S(1)} %get-tuple-element.17), channel_id=1, source_target_pairs={{0,96},{32,0},{64,32},{96,64},{1,97},{33,1},{65,33},{97,65},{2,98}... | collective-permute-start | bytes 589832 | tf_op jit(solution)/shard_map/ppermute | solution.py:30
  110.4 4.5 %collective-permute-done.8 = bf16[4,3,16,512]{3,2,1,0:T(8,128)(2,1)S(1)} collective-permute-done((bf16[4,3,16,512]{3,2,1,0:T(8,128)(2,1)S(1)}, bf16[4,3,16,512]{3,2,1,0:T(8,128)(2,1)S(1)}, u32[]{:S(2)}, u32[]{:S(2)}) %collective-permute-start.8) | collective-permute-done | bytes 196640 | tf_op jit(solution)/shard_map/ppermute | solution.py:30
  114.9 3.7 %collective-permute-done.9 = bf16[4,3,16,512]{3,2,1,0:T(8,128)(2,1)S(1)} collective-permute-done((bf16[4,3,16,512]{3,2,1,0:T(8,128)(2,1)S(1)}, bf16[4,3,16,512]{3,2,1,0:T(8,128)(2,1)S(1)}, u32[]{:S(2)}, u32[]{:S(2)}) %collective-permute-start.9) | collective-permute-done | bytes 196640 | tf_op jit(solution)/shard_map/ppermute | solution.py:30
  118.9 3.6 %collective-permute-start.13 = (bf16[3,16,512]{2,1,0:T(8,128)(2,1)S(1)}, bf16[3,16,512]{2,1,0:T(8,128)(2,1)S(1)}, u32[]{:S(2)}, u32[]{:S(2)}) collective-permute-start(bf16[3,16,512]{2,1,0:T(8,128)(2,1)S(1)} %get-tuple-element.22), channel_id=1, source_target_pairs={{0,144},{16,0},{128,16},{144,128},{1,145},{17,1},{129,17},{145,129... | collective-permute-start | bytes 147464 | tf_op jit(solution)/shard_map/ppermute | solution.py:30
  122.5 1.1 collective-permute-start.12
  123.6 7.2 %collective-permute-done.11 = bf16[3,16,512]{2,1,0:T(8,128)(2,1)S(1)} collective-permute-done((bf16[3,16,512]{2,1,0:T(8,128)(2,1)S(1)}, bf16[3,16,512]{2,1,0:T(8,128)(2,1)S(1)}, u32[]{:S(2)}, u32[]{:S(2)}) %collective-permute-start.11) | collective-permute-done | bytes 49184 | tf_op jit(solution)/shard_map/ppermute | solution.py:30
  130.7 1.9 collective-permute-done.13
  132.6 2.8 %collective-permute-done.12 = bf16[3,16,512]{2,1,0:T(8,128)(2,1)S(1)} collective-permute-done((bf16[3,16,512]{2,1,0:T(8,128)(2,1)S(1)}, bf16[3,16,512]{2,1,0:T(8,128)(2,1)S(1)}, u32[]{:S(2)}, u32[]{:S(2)}) %collective-permute-start.12) | collective-permute-done | bytes 49184 | tf_op jit(solution)/shard_map/ppermute | solution.py:30
  135.5 1.1 collective-permute-start.15
  136.6 1.3 add_convert_fusion
  137.9 5.7 %all-to-all-start.1 = ((bf16[8,512,128]{2,1,0:T(8,128)(2,1)}), bf16[8,512,128]{2,1,0:T(8,128)(2,1)S(1)}, u32[]{:S(2)}, u32[]{:S(2)}) async-start(bf16[8,512,128]{2,1,0:T(8,128)(2,1)} %add_convert_fusion), calls=%async_computation.1 | async-start | bytes 2097152 | tf_op jit(solution)/shard_map/all_to_all | solution.py:294
  143.6 3.6 %collective-permute-start.18 = (bf16[3,16,512]{2,1,0:T(8,128)(2,1)S(1)}, bf16[3,16,512]{2,1,0:T(8,128)(2,1)S(1)}, u32[]{:S(2)}, u32[]{:S(2)}) collective-permute-start(bf16[3,16,512]{2,1,0:T(8,128)(2,1)S(1)} %add_convert_fusion.5), channel_id=1, source_target_pairs={{0,12},{2,14},{4,0},{6,2},{8,4},{10,6},{12,8},{14,10},{1,13},{3,15... | collective-permute-start | bytes 147464 | tf_op jit(solution)/shard_map/ppermute | solution.py:30
  147.2 4.2 %collective-permute-start.16 = (bf16[3,16,512]{2,1,0:T(8,128)(2,1)S(1)}, bf16[3,16,512]{2,1,0:T(8,128)(2,1)S(1)}, u32[]{:S(2)}, u32[]{:S(2)}) collective-permute-start(bf16[3,16,512]{2,1,0:T(8,128)(2,1)S(1)} %add_convert_fusion.5), channel_id=1, source_target_pairs={{0,8},{2,10},{4,12},{6,14},{8,0},{10,2},{12,4},{14,6},{1,9},{3,11}... | collective-permute-start | bytes 147464 | tf_op jit(solution)/shard_map/ppermute | solution.py:30
  151.4 12.2 %collective-permute-done.18 = bf16[3,16,512]{2,1,0:T(8,128)(2,1)S(1)} collective-permute-done((bf16[3,16,512]{2,1,0:T(8,128)(2,1)S(1)}, bf16[3,16,512]{2,1,0:T(8,128)(2,1)S(1)}, u32[]{:S(2)}, u32[]{:S(2)}) %collective-permute-start.18) | collective-permute-done | bytes 49184 | tf_op jit(solution)/shard_map/ppermute | solution.py:30
  163.5 8.0 %collective-permute-done.17 = bf16[3,16,512]{2,1,0:T(8,128)(2,1)S(1)} collective-permute-done((bf16[3,16,512]{2,1,0:T(8,128)(2,1)S(1)}, bf16[3,16,512]{2,1,0:T(8,128)(2,1)S(1)}, u32[]{:S(2)}, u32[]{:S(2)}) %collective-permute-start.17) | collective-permute-done | bytes 49184 | tf_op jit(solution)/shard_map/ppermute | solution.py:30
  171.6 4.1 %collective-permute-done.16 = bf16[3,16,512]{2,1,0:T(8,128)(2,1)S(1)} collective-permute-done((bf16[3,16,512]{2,1,0:T(8,128)(2,1)S(1)}, bf16[3,16,512]{2,1,0:T(8,128)(2,1)S(1)}, u32[]{:S(2)}, u32[]{:S(2)}) %collective-permute-start.16) | collective-permute-done | bytes 49184 | tf_op jit(solution)/shard_map/ppermute | solution.py:30
  175.7 1.2 collective-permute-start.21
  177.6 1.1 collective-permute-done.21
  178.7 2.7 %collective-permute-done.20 = bf16[3,16,512]{2,1,0:T(8,128)(2,1)S(1)} collective-permute-done((bf16[3,16,512]{2,1,0:T(8,128)(2,1)S(1)}, bf16[3,16,512]{2,1,0:T(8,128)(2,1)S(1)}, u32[]{:S(2)}, u32[]{:S(2)}) %collective-permute-start.20) | collective-permute-done | bytes 49184 | tf_op jit(solution)/shard_map/ppermute | solution.py:30
  181.7 1.0 collective-permute-start.23
  182.7 1.2 collective-permute-start.22
  183.9 1.5 collective-permute-start.24
  185.3 2.6 %collective-permute-done.23 = bf16[4,3,16,512]{3,2,1,0:T(8,128)(2,1)S(1)} collective-permute-done((bf16[4,3,16,512]{3,2,1,0:T(8,128)(2,1)S(1)}, bf16[4,3,16,512]{3,2,1,0:T(8,128)(2,1)S(1)}, u32[]{:S(2)}, u32[]{:S(2)}) %collective-permute-start.23) | collective-permute-done | bytes 196640 | tf_op jit(solution)/shard_map/ppermute | solution.py:30
  187.9 5.7 %collective-permute-done.22 = bf16[4,3,16,512]{3,2,1,0:T(8,128)(2,1)S(1)} collective-permute-done((bf16[4,3,16,512]{3,2,1,0:T(8,128)(2,1)S(1)}, bf16[4,3,16,512]{3,2,1,0:T(8,128)(2,1)S(1)}, u32[]{:S(2)}, u32[]{:S(2)}) %collective-permute-start.22) | collective-permute-done | bytes 196640 | tf_op jit(solution)/shard_map/ppermute | solution.py:30
  193.7 1.3 collective-permute-start.25
  195.0 1.9 collective-permute-done.25.other
  196.9 2.3 %join.1 = f32[3,512,512]{2,1,0:T(8,128)} custom-call(bf16[4,4,3,16,512]{4,3,2,1,0:T(8,128)(2,1)S(1)} %pad_maximum_fusion.own, bf16[4,4,3,16,512]{4,3,2,1,0:T(8,128)(2,1)S(1)} %collective-permute-done.25.other), custom_call_target="tpu_custom_call" | custom-call | tf_op jit(solution)/shard_map/join/pallas_call | solution.py:309
  199.2 0.9 nodes.1
  (45 shorter events, 3.8 us)
Async XLA Ops:
  0.6 28.0 %copy-start = (bf16[128,512]{1,0:T(8,128)(2,1)S(1)}, bf16[128,512]{1,0:T(8,128)(2,1)}, u32[]{:S(2)}) copy-start(bf16[128,512]{1,0:T(8,128)(2,1)} %node_in.1) | copy-start | bytes 393220
  0.6 41.0 %collective-permute-start.6 = (bf16[3,32,128,128]{3,2,1,0:T(8,128)(2,1)}, bf16[3,32,128,128]{3,2,1,0:T(8,128)(2,1)}, u32[]{:S(2)}, u32[]{:S(2)}) collective-permute-start(bf16[3,32,128,128]{3,2,1,0:T(8,128)(2,1)} %bitcast.47), channel_id=1, source_target_pairs={{0,1},{1,0},{2,3},{3,2},{4,5},{5,4},{6,7},{7,6},{8,9},{9,8},{10,11... | collective-permute-start | bytes 9437192 | tf_op jit(solution)/shard_map/ppermute | solution.py:30
  3.9 6.7 %collective-permute-start.1 = (bf16[64,1024]{1,0:T(8,128)(2,1)}, bf16[64,1024]{1,0:T(8,128)(2,1)S(1)}, u32[]{:S(2)}, u32[]{:S(2)}) collective-permute-start(bf16[64,1024]{1,0:T(8,128)(2,1)} %bitcast.54), channel_id=1, source_target_pairs={{0,128},{128,0},{1,129},{129,1},{2,130},{130,2},{3,131},{131,3},{4... | collective-permute-start | bytes 393224 | tf_op jit(solution)/shard_map/ppermute | solution.py:30
  11.5 7.0 %collective-permute-start.4 = (bf16[2,64,1024]{2,1,0:T(8,128)(2,1)S(1)}, bf16[2,64,1024]{2,1,0:T(8,128)(2,1)S(1)}, u32[]{:S(2)}, u32[]{:S(2)}) collective-permute-start(bf16[2,64,1024]{2,1,0:T(8,128)(2,1)S(1)} %pad_maximum_fusion.1.g0), channel_id=1, source_target_pairs={{0,96},{32,0},{64,32},{96,64},{1,97},{33,1},{65,33},{97,65},{2,98}... | collective-permute-start | bytes 786440 | tf_op jit(solution)/shard_map/ppermute | solution.py:30
  12.6 8.2 %collective-permute-start.3 = (bf16[2,64,1024]{2,1,0:T(8,128)(2,1)S(1)}, bf16[2,64,1024]{2,1,0:T(8,128)(2,1)S(1)}, u32[]{:S(2)}, u32[]{:S(2)}) collective-permute-start(bf16[2,64,1024]{2,1,0:T(8,128)(2,1)S(1)} %pad_maximum_fusion.1.g0), channel_id=1, source_target_pairs={{0,64},{32,96},{64,0},{96,32},{1,65},{33,97},{65,1},{97,33},{2,66}... | collective-permute-start | bytes 786440 | tf_op jit(solution)/shard_map/ppermute | solution.py:30
  13.0 15.0 %collective-permute-start.2 = (bf16[2,64,1024]{2,1,0:T(8,128)(2,1)S(1)}, bf16[2,64,1024]{2,1,0:T(8,128)(2,1)S(1)}, u32[]{:S(2)}, u32[]{:S(2)}) collective-permute-start(bf16[2,64,1024]{2,1,0:T(8,128)(2,1)S(1)} %pad_maximum_fusion.1.g0), channel_id=1, source_target_pairs={{0,32},{32,64},{64,96},{96,0},{1,33},{33,65},{65,97},{97,1},{2,34}... | collective-permute-start | bytes 786440 | tf_op jit(solution)/shard_map/ppermute | solution.py:30
  28.1 13.6 %collective-permute-start.5 = (bf16[512,1024]{1,0:T(8,128)(2,1)S(1)}, bf16[512,1024]{1,0:T(8,128)(2,1)}, u32[]{:S(2)}, u32[]{:S(2)}) collective-permute-start(bf16[512,1024]{1,0:T(8,128)(2,1)S(1)} %bitcast.43), channel_id=1, source_target_pairs={{0,1},{1,0},{2,3},{3,2},{4,5},{5,4},{6,7},{7,6},{8,9},{9,8},{10,11... | collective-permute-start | bytes 3145736 | tf_op jit(solution)/shard_map/ppermute | solution.py:30
  30.5 9.4 %copy-start.1 = (s32[3,1,1,32]{3,2,1,0:T(1,128)S(1)}, s32[3,1,1,32]{3,2,1,0:T(1,128)}, u32[]{:S(2)}) copy-start(s32[3,1,1,32]{3,2,1,0:T(1,128)} %rows.1) | copy-start | bytes 1156
  30.5 9.4 %copy-start.2 = (s32[3,1,1,32]{3,2,1,0:T(1,128)S(1)}, s32[3,1,1,32]{3,2,1,0:T(1,128)}, u32[]{:S(2)}) copy-start(s32[3,1,1,32]{3,2,1,0:T(1,128)} %cols.1) | copy-start | bytes 1156
  30.5 9.4 %copy-start.3 = (s32[3,1,1]{0,2,1:T(1,128)S(1)}, s32[3,1,1]{0,2,1:T(1,128)}, u32[]{:S(2)}) copy-start(s32[3,1,1]{0,2,1:T(1,128)} %param.13) | copy-start | bytes 40
  30.5 57.9 %all-to-all-start = ((bf16[16,512,128]{2,1,0:T(8,128)(2,1)}), bf16[16,512,128]{2,1,0:T(8,128)(2,1)S(1)}, u32[]{:S(2)}, u32[]{:S(2)}) async-start(bf16[16,512,128]{2,1,0:T(8,128)(2,1)} %broadcast_in_dim.2), calls=%async_computation | async-start | bytes 4194304 | tf_op jit(solution)/shard_map/all_to_all | solution.py:35
  40.5 1.2 collective-permute-start
  41.7 1.9 copy-start.4
  52.8 2.7 %copy-start.7 = (bf16[3,512,2048]{2,1,0:T(8,128)(2,1)}, bf16[3,512,2048]{2,1,0:T(8,128)(2,1)S(1)}, u32[]{:S(2)}) copy-start(bf16[3,512,2048]{2,1,0:T(8,128)(2,1)S(1)} %own.1.sums) | copy-start | bytes 18874372
  88.4 2.8 %copy-start.8 = (bf16[3,512,2048]{2,1,0:T(8,128)(2,1)S(1)}, bf16[3,512,2048]{2,1,0:T(8,128)(2,1)}, u32[]{:S(2)}) copy-start(bf16[3,512,2048]{2,1,0:T(8,128)(2,1)} %copy-done.7) | copy-start | bytes 18874372
  91.2 5.0 %copy-start.5 = (bf16[3,1,1,32,128,128]{5,4,3,2,1,0:T(8,128)(2,1)S(1)}, bf16[3,1,1,32,128,128]{5,4,3,2,1,0:T(8,128)(2,1)}, u32[]{:S(2)}) copy-start(bf16[3,1,1,32,128,128]{5,4,3,2,1,0:T(8,128)(2,1)} %param.10) | copy-start | bytes 9437188
  91.2 5.0 %copy-start.6 = (bf16[3,512,512]{2,1,0:T(8,128)(2,1)S(1)}, bf16[3,512,512]{2,1,0:T(8,128)(2,1)}, u32[]{:S(2)}) copy-start(bf16[3,512,512]{2,1,0:T(8,128)(2,1)} %weights.1) | copy-start | bytes 4718596
  94.8 12.6 %collective-permute-start.7 = (bf16[4,4,3,16,512]{4,3,2,1,0:T(8,128)(2,1)S(1)}, bf16[4,4,3,16,512]{4,3,2,1,0:T(8,128)(2,1)S(1)}, u32[]{:S(2)}, u32[]{:S(2)}) collective-permute-start(bf16[4,4,3,16,512]{4,3,2,1,0:T(8,128)(2,1)S(1)} %get-tuple-element.10), channel_id=1, source_target_pairs={{0,1},{1,0},{2,3},{3,2},{4,5},{5,4},{6,7},{7,6},{8,9},{9,8},{10,11... | collective-permute-start | bytes 2359304 | tf_op jit(solution)/shard_map/ppermute | solution.py:30
  107.3 28.2 %collective-permute-start.14 = (bf16[8,512,128]{2,1,0:T(8,128)(2,1)S(1)}, bf16[8,512,128]{2,1,0:T(8,128)(2,1)S(1)}, u32[]{:S(2)}, u32[]{:S(2)}) collective-permute-start(bf16[8,512,128]{2,1,0:T(8,128)(2,1)S(1)} %get-tuple-element.11), channel_id=1, source_target_pairs={{0,16},{16,0},{1,17},{17,1},{2,18},{18,2},{3,19},{19,3},{4,20},{20... | collective-permute-start | bytes 3145736 | tf_op jit(solution)/shard_map/ppermute | solution.py:30
  107.6 7.2 %collective-permute-start.8 = (bf16[4,3,16,512]{3,2,1,0:T(8,128)(2,1)S(1)}, bf16[4,3,16,512]{3,2,1,0:T(8,128)(2,1)S(1)}, u32[]{:S(2)}, u32[]{:S(2)}) collective-permute-start(bf16[4,3,16,512]{3,2,1,0:T(8,128)(2,1)S(1)} %get-tuple-element.16), channel_id=1, source_target_pairs={{0,32},{32,64},{64,96},{96,0},{1,33},{33,65},{65,97},{97,1},{2,34}... | collective-permute-start | bytes 589832 | tf_op jit(solution)/shard_map/ppermute | solution.py:30
  107.7 7.2 %collective-permute-start.10 = (bf16[4,3,16,512]{3,2,1,0:T(8,128)(2,1)S(1)}, bf16[4,3,16,512]{3,2,1,0:T(8,128)(2,1)S(1)}, u32[]{:S(2)}, u32[]{:S(2)}) collective-permute-start(bf16[4,3,16,512]{3,2,1,0:T(8,128)(2,1)S(1)} %get-tuple-element.17), channel_id=1, source_target_pairs={{0,96},{32,0},{64,32},{96,64},{1,97},{33,1},{65,33},{97,65},{2,98}... | collective-permute-start | bytes 589832 | tf_op jit(solution)/shard_map/ppermute | solution.py:30
  110.4 8.2 %collective-permute-start.9 = (bf16[4,3,16,512]{3,2,1,0:T(8,128)(2,1)S(1)}, bf16[4,3,16,512]{3,2,1,0:T(8,128)(2,1)S(1)}, u32[]{:S(2)}, u32[]{:S(2)}) collective-permute-start(bf16[4,3,16,512]{3,2,1,0:T(8,128)(2,1)S(1)} %get-tuple-element.18), channel_id=1, source_target_pairs={{0,64},{32,96},{64,0},{96,32},{1,65},{33,97},{65,1},{97,33},{2,66}... | collective-permute-start | bytes 589832 | tf_op jit(solution)/shard_map/ppermute | solution.py:30
  118.8 12.0 %collective-permute-start.11 = (bf16[3,16,512]{2,1,0:T(8,128)(2,1)S(1)}, bf16[3,16,512]{2,1,0:T(8,128)(2,1)S(1)}, u32[]{:S(2)}, u32[]{:S(2)}) collective-permute-start(bf16[3,16,512]{2,1,0:T(8,128)(2,1)S(1)} %get-tuple-element.21), channel_id=1, source_target_pairs={{0,16},{16,128},{128,144},{144,0},{1,17},{17,129},{129,145},{145,1... | collective-permute-start | bytes 147464 | tf_op jit(solution)/shard_map/ppermute | solution.py:30
  118.9 13.8 %collective-permute-start.13 = (bf16[3,16,512]{2,1,0:T(8,128)(2,1)S(1)}, bf16[3,16,512]{2,1,0:T(8,128)(2,1)S(1)}, u32[]{:S(2)}, u32[]{:S(2)}) collective-permute-start(bf16[3,16,512]{2,1,0:T(8,128)(2,1)S(1)} %get-tuple-element.22), channel_id=1, source_target_pairs={{0,144},{16,0},{128,16},{144,128},{1,145},{17,1},{129,17},{145,129... | collective-permute-start | bytes 147464 | tf_op jit(solution)/shard_map/ppermute | solution.py:30
  122.5 13.0 %collective-permute-start.12 = (bf16[3,16,512]{2,1,0:T(8,128)(2,1)S(1)}, bf16[3,16,512]{2,1,0:T(8,128)(2,1)S(1)}, u32[]{:S(2)}, u32[]{:S(2)}) collective-permute-start(bf16[3,16,512]{2,1,0:T(8,128)(2,1)S(1)} %get-tuple-element.23), channel_id=1, source_target_pairs={{0,128},{16,144},{128,0},{144,16},{1,129},{17,145},{129,1},{145,17... | collective-permute-start | bytes 147464 | tf_op jit(solution)/shard_map/ppermute | solution.py:30
  135.5 8.1 %collective-permute-start.15 = (f32[3,16,512]{2,1,0:T(8,128)S(1)}, f32[3,16,512]{2,1,0:T(8,128)S(1)}, u32[]{:S(2)}, u32[]{:S(2)}) collective-permute-start(f32[3,16,512]{2,1,0:T(8,128)S(1)} %fusion.7), channel_id=1, source_target_pairs={{0,2},{2,0},{4,6},{6,4},{8,10},{10,8},{12,14},{14,12},{1,3},{3,1},... | collective-permute-start | bytes 294920 | tf_op jit(solution)/shard_map/ppermute | solution.py:39
  137.9 61.3 %all-to-all-start.1 = ((bf16[8,512,128]{2,1,0:T(8,128)(2,1)}), bf16[8,512,128]{2,1,0:T(8,128)(2,1)S(1)}, u32[]{:S(2)}, u32[]{:S(2)}) async-start(bf16[8,512,128]{2,1,0:T(8,128)(2,1)} %add_convert_fusion), calls=%async_computation.1 | async-start | bytes 2097152 | tf_op jit(solution)/shard_map/all_to_all | solution.py:294
  143.6 20.0 %collective-permute-start.18 = (bf16[3,16,512]{2,1,0:T(8,128)(2,1)S(1)}, bf16[3,16,512]{2,1,0:T(8,128)(2,1)S(1)}, u32[]{:S(2)}, u32[]{:S(2)}) collective-permute-start(bf16[3,16,512]{2,1,0:T(8,128)(2,1)S(1)} %add_convert_fusion.5), channel_id=1, source_target_pairs={{0,12},{2,14},{4,0},{6,2},{8,4},{10,6},{12,8},{14,10},{1,13},{3,15... | collective-permute-start | bytes 147464 | tf_op jit(solution)/shard_map/ppermute | solution.py:30
  147.2 24.3 %collective-permute-start.17 = (bf16[3,16,512]{2,1,0:T(8,128)(2,1)S(1)}, bf16[3,16,512]{2,1,0:T(8,128)(2,1)S(1)}, u32[]{:S(2)}, u32[]{:S(2)}) collective-permute-start(bf16[3,16,512]{2,1,0:T(8,128)(2,1)S(1)} %add_convert_fusion.5), channel_id=1, source_target_pairs={{0,4},{2,6},{4,8},{6,10},{8,12},{10,14},{12,0},{14,2},{1,5},{3,7},... | collective-permute-start | bytes 147464 | tf_op jit(solution)/shard_map/ppermute | solution.py:30
  147.2 28.5 %collective-permute-start.16 = (bf16[3,16,512]{2,1,0:T(8,128)(2,1)S(1)}, bf16[3,16,512]{2,1,0:T(8,128)(2,1)S(1)}, u32[]{:S(2)}, u32[]{:S(2)}) collective-permute-start(bf16[3,16,512]{2,1,0:T(8,128)(2,1)S(1)} %add_convert_fusion.5), channel_id=1, source_target_pairs={{0,8},{2,10},{4,12},{6,14},{8,0},{10,2},{12,4},{14,6},{1,9},{3,11}... | collective-permute-start | bytes 147464 | tf_op jit(solution)/shard_map/ppermute | solution.py:30
  175.7 3.0 %collective-permute-start.21 = (bf16[3,16,512]{2,1,0:T(8,128)(2,1)S(1)}, bf16[3,16,512]{2,1,0:T(8,128)(2,1)S(1)}, u32[]{:S(2)}, u32[]{:S(2)}) collective-permute-start(bf16[3,16,512]{2,1,0:T(8,128)(2,1)S(1)} %add_convert_fusion.4), channel_id=1, source_target_pairs={{0,144},{16,0},{128,16},{144,128},{1,145},{17,1},{129,17},{145,129... | collective-permute-start | bytes 147464 | tf_op jit(solution)/shard_map/ppermute | solution.py:30
  176.9 4.5 %collective-permute-start.20 = (bf16[3,16,512]{2,1,0:T(8,128)(2,1)S(1)}, bf16[3,16,512]{2,1,0:T(8,128)(2,1)S(1)}, u32[]{:S(2)}, u32[]{:S(2)}) collective-permute-start(bf16[3,16,512]{2,1,0:T(8,128)(2,1)S(1)} %add_convert_fusion.4), channel_id=1, source_target_pairs={{0,128},{16,144},{128,0},{144,16},{1,129},{17,145},{129,1},{145,17... | collective-permute-start | bytes 147464 | tf_op jit(solution)/shard_map/ppermute | solution.py:30
  176.9 4.7 %collective-permute-start.19 = (bf16[3,16,512]{2,1,0:T(8,128)(2,1)S(1)}, bf16[3,16,512]{2,1,0:T(8,128)(2,1)S(1)}, u32[]{:S(2)}, u32[]{:S(2)}) collective-permute-start(bf16[3,16,512]{2,1,0:T(8,128)(2,1)S(1)} %add_convert_fusion.4), channel_id=1, source_target_pairs={{0,16},{16,128},{128,144},{144,0},{1,17},{17,129},{129,145},{145,1... | collective-permute-start | bytes 147464 | tf_op jit(solution)/shard_map/ppermute | solution.py:30
  181.7 6.2 %collective-permute-start.23 = (bf16[4,3,16,512]{3,2,1,0:T(8,128)(2,1)S(1)}, bf16[4,3,16,512]{3,2,1,0:T(8,128)(2,1)S(1)}, u32[]{:S(2)}, u32[]{:S(2)}) collective-permute-start(bf16[4,3,16,512]{3,2,1,0:T(8,128)(2,1)S(1)} %get-tuple-element.20), channel_id=1, source_target_pairs={{0,64},{32,96},{64,0},{96,32},{1,65},{33,97},{65,1},{97,33},{2,66}... | collective-permute-start | bytes 589832 | tf_op jit(solution)/shard_map/ppermute | solution.py:30
  182.7 11.0 %collective-permute-start.22 = (bf16[4,3,16,512]{3,2,1,0:T(8,128)(2,1)S(1)}, bf16[4,3,16,512]{3,2,1,0:T(8,128)(2,1)S(1)}, u32[]{:S(2)}, u32[]{:S(2)}) collective-permute-start(bf16[4,3,16,512]{3,2,1,0:T(8,128)(2,1)S(1)} %get-tuple-element.20), channel_id=1, source_target_pairs={{0,32},{32,64},{64,96},{96,0},{1,33},{33,65},{65,97},{97,1},{2,34}... | collective-permute-start | bytes 589832 | tf_op jit(solution)/shard_map/ppermute | solution.py:30
  183.9 9.8 %collective-permute-start.24 = (bf16[4,3,16,512]{3,2,1,0:T(8,128)(2,1)S(1)}, bf16[4,3,16,512]{3,2,1,0:T(8,128)(2,1)S(1)}, u32[]{:S(2)}, u32[]{:S(2)}) collective-permute-start(bf16[4,3,16,512]{3,2,1,0:T(8,128)(2,1)S(1)} %get-tuple-element.20), channel_id=1, source_target_pairs={{0,96},{32,0},{64,32},{96,64},{1,97},{33,1},{65,33},{97,65},{2,98}... | collective-permute-start | bytes 589832 | tf_op jit(solution)/shard_map/ppermute | solution.py:30
  193.7 3.2 %collective-permute-start.25 = (bf16[4,4,3,16,512]{4,3,2,1,0:T(8,128)(2,1)S(1)}, bf16[4,4,3,16,512]{4,3,2,1,0:T(8,128)(2,1)S(1)}, u32[]{:S(2)}, u32[]{:S(2)}) collective-permute-start(bf16[4,4,3,16,512]{4,3,2,1,0:T(8,128)(2,1)S(1)} %pad_maximum_fusion.own), channel_id=1, source_target_pairs={{0,1},{1,0},{2,3},{3,2},{4,5},{5,4},{6,7},{7,6},{8,9},{9,8},{10,11... | collective-permute-start | bytes 2359304 | tf_op jit(solution)/shard_map/ppermute | solution.py:30

commit v3 on v2

--- a/solution.py
+++ b/solution.py
@@ -11,6 +11,7 @@
 ROW = (XHI, Y)
 COL = (XLO, Z, CORE)
 X4 = (XHI, XLO)
+
 
 UNROLL = 8
 CAP = 32
@@ -30,11 +31,6 @@
     return lax.ppermute(value, axis, [(i, (i + step) % n) for i in range(n)])
 
 
-def gathered(value, axes):
-    copies = jnp.broadcast_to(value[None], (lax.axis_size(axes), *value.shape))
-    return lax.all_to_all(copies, axes, 0, 0)
-
-
 def swapped(value, axis, step):
     return lax.ppermute(value, axis, [(i, i ^ step) for i in range(lax.axis_size(axis))])
 
@@ -156,11 +152,15 @@
     lax.fori_loop(0, tiles0.shape[0], relation, 0)
 
 
-def weight_kernel(inputs, sums, kept, sent, held):
-    core, x_hi, y, x_lo = [lax.axis_index(a) for a in (CORE, XHI, Y, XLO)]
+def weight_kernel(*refs):
+    parts, (sums, kept, sent, inputs, held) = refs[:8], refs[8:]
+    core, x_hi, y, x_lo, z = [lax.axis_index(a) for a in (CORE, XHI, Y, XLO, Z)]
+    for k, part in enumerate(parts):
+        inputs[2 * k] = part[0]
+        inputs[2 * k + 1] = part[1]
     x = x_hi * 2 + x_lo
     for k in range(inputs.shape[0]):
-        held[:, TILE * k : TILE * (k + 1)] = inputs[k]
+        held[:, TILE * k : TILE * (k + 1)] = inputs[((z - (k & 7)) & 7) * 2 + ((k >> 3) ^ x_lo)]
     for r in range(sums.shape[0]):
         terms = lax.dot_general(held[...], sums[r], (((1,), (1,)), ((), ())), preferred_element_type=F32)
         half = terms.shape[0] // 2
@@ -215,7 +215,11 @@
     packed = out_grad.T
     pair = jnp.stack([packed, shifted(packed, XHI, 1)])
     grads = [pair] + [shifted(pair, Y, k) for k in (1, 2, 3)]
-    inputs = gathered(turned, (XLO, Z))
+    near = jnp.stack([turned, shifted(turned, XLO, 1)])
+    parts = {0: near}
+    for k in (3, -3, 2, -2, 1, -1):
+        parts[k % 8] = shifted(near, Z, k)
+    parts[4] = shifted(parts[3], Z, 1)
     tiles_near = shifted(tiles, CORE, 1)
     meta_near = shifted(meta, CORE, 1)
 
@@ -275,13 +279,13 @@
             jax.ShapeDtypeStruct((4, 4, relations, 16, d_out), F32),
             jax.ShapeDtypeStruct((4, 4, relations, 16, d_out), BF16),
         ),
-        in_specs=[VMEM] * 2,
+        in_specs=[VMEM] * 9,
         out_specs=(VMEM, VMEM),
-        scratch_shapes=[pltpu.VMEM((d_in, 16 * TILE), BF16)],
+        scratch_shapes=[pltpu.VMEM((16, d_in, TILE), BF16), pltpu.VMEM((d_in, 16 * TILE), BF16)],
         compiler_params=pltpu.CompilerParams(vmem_limit_bytes=20 * 2**20),
         cost_estimate=BUSY,
         name="weight_terms",
-    )(inputs, sums)
+    )(*[parts[k] for k in range(8)], sums)
 
     met = shifted(sent, CORE, 1)
     on_y = [added(kept[k], met[k]) for k in range(4)]

time: 200 us -> 192 us (0.960)
  local copies, waits for them, and re-layouts: 9.1 us -> 0.04 us
  starting transfers between devices: 47.2 us -> 50.7 us
    all_to_all x1 -> x0, waiting for transfers between devices: 33 us -> none  [gathered(): return lax.all_to_all(copies, axes, 0, 0)]
    ppermute x25 -> x33, waiting for transfers between devices: 79.4 us -> 111 us  [shifted(): return lax.ppermute(value, axis, [(i, (i + step) % n) for i in range(n)])]
    ppermute x25 -> x33, starting transfers between devices: 31 us -> 44.1 us  [shifted(): return lax.ppermute(value, axis, [(i, (i + step) % n) for i in range(n)])]
    all_to_all x1 -> x0, starting transfers between devices: 9.35 us -> none  [gathered(): return lax.all_to_all(copies, axes, 0, 0)]
    unnamed x18 -> x12, local copies, waits for them, and re-layouts: 7.37 us -> 0.03 us
  transfers between devices with their start and end apart: 28 -> 35, of which waited for: 20 -> 25; matrix products, arithmetic and copies ran while one was open for 2% -> 1% of each run, Pallas kernels for 12% -> 12%
where the time goes in v3:
time: 192 us
  waiting for transfers between devices  111 us (58%)
  starting transfers between devices  50.7 us (26%)
  Pallas kernels  26.9 us (14%)
  other arithmetic  2.8 us (1%)
    ppermute x33, waiting for transfers between devices, shifted(): return lax.ppermute(value, axis, [(i, (i + step) % n) for i in range(n)])  111 us
    ppermute x33, starting transfers between devices, shifted(): return lax.ppermute(value, axis, [(i, (i + step) % n) for i in range(n)])  44.1 us
    pallas_call x1, Pallas kernels, body(): pl.pallas_call(mix_kernel, out_shape=(jax.ShapeDtypeStruct((8, d_in, TILE...  10.6 us
    pallas_call x1, Pallas kernels, body(): pl.pallas_call(own_kernel, out_shape=jax.ShapeDtypeStruct((relations, d_o...  8.73 us
    all_to_all x1, starting transfers between devices, body(): mixed = lax.all_to_all(mixed, Z, 0, 0)  4.97 us
  transfers between devices with their start and end apart: 35, of which 25 were waited for; matrix products, arithmetic and copies ran while one was open for 1% of the time, Pallas kernels for 12%

profile of v3, /device:TPU:1, one launch (start us, length us, event | category | flops | bytes accessed | tf_op | source)
XLA Modules:
  0.0 192.3 jit_solution(15006201970594832247)
XLA Ops:
  0.7 3.3 %collective-permute-start.6 = (bf16[3,32,128,128]{3,2,1,0:T(8,128)(2,1)}, bf16[3,32,128,128]{3,2,1,0:T(8,128)(2,1)S(1)}, u32[]{:S(2)}, u32[]{:S(2)}) collective-permute-start(bf16[3,32,128,128]{3,2,1,0:T(8,128)(2,1)} %bitcast.50), channel_id=1, source_target_pairs={{0,1},{1,0},{2,3},{3,2},{4,5},{5,4},{6,7},{7,6},{8,9},{9,8},{10,11... | collective-permute-start | bytes 9437192 | tf_op jit(solution)/shard_map/ppermute | solution.py:31
  4.0 1.0 collective-permute-start.1
  5.0 5.6 %collective-permute-done.1 = bf16[64,1024]{1,0:T(8,128)(2,1)S(1)} collective-permute-done((bf16[64,1024]{1,0:T(8,128)(2,1)}, bf16[64,1024]{1,0:T(8,128)(2,1)S(1)}, u32[]{:S(2)}, u32[]{:S(2)}) %collective-permute-start.1) | collective-permute-done | bytes 131104 | tf_op jit(solution)/shard_map/ppermute | solution.py:31
  10.6 0.9 pad_maximum_fusion.1.g0
  11.6 1.1 collective-permute-start.4
  13.7 4.8 %collective-permute-done.4.g3 = bf16[2,64,1024]{2,1,0:T(8,128)(2,1)S(1)} collective-permute-done((bf16[2,64,1024]{2,1,0:T(8,128)(2,1)S(1)}, bf16[2,64,1024]{2,1,0:T(8,128)(2,1)S(1)}, u32[]{:S(2)}, u32[]{:S(2)}) %collective-permute-start.4) | collective-permute-done | bytes 262176 | tf_op jit(solution)/shard_map/ppermute | solution.py:31
  18.6 2.3 %collective-permute-done.3.g2 = bf16[2,64,1024]{2,1,0:T(8,128)(2,1)S(1)} collective-permute-done((bf16[2,64,1024]{2,1,0:T(8,128)(2,1)S(1)}, bf16[2,64,1024]{2,1,0:T(8,128)(2,1)S(1)}, u32[]{:S(2)}, u32[]{:S(2)}) %collective-permute-start.3) | collective-permute-done | bytes 262176 | tf_op jit(solution)/shard_map/ppermute | solution.py:31
  20.9 7.2 %collective-permute-done.2.g1 = bf16[2,64,1024]{2,1,0:T(8,128)(2,1)S(1)} collective-permute-done((bf16[2,64,1024]{2,1,0:T(8,128)(2,1)S(1)}, bf16[2,64,1024]{2,1,0:T(8,128)(2,1)S(1)}, u32[]{:S(2)}, u32[]{:S(2)}) %collective-permute-start.2) | collective-permute-done | bytes 262176 | tf_op jit(solution)/shard_map/ppermute | solution.py:31
  28.8 1.3 collective-permute-start.7
  30.1 3.8 %collective-permute-done.7 = bf16[512,128]{1,0:T(8,128)(2,1)S(1)} collective-permute-done((bf16[512,128]{1,0:T(8,128)(2,1)S(1)}, bf16[512,128]{1,0:T(8,128)(2,1)S(1)}, u32[]{:S(2)}, u32[]{:S(2)}) %collective-permute-start.7) | collective-permute-done | bytes 131104 | tf_op jit(solution)/shard_map/ppermute | solution.py:31
  34.0 5.7 %collective-permute-start.14 = (bf16[2,512,128]{2,1,0:T(8,128)(2,1)S(1)}, bf16[2,512,128]{2,1,0:T(8,128)(2,1)S(1)}, u32[]{:S(2)}, u32[]{:S(2)}) collective-permute-start(bf16[2,512,128]{2,1,0:T(8,128)(2,1)S(1)} %pad_maximum_fusion.2.refs_0_), channel_id=1, source_target_pairs={{0,14},{2,0},{4,2},{6,4},{8,6},{10,8},{12,10},{14,12},{1,15},{3,1}... | collective-permute-start | bytes 786440 | tf_op jit(solution)/shard_map/ppermute | solution.py:31
  40.2 1.2 collective-permute-start
  42.2 1.2 collective-permute-start.13
  43.4 1.0 collective-permute-done.14.refs_7_
  44.4 3.8 %collective-permute-start.12 = (bf16[2,512,128]{2,1,0:T(8,128)(2,1)S(1)}, bf16[2,512,128]{2,1,0:T(8,128)(2,1)S(1)}, u32[]{:S(2)}, u32[]{:S(2)}) collective-permute-start(bf16[2,512,128]{2,1,0:T(8,128)(2,1)S(1)} %pad_maximum_fusion.2.refs_0_), channel_id=1, source_target_pairs={{0,10},{2,12},{4,14},{6,0},{8,2},{10,4},{12,6},{14,8},{1,11},{3,13... | collective-permute-start | bytes 786440 | tf_op jit(solution)/shard_map/ppermute | solution.py:31
  48.2 12.7 %collective-permute-done.10.refs_3_ = bf16[2,512,128]{2,1,0:T(8,128)(2,1)S(1)} collective-permute-done((bf16[2,512,128]{2,1,0:T(8,128)(2,1)S(1)}, bf16[2,512,128]{2,1,0:T(8,128)(2,1)S(1)}, u32[]{:S(2)}, u32[]{:S(2)}) %collective-permute-start.10) | collective-permute-done | bytes 262176 | tf_op jit(solution)/shard_map/ppermute | solution.py:31
  60.9 1.2 collective-permute-start.11
  62.1 8.7 %own.1.refs_8_ = bf16[3,512,2048]{2,1,0:T(8,128)(2,1)S(1)} custom-call(s32[3,128]{1,0:T(4,128)S(1)} %meta.1.meta0, s32[3,128]{1,0:T(4,128)S(1)} %collective-permute-done.meta1, bf16[512,1024]{1,0:T(8,128)(2,1)S(1)} %bitcast.46, bf16[512,1024]{1,0:T(8,128)(2,1)S(1)} %collective-permute-done.5.grad1, bf16[3,32,128,128]{3,2,1,0:T(8,128)(2,1)S(1)} %bitcast.51, ...), custom_call_target="tpu_custom_call" | custom-call | flops 40000000000 | bytes 8388608 | tf_op jit(solution)/shard_map/own/pallas_call | solution.py:258
  70.9 1.8 collective-permute-done.9.refs_2_
  72.7 4.0 %collective-permute-done.8.refs_1_ = bf16[2,512,128]{2,1,0:T(8,128)(2,1)S(1)} collective-permute-done((bf16[2,512,128]{2,1,0:T(8,128)(2,1)S(1)}, bf16[2,512,128]{2,1,0:T(8,128)(2,1)S(1)}, u32[]{:S(2)}, u32[]{:S(2)}) %collective-permute-start.8) | collective-permute-done | bytes 262176 | tf_op jit(solution)/shard_map/ppermute | solution.py:31
  76.7 5.6 %collective-permute-done.11.refs_4_ = bf16[2,512,128]{2,1,0:T(8,128)(2,1)S(1)} collective-permute-done((bf16[2,512,128]{2,1,0:T(8,128)(2,1)S(1)}, bf16[2,512,128]{2,1,0:T(8,128)(2,1)S(1)}, u32[]{:S(2)}, u32[]{:S(2)}) %collective-permute-start.11) | collective-permute-done | bytes 262176 | tf_op jit(solution)/shard_map/ppermute | solution.py:31
  82.4 3.6 %weight_terms.1 = (f32[4,4,3,16,512]{4,3,2,1,0:T(8,128)S(1)}, bf16[4,4,3,16,512]{4,3,2,1,0:T(8,128)(2,1)S(1)}) custom-call(bf16[2,512,128]{2,1,0:T(8,128)(2,1)S(1)} %pad_maximum_fusion.2.refs_0_, bf16[2,512,128]{2,1,0:T(8,128)(2,1)S(1)} %collective-permute-done.8.refs_1_, bf16[2,512,128]{2,1,0:T(8,128)(2,1)S(1)} %collective-permute-done.9.refs_2_, ...), custom_call_target="tpu_custom_call" | custom-call | flops 40000000000 | bytes 8388608 | tf_op jit(solution)/shard_map/weight_terms/pallas_call | solution.py:276
  86.0 1.6 collective-permute-start.15
  87.6 10.6 %mix.1 = (bf16[8,512,128]{2,1,0:T(8,128)(2,1)S(1)}, bf16[8,512,128]{2,1,0:T(8,128)(2,1)S(1)}) custom-call(s32[3,128]{1,0:T(4,128)S(1)} %meta.1.meta0, s32[3,128]{1,0:T(4,128)S(1)} %collective-permute-done.meta1, bf16[512,1024]{1,0:T(8,128)(2,1)S(1)} %bitcast.47, bf16[512,1024]{1,0:T(8,128)(2,1)S(1)} %collective-permute-done.5.grad1, ...), custom_call_target="tpu_custom_call" | custom-call | flops 40000000000 | bytes 8388608 | tf_op jit(solution)/shard_map/mix/pallas_call | solution.py:240
  98.6 2.7 %collective-permute-start.18 = (bf16[4,3,16,512]{3,2,1,0:T(8,128)(2,1)S(1)}, bf16[4,3,16,512]{3,2,1,0:T(8,128)(2,1)S(1)}, u32[]{:S(2)}, u32[]{:S(2)}) collective-permute-start(bf16[4,3,16,512]{3,2,1,0:T(8,128)(2,1)S(1)} %get-tuple-element.17), channel_id=1, source_target_pairs={{0,96},{32,0},{64,32},{96,64},{1,97},{33,1},{65,33},{97,65},{2,98}... | collective-permute-start | bytes 589832 | tf_op jit(solution)/shard_map/ppermute | solution.py:31
  101.3 4.5 %collective-permute-done.16 = bf16[4,3,16,512]{3,2,1,0:T(8,128)(2,1)S(1)} collective-permute-done((bf16[4,3,16,512]{3,2,1,0:T(8,128)(2,1)S(1)}, bf16[4,3,16,512]{3,2,1,0:T(8,128)(2,1)S(1)}, u32[]{:S(2)}, u32[]{:S(2)}) %collective-permute-start.16) | collective-permute-done | bytes 196640 | tf_op jit(solution)/shard_map/ppermute | solution.py:31
  105.7 4.4 %collective-permute-done.17 = bf16[4,3,16,512]{3,2,1,0:T(8,128)(2,1)S(1)} collective-permute-done((bf16[4,3,16,512]{3,2,1,0:T(8,128)(2,1)S(1)}, bf16[4,3,16,512]{3,2,1,0:T(8,128)(2,1)S(1)}, u32[]{:S(2)}, u32[]{:S(2)}) %collective-permute-start.17) | collective-permute-done | bytes 196640 | tf_op jit(solution)/shard_map/ppermute | solution.py:31
  110.4 3.4 %collective-permute-start.21 = (bf16[3,16,512]{2,1,0:T(8,128)(2,1)S(1)}, bf16[3,16,512]{2,1,0:T(8,128)(2,1)S(1)}, u32[]{:S(2)}, u32[]{:S(2)}) collective-permute-start(bf16[3,16,512]{2,1,0:T(8,128)(2,1)S(1)} %get-tuple-element.22), channel_id=1, source_target_pairs={{0,144},{16,0},{128,16},{144,128},{1,145},{17,1},{129,17},{145,129... | collective-permute-start | bytes 147464 | tf_op jit(solution)/shard_map/ppermute | solution.py:31
  114.7 6.9 %collective-permute-done.19 = bf16[3,16,512]{2,1,0:T(8,128)(2,1)S(1)} collective-permute-done((bf16[3,16,512]{2,1,0:T(8,128)(2,1)S(1)}, bf16[3,16,512]{2,1,0:T(8,128)(2,1)S(1)}, u32[]{:S(2)}, u32[]{:S(2)}) %collective-permute-start.19) | collective-permute-done | bytes 49184 | tf_op jit(solution)/shard_map/ppermute | solution.py:31
  121.6 2.0 %collective-permute-done.21 = bf16[3,16,512]{2,1,0:T(8,128)(2,1)S(1)} collective-permute-done((bf16[3,16,512]{2,1,0:T(8,128)(2,1)S(1)}, bf16[3,16,512]{2,1,0:T(8,128)(2,1)S(1)}, u32[]{:S(2)}, u32[]{:S(2)}) %collective-permute-start.21) | collective-permute-done | bytes 49184 | tf_op jit(solution)/shard_map/ppermute | solution.py:31
  123.5 3.1 %collective-permute-done.20 = bf16[3,16,512]{2,1,0:T(8,128)(2,1)S(1)} collective-permute-done((bf16[3,16,512]{2,1,0:T(8,128)(2,1)S(1)}, bf16[3,16,512]{2,1,0:T(8,128)(2,1)S(1)}, u32[]{:S(2)}, u32[]{:S(2)}) %collective-permute-start.20) | collective-permute-done | bytes 49184 | tf_op jit(solution)/shard_map/ppermute | solution.py:31
  126.7 1.6 collective-permute-start.23
  128.3 1.3 add_convert_fusion
  129.6 5.0 %all-to-all-start = ((bf16[8,512,128]{2,1,0:T(8,128)(2,1)}), bf16[8,512,128]{2,1,0:T(8,128)(2,1)S(1)}, u32[]{:S(2)}, u32[]{:S(2)}) async-start(bf16[8,512,128]{2,1,0:T(8,128)(2,1)} %add_convert_fusion), calls=%async_computation | async-start | bytes 2097152 | tf_op jit(solution)/shard_map/all_to_all | solution.py:298
  134.6 3.6 %collective-permute-start.26 = (bf16[3,16,512]{2,1,0:T(8,128)(2,1)S(1)}, bf16[3,16,512]{2,1,0:T(8,128)(2,1)S(1)}, u32[]{:S(2)}, u32[]{:S(2)}) collective-permute-start(bf16[3,16,512]{2,1,0:T(8,128)(2,1)S(1)} %add_convert_fusion.5), channel_id=1, source_target_pairs={{0,12},{2,14},{4,0},{6,2},{8,4},{10,6},{12,8},{14,10},{1,13},{3,15... | collective-permute-start | bytes 147464 | tf_op jit(solution)/shard_map/ppermute | solution.py:31
  138.3 4.2 %collective-permute-start.24 = (bf16[3,16,512]{2,1,0:T(8,128)(2,1)S(1)}, bf16[3,16,512]{2,1,0:T(8,128)(2,1)S(1)}, u32[]{:S(2)}, u32[]{:S(2)}) collective-permute-start(bf16[3,16,512]{2,1,0:T(8,128)(2,1)S(1)} %add_convert_fusion.5), channel_id=1, source_target_pairs={{0,8},{2,10},{4,12},{6,14},{8,0},{10,2},{12,4},{14,6},{1,9},{3,11}... | collective-permute-start | bytes 147464 | tf_op jit(solution)/shard_map/ppermute | solution.py:31
  142.4 12.2 %collective-permute-done.26 = bf16[3,16,512]{2,1,0:T(8,128)(2,1)S(1)} collective-permute-done((bf16[3,16,512]{2,1,0:T(8,128)(2,1)S(1)}, bf16[3,16,512]{2,1,0:T(8,128)(2,1)S(1)}, u32[]{:S(2)}, u32[]{:S(2)}) %collective-permute-start.26) | collective-permute-done | bytes 49184 | tf_op jit(solution)/shard_map/ppermute | solution.py:31
  154.6 8.0 %collective-permute-done.25 = bf16[3,16,512]{2,1,0:T(8,128)(2,1)S(1)} collective-permute-done((bf16[3,16,512]{2,1,0:T(8,128)(2,1)S(1)}, bf16[3,16,512]{2,1,0:T(8,128)(2,1)S(1)}, u32[]{:S(2)}, u32[]{:S(2)}) %collective-permute-start.25) | collective-permute-done | bytes 49184 | tf_op jit(solution)/shard_map/ppermute | solution.py:31
  162.6 4.1 %collective-permute-done.24 = bf16[3,16,512]{2,1,0:T(8,128)(2,1)S(1)} collective-permute-done((bf16[3,16,512]{2,1,0:T(8,128)(2,1)S(1)}, bf16[3,16,512]{2,1,0:T(8,128)(2,1)S(1)}, u32[]{:S(2)}, u32[]{:S(2)}) %collective-permute-start.24) | collective-permute-done | bytes 49184 | tf_op jit(solution)/shard_map/ppermute | solution.py:31
  167.5 1.8 collective-permute-start.28
  169.8 2.2 %collective-permute-done.28 = bf16[3,16,512]{2,1,0:T(8,128)(2,1)S(1)} collective-permute-done((bf16[3,16,512]{2,1,0:T(8,128)(2,1)S(1)}, bf16[3,16,512]{2,1,0:T(8,128)(2,1)S(1)}, u32[]{:S(2)}, u32[]{:S(2)}) %collective-permute-start.28) | collective-permute-done | bytes 49184 | tf_op jit(solution)/shard_map/ppermute | solution.py:31
  172.0 2.1 %collective-permute-done.27 = bf16[3,16,512]{2,1,0:T(8,128)(2,1)S(1)} collective-permute-done((bf16[3,16,512]{2,1,0:T(8,128)(2,1)S(1)}, bf16[3,16,512]{2,1,0:T(8,128)(2,1)S(1)}, u32[]{:S(2)}, u32[]{:S(2)}) %collective-permute-start.27) | collective-permute-done | bytes 49184 | tf_op jit(solution)/shard_map/ppermute | solution.py:31
  174.2 1.8 collective-permute-start.30
  176.0 1.0 collective-permute-start.32
  177.0 3.6 %collective-permute-done.31 = bf16[4,3,16,512]{3,2,1,0:T(8,128)(2,1)S(1)} collective-permute-done((bf16[4,3,16,512]{3,2,1,0:T(8,128)(2,1)S(1)}, bf16[4,3,16,512]{3,2,1,0:T(8,128)(2,1)S(1)}, u32[]{:S(2)}, u32[]{:S(2)}) %collective-permute-start.31) | collective-permute-done | bytes 196640 | tf_op jit(solution)/shard_map/ppermute | solution.py:31
  180.6 5.7 %collective-permute-done.30 = bf16[4,3,16,512]{3,2,1,0:T(8,128)(2,1)S(1)} collective-permute-done((bf16[4,3,16,512]{3,2,1,0:T(8,128)(2,1)S(1)}, bf16[4,3,16,512]{3,2,1,0:T(8,128)(2,1)S(1)}, u32[]{:S(2)}, u32[]{:S(2)}) %collective-permute-start.30) | collective-permute-done | bytes 196640 | tf_op jit(solution)/shard_map/ppermute | solution.py:31
  187.2 1.9 collective-permute-done.33.other
  189.1 2.3 %join.1 = f32[3,512,512]{2,1,0:T(8,128)} custom-call(bf16[4,4,3,16,512]{4,3,2,1,0:T(8,128)(2,1)S(1)} %pad_maximum_fusion.own, bf16[4,4,3,16,512]{4,3,2,1,0:T(8,128)(2,1)S(1)} %collective-permute-done.33.other), custom_call_target="tpu_custom_call" | custom-call | tf_op jit(solution)/shard_map/join/pallas_call | solution.py:313
  (53 shorter events, 8.0 us)
Async XLA Ops:
  0.6 28.1 %copy-start = (bf16[128,512]{1,0:T(8,128)(2,1)S(1)}, bf16[128,512]{1,0:T(8,128)(2,1)}, u32[]{:S(2)}) copy-start(bf16[128,512]{1,0:T(8,128)(2,1)} %node_in.1) | copy-start | bytes 393220
  0.6 61.5 %copy-start.4 = (bf16[3,1,1,32,128,128]{5,4,3,2,1,0:T(8,128)(2,1)S(1)}, bf16[3,1,1,32,128,128]{5,4,3,2,1,0:T(8,128)(2,1)}, u32[]{:S(2)}) copy-start(bf16[3,1,1,32,128,128]{5,4,3,2,1,0:T(8,128)(2,1)} %param.10) | copy-start | bytes 9437188
  0.7 39.0 %copy-start.3 = (s32[3,1,1]{0,2,1:T(1,128)S(1)}, s32[3,1,1]{0,2,1:T(1,128)}, u32[]{:S(2)}) copy-start(s32[3,1,1]{0,2,1:T(1,128)} %param.13) | copy-start | bytes 40
  0.7 39.0 %copy-start.2 = (s32[3,1,1,32]{3,2,1,0:T(1,128)S(1)}, s32[3,1,1,32]{3,2,1,0:T(1,128)}, u32[]{:S(2)}) copy-start(s32[3,1,1,32]{3,2,1,0:T(1,128)} %cols.1) | copy-start | bytes 1156
  0.7 38.9 %copy-start.1 = (s32[3,1,1,32]{3,2,1,0:T(1,128)S(1)}, s32[3,1,1,32]{3,2,1,0:T(1,128)}, u32[]{:S(2)}) copy-start(s32[3,1,1,32]{3,2,1,0:T(1,128)} %rows.1) | copy-start | bytes 1156
  0.7 60.2 %collective-permute-start.6 = (bf16[3,32,128,128]{3,2,1,0:T(8,128)(2,1)}, bf16[3,32,128,128]{3,2,1,0:T(8,128)(2,1)S(1)}, u32[]{:S(2)}, u32[]{:S(2)}) collective-permute-start(bf16[3,32,128,128]{3,2,1,0:T(8,128)(2,1)} %bitcast.50), channel_id=1, source_target_pairs={{0,1},{1,0},{2,3},{3,2},{4,5},{5,4},{6,7},{7,6},{8,9},{9,8},{10,11... | collective-permute-start | bytes 9437192 | tf_op jit(solution)/shard_map/ppermute | solution.py:31
  4.0 6.7 %collective-permute-start.1 = (bf16[64,1024]{1,0:T(8,128)(2,1)}, bf16[64,1024]{1,0:T(8,128)(2,1)S(1)}, u32[]{:S(2)}, u32[]{:S(2)}) collective-permute-start(bf16[64,1024]{1,0:T(8,128)(2,1)} %bitcast.57), channel_id=1, source_target_pairs={{0,128},{128,0},{1,129},{129,1},{2,130},{130,2},{3,131},{131,3},{4... | collective-permute-start | bytes 393224 | tf_op jit(solution)/shard_map/ppermute | solution.py:31
  11.6 7.0 %collective-permute-start.4 = (bf16[2,64,1024]{2,1,0:T(8,128)(2,1)S(1)}, bf16[2,64,1024]{2,1,0:T(8,128)(2,1)S(1)}, u32[]{:S(2)}, u32[]{:S(2)}) collective-permute-start(bf16[2,64,1024]{2,1,0:T(8,128)(2,1)S(1)} %pad_maximum_fusion.1.g0), channel_id=1, source_target_pairs={{0,96},{32,0},{64,32},{96,64},{1,97},{33,1},{65,33},{97,65},{2,98}... | collective-permute-start | bytes 786440 | tf_op jit(solution)/shard_map/ppermute | solution.py:31
  12.7 8.2 %collective-permute-start.3 = (bf16[2,64,1024]{2,1,0:T(8,128)(2,1)S(1)}, bf16[2,64,1024]{2,1,0:T(8,128)(2,1)S(1)}, u32[]{:S(2)}, u32[]{:S(2)}) collective-permute-start(bf16[2,64,1024]{2,1,0:T(8,128)(2,1)S(1)} %pad_maximum_fusion.1.g0), channel_id=1, source_target_pairs={{0,64},{32,96},{64,0},{96,32},{1,65},{33,97},{65,1},{97,33},{2,66}... | collective-permute-start | bytes 786440 | tf_op jit(solution)/shard_map/ppermute | solution.py:31
  13.0 15.0 %collective-permute-start.2 = (bf16[2,64,1024]{2,1,0:T(8,128)(2,1)S(1)}, bf16[2,64,1024]{2,1,0:T(8,128)(2,1)S(1)}, u32[]{:S(2)}, u32[]{:S(2)}) collective-permute-start(bf16[2,64,1024]{2,1,0:T(8,128)(2,1)S(1)} %pad_maximum_fusion.1.g0), channel_id=1, source_target_pairs={{0,32},{32,64},{64,96},{96,0},{1,33},{33,65},{65,97},{97,1},{2,34}... | collective-permute-start | bytes 786440 | tf_op jit(solution)/shard_map/ppermute | solution.py:31
  28.1 32.8 %collective-permute-start.5 = (bf16[512,1024]{1,0:T(8,128)(2,1)S(1)}, bf16[512,1024]{1,0:T(8,128)(2,1)S(1)}, u32[]{:S(2)}, u32[]{:S(2)}) collective-permute-start(bf16[512,1024]{1,0:T(8,128)(2,1)S(1)} %bitcast.45), channel_id=1, source_target_pairs={{0,1},{1,0},{2,3},{3,2},{4,5},{5,4},{6,7},{7,6},{8,9},{9,8},{10,11... | collective-permute-start | bytes 3145736 | tf_op jit(solution)/shard_map/ppermute | solution.py:31
  28.8 5.1 %collective-permute-start.7 = (bf16[512,128]{1,0:T(8,128)(2,1)S(1)}, bf16[512,128]{1,0:T(8,128)(2,1)S(1)}, u32[]{:S(2)}, u32[]{:S(2)}) collective-permute-start(bf16[512,128]{1,0:T(8,128)(2,1)S(1)} %turn.1), channel_id=1, source_target_pairs={{0,16},{16,0},{1,17},{17,1},{2,18},{18,2},{3,19},{19,3},{4,20},{20... | collective-permute-start | bytes 393224 | tf_op jit(solution)/shard_map/ppermute | solution.py:31
  34.0 10.4 %collective-permute-start.14 = (bf16[2,512,128]{2,1,0:T(8,128)(2,1)S(1)}, bf16[2,512,128]{2,1,0:T(8,128)(2,1)S(1)}, u32[]{:S(2)}, u32[]{:S(2)}) collective-permute-start(bf16[2,512,128]{2,1,0:T(8,128)(2,1)S(1)} %pad_maximum_fusion.2.refs_0_), channel_id=1, source_target_pairs={{0,14},{2,0},{4,2},{6,4},{8,6},{10,8},{12,10},{14,12},{1,15},{3,1}... | collective-permute-start | bytes 786440 | tf_op jit(solution)/shard_map/ppermute | solution.py:31
  39.6 21.3 %collective-permute-start.10 = (bf16[2,512,128]{2,1,0:T(8,128)(2,1)S(1)}, bf16[2,512,128]{2,1,0:T(8,128)(2,1)S(1)}, u32[]{:S(2)}, u32[]{:S(2)}) collective-permute-start(bf16[2,512,128]{2,1,0:T(8,128)(2,1)S(1)} %pad_maximum_fusion.2.refs_0_), channel_id=1, source_target_pairs={{0,6},{2,8},{4,10},{6,12},{8,14},{10,0},{12,2},{14,4},{1,7},{3,9},... | collective-permute-start | bytes 786440 | tf_op jit(solution)/shard_map/ppermute | solution.py:31
  40.2 2.0 %collective-permute-start = (s32[3,128]{1,0:T(4,128)S(1)}, s32[3,128]{1,0:T(4,128)S(1)}, u32[]{:S(2)}, u32[]{:S(2)}) collective-permute-start(s32[3,128]{1,0:T(4,128)S(1)} %meta.1.meta0), channel_id=1, source_target_pairs={{0,1},{1,0},{2,3},{3,2},{4,5},{5,4},{6,7},{7,6},{8,9},{9,8},{10,11... | collective-permute-start | bytes 4616 | tf_op jit(solution)/shard_map/ppermute | solution.py:31
  42.2 28.6 %collective-permute-start.13 = (bf16[2,512,128]{2,1,0:T(8,128)(2,1)S(1)}, bf16[2,512,128]{2,1,0:T(8,128)(2,1)S(1)}, u32[]{:S(2)}, u32[]{:S(2)}) collective-permute-start(bf16[2,512,128]{2,1,0:T(8,128)(2,1)S(1)} %pad_maximum_fusion.2.refs_0_), channel_id=1, source_target_pairs={{0,12},{2,14},{4,0},{6,2},{8,4},{10,6},{12,8},{14,10},{1,13},{3,15... | collective-permute-start | bytes 786440 | tf_op jit(solution)/shard_map/ppermute | solution.py:31
  44.4 26.5 %collective-permute-start.12 = (bf16[2,512,128]{2,1,0:T(8,128)(2,1)S(1)}, bf16[2,512,128]{2,1,0:T(8,128)(2,1)S(1)}, u32[]{:S(2)}, u32[]{:S(2)}) collective-permute-start(bf16[2,512,128]{2,1,0:T(8,128)(2,1)S(1)} %pad_maximum_fusion.2.refs_0_), channel_id=1, source_target_pairs={{0,10},{2,12},{4,14},{6,0},{8,2},{10,4},{12,6},{14,8},{1,11},{3,13... | collective-permute-start | bytes 786440 | tf_op jit(solution)/shard_map/ppermute | solution.py:31
  60.9 11.8 %collective-permute-start.9 = (bf16[2,512,128]{2,1,0:T(8,128)(2,1)S(1)}, bf16[2,512,128]{2,1,0:T(8,128)(2,1)S(1)}, u32[]{:S(2)}, u32[]{:S(2)}) collective-permute-start(bf16[2,512,128]{2,1,0:T(8,128)(2,1)S(1)} %pad_maximum_fusion.2.refs_0_), channel_id=1, source_target_pairs={{0,4},{2,6},{4,8},{6,10},{8,12},{10,14},{12,0},{14,2},{1,5},{3,7},... | collective-permute-start | bytes 786440 | tf_op jit(solution)/shard_map/ppermute | solution.py:31
  60.9 15.9 %collective-permute-start.8 = (bf16[2,512,128]{2,1,0:T(8,128)(2,1)S(1)}, bf16[2,512,128]{2,1,0:T(8,128)(2,1)S(1)}, u32[]{:S(2)}, u32[]{:S(2)}) collective-permute-start(bf16[2,512,128]{2,1,0:T(8,128)(2,1)S(1)} %pad_maximum_fusion.2.refs_0_), channel_id=1, source_target_pairs={{0,2},{2,4},{4,6},{6,8},{8,10},{10,12},{12,14},{14,0},{1,3},{3,5},... | collective-permute-start | bytes 786440 | tf_op jit(solution)/shard_map/ppermute | solution.py:31
  60.9 21.5 %collective-permute-start.11 = (bf16[2,512,128]{2,1,0:T(8,128)(2,1)S(1)}, bf16[2,512,128]{2,1,0:T(8,128)(2,1)S(1)}, u32[]{:S(2)}, u32[]{:S(2)}) collective-permute-start(bf16[2,512,128]{2,1,0:T(8,128)(2,1)S(1)} %collective-permute-done.10.refs_3_), channel_id=1, source_target_pairs={{0,2},{2,4},{4,6},{6,8},{8,10},{10,12},{12,14},{14,0},{1,3},{3,5},... | collective-permute-start | bytes 786440 | tf_op jit(solution)/shard_map/ppermute | solution.py:31
  70.8 16.7 %copy-start.5 = (bf16[3,512,512]{2,1,0:T(8,128)(2,1)S(1)}, bf16[3,512,512]{2,1,0:T(8,128)(2,1)}, u32[]{:S(2)}) copy-start(bf16[3,512,512]{2,1,0:T(8,128)(2,1)} %weights.1) | copy-start | bytes 4718596
  86.0 12.3 %collective-permute-start.15 = (bf16[4,4,3,16,512]{4,3,2,1,0:T(8,128)(2,1)S(1)}, bf16[4,4,3,16,512]{4,3,2,1,0:T(8,128)(2,1)S(1)}, u32[]{:S(2)}, u32[]{:S(2)}) collective-permute-start(bf16[4,4,3,16,512]{4,3,2,1,0:T(8,128)(2,1)S(1)} %get-tuple-element.10), channel_id=1, source_target_pairs={{0,1},{1,0},{2,3},{3,2},{4,5},{5,4},{6,7},{7,6},{8,9},{9,8},{10,11... | collective-permute-start | bytes 2359304 | tf_op jit(solution)/shard_map/ppermute | solution.py:31
  98.2 28.5 %collective-permute-start.22 = (bf16[8,512,128]{2,1,0:T(8,128)(2,1)S(1)}, bf16[8,512,128]{2,1,0:T(8,128)(2,1)S(1)}, u32[]{:S(2)}, u32[]{:S(2)}) collective-permute-start(bf16[8,512,128]{2,1,0:T(8,128)(2,1)S(1)} %get-tuple-element.11), channel_id=1, source_target_pairs={{0,16},{16,0},{1,17},{17,1},{2,18},{18,2},{3,19},{19,3},{4,20},{20... | collective-permute-start | bytes 3145736 | tf_op jit(solution)/shard_map/ppermute | solution.py:31
  98.5 7.2 %collective-permute-start.16 = (bf16[4,3,16,512]{3,2,1,0:T(8,128)(2,1)S(1)}, bf16[4,3,16,512]{3,2,1,0:T(8,128)(2,1)S(1)}, u32[]{:S(2)}, u32[]{:S(2)}) collective-permute-start(bf16[4,3,16,512]{3,2,1,0:T(8,128)(2,1)S(1)} %get-tuple-element.16), channel_id=1, source_target_pairs={{0,32},{32,64},{64,96},{96,0},{1,33},{33,65},{65,97},{97,1},{2,34}... | collective-permute-start | bytes 589832 | tf_op jit(solution)/shard_map/ppermute | solution.py:31
  98.6 7.1 %collective-permute-start.18 = (bf16[4,3,16,512]{3,2,1,0:T(8,128)(2,1)S(1)}, bf16[4,3,16,512]{3,2,1,0:T(8,128)(2,1)S(1)}, u32[]{:S(2)}, u32[]{:S(2)}) collective-permute-start(bf16[4,3,16,512]{3,2,1,0:T(8,128)(2,1)S(1)} %get-tuple-element.17), channel_id=1, source_target_pairs={{0,96},{32,0},{64,32},{96,64},{1,97},{33,1},{65,33},{97,65},{2,98}... | collective-permute-start | bytes 589832 | tf_op jit(solution)/shard_map/ppermute | solution.py:31
  101.3 8.9 %collective-permute-start.17 = (bf16[4,3,16,512]{3,2,1,0:T(8,128)(2,1)S(1)}, bf16[4,3,16,512]{3,2,1,0:T(8,128)(2,1)S(1)}, u32[]{:S(2)}, u32[]{:S(2)}) collective-permute-start(bf16[4,3,16,512]{3,2,1,0:T(8,128)(2,1)S(1)} %get-tuple-element.18), channel_id=1, source_target_pairs={{0,64},{32,96},{64,0},{96,32},{1,65},{33,97},{65,1},{97,33},{2,66}... | collective-permute-start | bytes 589832 | tf_op jit(solution)/shard_map/ppermute | solution.py:31
  110.3 11.3 %collective-permute-start.19 = (bf16[3,16,512]{2,1,0:T(8,128)(2,1)S(1)}, bf16[3,16,512]{2,1,0:T(8,128)(2,1)S(1)}, u32[]{:S(2)}, u32[]{:S(2)}) collective-permute-start(bf16[3,16,512]{2,1,0:T(8,128)(2,1)S(1)} %get-tuple-element.21), channel_id=1, source_target_pairs={{0,16},{16,128},{128,144},{144,0},{1,17},{17,129},{129,145},{145,1... | collective-permute-start | bytes 147464 | tf_op jit(solution)/shard_map/ppermute | solution.py:31
  110.4 13.2 %collective-permute-start.21 = (bf16[3,16,512]{2,1,0:T(8,128)(2,1)S(1)}, bf16[3,16,512]{2,1,0:T(8,128)(2,1)S(1)}, u32[]{:S(2)}, u32[]{:S(2)}) collective-permute-start(bf16[3,16,512]{2,1,0:T(8,128)(2,1)S(1)} %get-tuple-element.22), channel_id=1, source_target_pairs={{0,144},{16,0},{128,16},{144,128},{1,145},{17,1},{129,17},{145,129... | collective-permute-start | bytes 147464 | tf_op jit(solution)/shard_map/ppermute | solution.py:31
  113.8 12.9 %collective-permute-start.20 = (bf16[3,16,512]{2,1,0:T(8,128)(2,1)S(1)}, bf16[3,16,512]{2,1,0:T(8,128)(2,1)S(1)}, u32[]{:S(2)}, u32[]{:S(2)}) collective-permute-start(bf16[3,16,512]{2,1,0:T(8,128)(2,1)S(1)} %get-tuple-element.23), channel_id=1, source_target_pairs={{0,128},{16,144},{128,0},{144,16},{1,129},{17,145},{129,1},{145,17... | collective-permute-start | bytes 147464 | tf_op jit(solution)/shard_map/ppermute | solution.py:31
  126.7 7.9 %collective-permute-start.23 = (f32[3,16,512]{2,1,0:T(8,128)S(1)}, f32[3,16,512]{2,1,0:T(8,128)S(1)}, u32[]{:S(2)}, u32[]{:S(2)}) collective-permute-start(f32[3,16,512]{2,1,0:T(8,128)S(1)} %fusion.7), channel_id=1, source_target_pairs={{0,2},{2,0},{4,6},{6,4},{8,10},{10,8},{12,14},{14,12},{1,3},{3,1},... | collective-permute-start | bytes 294920 | tf_op jit(solution)/shard_map/ppermute | solution.py:35
  129.6 61.8 %all-to-all-start = ((bf16[8,512,128]{2,1,0:T(8,128)(2,1)}), bf16[8,512,128]{2,1,0:T(8,128)(2,1)S(1)}, u32[]{:S(2)}, u32[]{:S(2)}) async-start(bf16[8,512,128]{2,1,0:T(8,128)(2,1)} %add_convert_fusion), calls=%async_computation | async-start | bytes 2097152 | tf_op jit(solution)/shard_map/all_to_all | solution.py:298
  134.6 20.0 %collective-permute-start.26 = (bf16[3,16,512]{2,1,0:T(8,128)(2,1)S(1)}, bf16[3,16,512]{2,1,0:T(8,128)(2,1)S(1)}, u32[]{:S(2)}, u32[]{:S(2)}) collective-permute-start(bf16[3,16,512]{2,1,0:T(8,128)(2,1)S(1)} %add_convert_fusion.5), channel_id=1, source_target_pairs={{0,12},{2,14},{4,0},{6,2},{8,4},{10,6},{12,8},{14,10},{1,13},{3,15... | collective-permute-start | bytes 147464 | tf_op jit(solution)/shard_map/ppermute | solution.py:31
  138.2 24.3 %collective-permute-start.25 = (bf16[3,16,512]{2,1,0:T(8,128)(2,1)S(1)}, bf16[3,16,512]{2,1,0:T(8,128)(2,1)S(1)}, u32[]{:S(2)}, u32[]{:S(2)}) collective-permute-start(bf16[3,16,512]{2,1,0:T(8,128)(2,1)S(1)} %add_convert_fusion.5), channel_id=1, source_target_pairs={{0,4},{2,6},{4,8},{6,10},{8,12},{10,14},{12,0},{14,2},{1,5},{3,7},... | collective-permute-start | bytes 147464 | tf_op jit(solution)/shard_map/ppermute | solution.py:31
  138.3 28.5 %collective-permute-start.24 = (bf16[3,16,512]{2,1,0:T(8,128)(2,1)S(1)}, bf16[3,16,512]{2,1,0:T(8,128)(2,1)S(1)}, u32[]{:S(2)}, u32[]{:S(2)}) collective-permute-start(bf16[3,16,512]{2,1,0:T(8,128)(2,1)S(1)} %add_convert_fusion.5), channel_id=1, source_target_pairs={{0,8},{2,10},{4,12},{6,14},{8,0},{10,2},{12,4},{14,6},{1,9},{3,11}... | collective-permute-start | bytes 147464 | tf_op jit(solution)/shard_map/ppermute | solution.py:31
  166.8 3.0 %collective-permute-start.29 = (bf16[3,16,512]{2,1,0:T(8,128)(2,1)S(1)}, bf16[3,16,512]{2,1,0:T(8,128)(2,1)S(1)}, u32[]{:S(2)}, u32[]{:S(2)}) collective-permute-start(bf16[3,16,512]{2,1,0:T(8,128)(2,1)S(1)} %add_convert_fusion.4), channel_id=1, source_target_pairs={{0,144},{16,0},{128,16},{144,128},{1,145},{17,1},{129,17},{145,129... | collective-permute-start | bytes 147464 | tf_op jit(solution)/shard_map/ppermute | solution.py:31
  167.5 4.4 %collective-permute-start.28 = (bf16[3,16,512]{2,1,0:T(8,128)(2,1)S(1)}, bf16[3,16,512]{2,1,0:T(8,128)(2,1)S(1)}, u32[]{:S(2)}, u32[]{:S(2)}) collective-permute-start(bf16[3,16,512]{2,1,0:T(8,128)(2,1)S(1)} %add_convert_fusion.4), channel_id=1, source_target_pairs={{0,128},{16,144},{128,0},{144,16},{1,129},{17,145},{129,1},{145,17... | collective-permute-start | bytes 147464 | tf_op jit(solution)/shard_map/ppermute | solution.py:31
  169.4 4.7 %collective-permute-start.27 = (bf16[3,16,512]{2,1,0:T(8,128)(2,1)S(1)}, bf16[3,16,512]{2,1,0:T(8,128)(2,1)S(1)}, u32[]{:S(2)}, u32[]{:S(2)}) collective-permute-start(bf16[3,16,512]{2,1,0:T(8,128)(2,1)S(1)} %add_convert_fusion.4), channel_id=1, source_target_pairs={{0,16},{16,128},{128,144},{144,0},{1,17},{17,129},{129,145},{145,1... | collective-permute-start | bytes 147464 | tf_op jit(solution)/shard_map/ppermute | solution.py:31
  174.1 6.5 %collective-permute-start.31 = (bf16[4,3,16,512]{3,2,1,0:T(8,128)(2,1)S(1)}, bf16[4,3,16,512]{3,2,1,0:T(8,128)(2,1)S(1)}, u32[]{:S(2)}, u32[]{:S(2)}) collective-permute-start(bf16[4,3,16,512]{3,2,1,0:T(8,128)(2,1)S(1)} %get-tuple-element.20), channel_id=1, source_target_pairs={{0,64},{32,96},{64,0},{96,32},{1,65},{33,97},{65,1},{97,33},{2,66}... | collective-permute-start | bytes 589832 | tf_op jit(solution)/shard_map/ppermute | solution.py:31
  174.2 12.1 %collective-permute-start.30 = (bf16[4,3,16,512]{3,2,1,0:T(8,128)(2,1)S(1)}, bf16[4,3,16,512]{3,2,1,0:T(8,128)(2,1)S(1)}, u32[]{:S(2)}, u32[]{:S(2)}) collective-permute-start(bf16[4,3,16,512]{3,2,1,0:T(8,128)(2,1)S(1)} %get-tuple-element.20), channel_id=1, source_target_pairs={{0,32},{32,64},{64,96},{96,0},{1,33},{33,65},{65,97},{97,1},{2,34}... | collective-permute-start | bytes 589832 | tf_op jit(solution)/shard_map/ppermute | solution.py:31
  176.0 10.4 %collective-permute-start.32 = (bf16[4,3,16,512]{3,2,1,0:T(8,128)(2,1)S(1)}, bf16[4,3,16,512]{3,2,1,0:T(8,128)(2,1)S(1)}, u32[]{:S(2)}, u32[]{:S(2)}) collective-permute-start(bf16[4,3,16,512]{3,2,1,0:T(8,128)(2,1)S(1)} %get-tuple-element.20), channel_id=1, source_target_pairs={{0,96},{32,0},{64,32},{96,64},{1,97},{33,1},{65,33},{97,65},{2,98}... | collective-permute-start | bytes 589832 | tf_op jit(solution)/shard_map/ppermute | solution.py:31
  186.4 2.7 %collective-permute-start.33 = (bf16[4,4,3,16,512]{4,3,2,1,0:T(8,128)(2,1)S(1)}, bf16[4,4,3,16,512]{4,3,2,1,0:T(8,128)(2,1)S(1)}, u32[]{:S(2)}, u32[]{:S(2)}) collective-permute-start(bf16[4,4,3,16,512]{4,3,2,1,0:T(8,128)(2,1)S(1)} %pad_maximum_fusion.own), channel_id=1, source_target_pairs={{0,1},{1,0},{2,3},{3,2},{4,5},{5,4},{6,7},{7,6},{8,9},{9,8},{10,11... | collective-permute-start | bytes 2359304 | tf_op jit(solution)/shard_map/ppermute | solution.py:31
